TPU v7x, 128 devices: a whole 4x4x4 slice. The times are simulated.
128 devices in a mesh: gx: 16 (over y_hi, z, core), gy: 8 (over y_lo, x).
Axes of the slice: x: 4, y: 4 (y_hi: 2, y_lo: 2; y = y_hi * 2 + y_lo), z: 4, core: 2. Of those that a mesh axis runs over, the one named last changes fastest.
Arguments:
- features: bfloat16 [32, 128, 64, 128], P(None, 'gx', 'gy'), may hold values from -6 to 6
- occupancy: int32 [16, 8, 16], replicated, may hold values 0 or 1
- weight_one: bfloat16 [32, 3, 3, 3, 32], replicated, may hold values from -0.21875 to 0.21875
- bias_one: float32 [32], replicated, may hold values from -3 to 3
- weight_two: bfloat16 [32, 3, 3, 3, 32], replicated, may hold values from -0.21875 to 0.21875
- bias_two: float32 [32], replicated, may hold values from -3 to 3
- grad_pooled: bfloat16 [32, 64, 32, 64], P(None, 'gx', 'gy'), may hold values from -24 to 24
- pool_choice: int32 [32, 64, 32, 64], P(None, 'gx', 'gy'), may hold values from 0 to 7
Outputs:
- grad_input: bfloat16 [32, 128, 64, 128], P(None, 'gx', 'gy')
- grad_weight_one: float32 [32, 3, 3, 3, 32], replicated
- grad_bias_one: float32 [32], replicated
- grad_weight_two: float32 [32, 3, 3, 3, 32], replicated
- grad_bias_two: float32 [32], replicated
All inputs are finite; a program needn't handle non-finite values.
Results may differ from a plain program's by a relative error of at most 0.035.
The roundings to bfloat16 on the way count: a program that leaves them out, or rounds other values in their place, can miss the bound.
Values may be sent and summed in bfloat16 or wider, within the bound.
No kernel may reach another device: no remote copies, remote signals or barrier semaphores. Data moves between devices by JAX's collectives and lax.ppermute only.
A program may use at most 64 MiB of HBM per device.

v0:
```python
import math

import jax
import jax.numpy as jnp
from jax import lax
from jax.sharding import PartitionSpec as P


def padded_2(x, sides, width):
    for axis, dim in sides:
        devices, length = (lax.axis_size(axis), x.shape[dim])
        up = [(i, (i + 1) % devices) for i in range(devices - 1)]
        down = [(j, i) for i, j in up]
        last = lax.slice_in_dim(x, length - width, length, axis=dim)
        first = lax.slice_in_dim(x, 0, width, axis=dim)
        before = lax.ppermute(last, axis, up)
        after = lax.ppermute(first, axis, down)
        x = jnp.concatenate([before, x, after], axis=dim)
    return x


def together(arrays, axis):
    ravelled, at, outs = (jnp.concatenate([a.reshape(-1) for a in arrays]), 0, [])
    running = lax.psum(ravelled, axis)
    for a in arrays:
        outs.append(running[at : at + a.size].reshape(a.shape))
        at += a.size
    return tuple(outs)


def depth_stack(padded):
    depth = padded.shape[3]
    framed = jnp.pad(padded, ((0, 0), (0, 0), (0, 0), (1, 1)))
    return jnp.concatenate(
        [framed[..., 0:depth], framed[..., 1 : depth + 1], framed[..., 2 : depth + 2]], axis=0
    )


def convolve(stacked, weight):
    width_x = stacked.shape[1] - 2
    width_y = stacked.shape[2] - 2
    channels = weight.shape[0]
    total = None
    for row_off in range(3):
        for col_off in range(3):
            kernel = weight[:, row_off, col_off].reshape(channels, -1)
            window = stacked[:, row_off : row_off + width_x, col_off : col_off + width_y, :]
            term = jnp.einsum("ok,kxyz->oxyz", kernel, window, preferred_element_type=jnp.float32)
            total = term if total is None else total + term
    return total


def weight_grad(upstream, stacked):
    width_x = upstream.shape[1]
    width_y = upstream.shape[2]
    channels = upstream.shape[0]
    blocks = []
    for row_off in range(3):
        column_parts = []
        for col_off in range(3):
            window = stacked[:, row_off : row_off + width_x, col_off : col_off + width_y, :]
            part = jnp.einsum("oxyz,kxyz->ok", upstream, window, preferred_element_type=jnp.float32)
            column_parts.append(part.reshape(channels, 3, -1))
        blocks.append(jnp.stack(column_parts, axis=1))
    return jnp.stack(blocks, axis=1)


def flipped(weight):
    return jnp.flip(weight, (1, 2, 3)).transpose(4, 1, 2, 3, 0)


def expand(field, factor):
    return jnp.repeat(
        jnp.repeat(jnp.repeat(field, factor, axis=-3), factor, axis=-2), factor, axis=-1
    )


def body(features, occupancy, weight_one, bias_one, weight_two, bias_two, grad_pooled, pool_choice):
    cells_x = features.shape[1]
    cells_y = features.shape[2]
    cells_z = features.shape[3]
    brick_x = cells_x // 8
    brick_y = cells_y // 8
    padded_flags = jnp.pad(occupancy, ((1, 1), (1, 1), (0, 0)))
    corner_x = lax.axis_index("gx") * brick_x
    corner_y = lax.axis_index("gy") * brick_y
    flag_window = lax.dynamic_slice(
        padded_flags,
        (corner_x, corner_y, jnp.int32(0)),
        (brick_x + 2, brick_y + 2, occupancy.shape[2]),
    )
    cell_flags = expand(flag_window, 8).astype(jnp.float32)
    mask_inner = cell_flags[8 : 8 + cells_x, 8 : 8 + cells_y]
    masked = (features.astype(jnp.float32) * mask_inner).astype(jnp.bfloat16)
    input_padded = padded_2(masked, (("gx", 1), ("gy", 2)), 1)
    input_stack = depth_stack(input_padded)
    pre_one = convolve(input_stack, weight_one) + bias_one[:, None, None, None]
    hidden = (jnp.maximum(pre_one, 0.0) * mask_inner).astype(jnp.bfloat16)
    hidden_padded = padded_2(hidden, (("gx", 1), ("gy", 2)), 1)
    hidden_stack = depth_stack(hidden_padded)
    pre_two = convolve(hidden_stack, weight_two) + bias_two[:, None, None, None]
    spread = expand(grad_pooled.astype(jnp.float32), 2)
    chosen = expand(pool_choice, 2)
    shape_cells = (cells_x, cells_y, cells_z)
    parity = (
        4 * (lax.broadcasted_iota(jnp.int32, shape_cells, 0) % 2)
        + 2 * (lax.broadcasted_iota(jnp.int32, shape_cells, 1) % 2)
        + lax.broadcasted_iota(jnp.int32, shape_cells, 2) % 2
    )
    upstream = jnp.where(chosen == parity[None], spread, 0.0)
    delta_two = (upstream * (pre_two > 0).astype(jnp.float32) * mask_inner).astype(jnp.bfloat16)
    local_w_two = weight_grad(delta_two, hidden_stack)
    local_b_two = jnp.sum(delta_two.astype(jnp.float32), axis=(1, 2, 3))
    delta_two_padded = padded_2(delta_two, (("gx", 1), ("gy", 2)), 1)
    back_one = convolve(depth_stack(delta_two_padded), flipped(weight_two))
    delta_one = (back_one * (pre_one > 0).astype(jnp.float32) * mask_inner).astype(jnp.bfloat16)
    local_w_one = weight_grad(delta_one, input_stack)
    local_b_one = jnp.sum(delta_one.astype(jnp.float32), axis=(1, 2, 3))
    summed_w_one, summed_b_one, summed_w_two, summed_b_two = together(
        (local_w_one, local_b_one, local_w_two, local_b_two), ("gx", "gy")
    )
    delta_one_padded = padded_2(delta_one, (("gx", 1), ("gy", 2)), 1)
    back_input = convolve(depth_stack(delta_one_padded), flipped(weight_one))
    grad_input = (back_input * mask_inner).astype(jnp.bfloat16)
    total_cells = cells_x * lax.axis_size("gx") * cells_y * lax.axis_size("gy") * cells_z
    scale = 1.0 / math.sqrt(total_cells)
    return (
        grad_input,
        summed_w_one * scale,
        summed_b_one * scale,
        summed_w_two * scale,
        summed_b_two * scale,
    )


def solution(mesh):
    placed = (
        P(None, "gx", "gy", None),
        P(),
        P(),
        P(),
        P(),
        P(),
        P(None, "gx", "gy", None),
        P(None, "gx", "gy", None),
    )
    return jax.shard_map(
        body,
        mesh=mesh,
        in_specs=placed,
        out_specs=(P(None, "gx", "gy", None), P(), P(), P(), P()),
        check_vma=False,
    )
```

profile of v0, /device:TPU:1, one launch (start us, length us, event | category | flops | bytes accessed | tf_op | source)
XLA Modules:
  0.0 310.1 jit_solution(7934017249467041847)
XLA Ops:
  9.3 3.3 %collective-permute-start.1 = (bf16[32,1,8,128]{3,0,2,1:T(8,128)(2,1)S(1)}, bf16[32,1,8,128]{3,0,2,1:T(8,128)(2,1)S(1)}, u32[]{:S(2)}, u32[]{:S(2)}) collective-permute-start(bf16[32,1,8,128]{3,0,2,1:T(8,128)(2,1)S(1)} %get-tuple-element.50), channel_id=1, source_target_pairs={{8,0},{16,8},{24,16},{32,24},{40,32},{48,40},{56,48},{64,56},{72,6... | collective-permute-start | bytes 196616 | tf_op jit(solution)/shard_map/ppermute | solution.py:17
  12.6 3.6 %collective-permute-start = (bf16[32,1,8,128]{3,0,2,1:T(8,128)(2,1)S(1)}, bf16[32,1,8,128]{3,0,2,1:T(8,128)(2,1)S(1)}, u32[]{:S(2)}, u32[]{:S(2)}) collective-permute-start(bf16[32,1,8,128]{3,0,2,1:T(8,128)(2,1)S(1)} %get-tuple-element.49), channel_id=1, source_target_pairs={{0,8},{8,16},{16,24},{24,32},{32,40},{40,48},{48,56},{56,64},{64,7... | collective-permute-start | bytes 196616 | tf_op jit(solution)/shard_map/ppermute | solution.py:16
  20.8 4.0 %collective-permute-start.2 = (bf16[32,10,1,128]{3,0,2,1:T(8,128)(2,1)S(1)}, bf16[32,10,1,128]{3,0,2,1:T(8,128)(2,1)S(1)}, u32[]{:S(2)}, u32[]{:S(2)}) collective-permute-start(bf16[32,10,1,128]{3,0,2,1:T(8,128)(2,1)S(1)} %get-tuple-element.41), channel_id=1, source_target_pairs={{0,1},{1,2},{2,3},{3,4},{4,5},{5,6},{6,7},{8,9},{9,10},{10,11},{11... | collective-permute-start | bytes 245768 | tf_op jit(solution)/shard_map/ppermute | solution.py:16
  24.8 1.8 collective-permute-done.2
  26.6 1.5 fusion.20
  34.1 1.9 collective-permute-start.5
  36.0 3.7 %collective-permute-start.4 = (bf16[32,1,8,128]{3,0,2,1:T(8,128)(2,1)S(1)}, bf16[32,1,8,128]{3,0,2,1:T(8,128)(2,1)S(1)}, u32[]{:S(2)}, u32[]{:S(2)}) collective-permute-start(bf16[32,1,8,128]{3,0,2,1:T(8,128)(2,1)S(1)} %get-tuple-element.47), channel_id=1, source_target_pairs={{0,8},{8,16},{16,24},{24,32},{32,40},{40,48},{48,56},{56,64},{64,7... | collective-permute-start | bytes 196616 | tf_op jit(solution)/shard_map/ppermute | solution.py:16
  43.0 5.4 %collective-permute-start.6 = (bf16[32,10,1,128]{3,0,2,1:T(8,128)(2,1)}, bf16[32,10,1,128]{3,0,2,1:T(8,128)(2,1)}, u32[]{:S(2)}, u32[]{:S(2)}) collective-permute-start(bf16[32,10,1,128]{3,0,2,1:T(8,128)(2,1)} %get-tuple-element.39), channel_id=1, source_target_pairs={{0,1},{1,2},{2,3},{3,4},{4,5},{5,6},{6,7},{8,9},{9,10},{10,11},{11... | collective-permute-start | bytes 245768 | tf_op jit(solution)/shard_map/ppermute | solution.py:16
  51.1 2.3 broadcast_in_dim.48
  53.4 3.6 %copy.179 = f32[32,8,8,128]{3,0,2,1:T(8,128)} copy(f32[32,8,8,128]{0,2,3,1:T(8,128)} %bitcast.296) | data formatting | bytes 2097152 | tf_op jit(solution)/shard_map/reshape | solution.py:73
  59.0 2.3 broadcast_in_dim.45
  61.4 3.8 %copy.177 = s32[32,8,8,128]{3,0,2,1:T(8,128)} copy(s32[32,8,8,128]{0,2,3,1:T(8,128)} %bitcast.297) | data formatting | bytes 2097152 | tf_op jit(solution)/shard_map/reshape | solution.py:73
  66.2 2.4 fusion.26
  74.2 1.5 convert_reduce_fusion
  84.0 1.9 collective-permute-start.9
  85.9 4.5 %collective-permute-start.8 = (bf16[32,1,8,128]{3,0,2,1:T(8,128)(2,1)}, bf16[32,1,8,128]{3,0,2,1:T(8,128)(2,1)S(1)}, u32[]{:S(2)}, u32[]{:S(2)}) collective-permute-start(bf16[32,1,8,128]{3,0,2,1:T(8,128)(2,1)} %get-tuple-element.45), channel_id=1, source_target_pairs={{0,8},{8,16},{16,24},{24,32},{32,40},{40,48},{48,56},{56,64},{64,7... | collective-permute-start | bytes 196616 | tf_op jit(solution)/shard_map/ppermute | solution.py:16
  98.6 3.8 %collective-permute-start.10 = (bf16[32,10,1,128]{3,0,2,1:T(8,128)(2,1)S(1)}, bf16[32,10,1,128]{3,0,2,1:T(8,128)(2,1)S(1)}, u32[]{:S(2)}, u32[]{:S(2)}) collective-permute-start(bf16[32,10,1,128]{3,0,2,1:T(8,128)(2,1)S(1)} %get-tuple-element.37), channel_id=1, source_target_pairs={{0,1},{1,2},{2,3},{3,4},{4,5},{5,6},{6,7},{8,9},{9,10},{10,11},{11... | collective-permute-start | bytes 245768 | tf_op jit(solution)/shard_map/ppermute | solution.py:16
  105.0 1.5 fusion.24
  118.5 1.9 collective-permute-start.13
  120.4 3.6 %collective-permute-start.12 = (bf16[32,1,8,128]{3,0,2,1:T(8,128)(2,1)S(1)}, bf16[32,1,8,128]{3,0,2,1:T(8,128)(2,1)S(1)}, u32[]{:S(2)}, u32[]{:S(2)}) collective-permute-start(bf16[32,1,8,128]{3,0,2,1:T(8,128)(2,1)S(1)} %get-tuple-element.43), channel_id=1, source_target_pairs={{0,8},{8,16},{16,24},{24,32},{32,40},{40,48},{48,56},{56,64},{64,7... | collective-permute-start | bytes 196616 | tf_op jit(solution)/shard_map/ppermute | solution.py:16
  125.7 3.1 %concatenate.51 = f32[55360]{0:T(1024)} concatenate(f32[27648]{0:T(1024)S(1)} %reshape.62, f32[32]{0:T(128)S(1)} %get-tuple-element.25, f32[27648]{0:T(1024)S(1)} %reshape.63, f32[32]{0:T(128)S(1)} %copy-done.39), dimensions={0} | concatenate | bytes 442880 | tf_op jit(solution)/shard_map/concatenate | solution.py:23
  130.2 4.4 %collective-permute-start.14 = (bf16[32,10,1,128]{3,0,2,1:T(8,128)(2,1)S(1)}, bf16[32,10,1,128]{3,0,2,1:T(8,128)(2,1)S(1)}, u32[]{:S(2)}, u32[]{:S(2)}) collective-permute-start(bf16[32,10,1,128]{3,0,2,1:T(8,128)(2,1)S(1)} %get-tuple-element.35), channel_id=1, source_target_pairs={{0,1},{1,2},{2,3},{3,4},{4,5},{5,6},{6,7},{8,9},{9,10},{10,11},{11... | collective-permute-start | bytes 245768 | tf_op jit(solution)/shard_map/ppermute | solution.py:16
  134.6 156.0 %all-reduce.7.cloned.1.call-done = f32[55360]{0:T(1024)} async-done(((f32[55360]{0:T(1024)}), f32[55360]{0:T(1024)}) %all-reduce.7.cloned.1.call-update) | async-done | bytes 221456 | tf_op jit(solution)/shard_map/psum | solution.py:24
  295.3 1.5 select_maximum_fusion
  (275 shorter events, 71.5 us)
Async XLA Ops:
  7.2 283.5 %all-reduce.7.cloned.1.call-start = ((), (), s32[]{:S(2)}) async-start(), calls=%async_computation | async-start | bytes 450560 | tf_op jit(solution)/shard_map/psum | solution.py:24
  8.3 7.9 %copy-start.4 = (bf16[32,3,3,3,32]{4,0,3,2,1:T(8,128)(2,1)S(1)}, bf16[32,3,3,3,32]{4,0,3,2,1:T(8,128)(2,1)}, u32[]{:S(2)}) copy-start(bf16[32,3,3,3,32]{4,0,3,2,1:T(8,128)(2,1)} %param.10) | copy-start | bytes 165892
  8.3 7.9 %copy-start.5 = (bf16[32,3,3,3,32]{4,0,3,2,1:T(8,128)(2,1)S(1)}, bf16[32,3,3,3,32]{4,0,3,2,1:T(8,128)(2,1)}, u32[]{:S(2)}) copy-start(bf16[32,3,3,3,32]{4,0,3,2,1:T(8,128)(2,1)} %param.12) | copy-start | bytes 165892
  9.3 10.1 %collective-permute-start.1 = (bf16[32,1,8,128]{3,0,2,1:T(8,128)(2,1)S(1)}, bf16[32,1,8,128]{3,0,2,1:T(8,128)(2,1)S(1)}, u32[]{:S(2)}, u32[]{:S(2)}) collective-permute-start(bf16[32,1,8,128]{3,0,2,1:T(8,128)(2,1)S(1)} %get-tuple-element.50), channel_id=1, source_target_pairs={{8,0},{16,8},{24,16},{32,24},{40,32},{48,40},{56,48},{64,56},{72,6... | collective-permute-start | bytes 196616 | tf_op jit(solution)/shard_map/ppermute | solution.py:17
  12.6 6.9 %collective-permute-start = (bf16[32,1,8,128]{3,0,2,1:T(8,128)(2,1)S(1)}, bf16[32,1,8,128]{3,0,2,1:T(8,128)(2,1)S(1)}, u32[]{:S(2)}, u32[]{:S(2)}) collective-permute-start(bf16[32,1,8,128]{3,0,2,1:T(8,128)(2,1)S(1)} %get-tuple-element.49), channel_id=1, source_target_pairs={{0,8},{8,16},{16,24},{24,32},{32,40},{40,48},{48,56},{56,64},{64,7... | collective-permute-start | bytes 196616 | tf_op jit(solution)/shard_map/ppermute | solution.py:16
  19.5 5.4 %collective-permute-start.3 = (bf16[32,10,1,128]{3,0,2,1:T(8,128)(2,1)S(1)}, bf16[32,10,1,128]{3,0,2,1:T(8,128)(2,1)S(1)}, u32[]{:S(2)}, u32[]{:S(2)}) collective-permute-start(bf16[32,10,1,128]{3,0,2,1:T(8,128)(2,1)S(1)} %get-tuple-element.42), channel_id=1, source_target_pairs={{1,0},{2,1},{3,2},{4,3},{5,4},{6,5},{7,6},{9,8},{10,9},{11,10},{12... | collective-permute-start | bytes 245768 | tf_op jit(solution)/shard_map/ppermute | solution.py:17
  20.8 5.8 %collective-permute-start.2 = (bf16[32,10,1,128]{3,0,2,1:T(8,128)(2,1)S(1)}, bf16[32,10,1,128]{3,0,2,1:T(8,128)(2,1)S(1)}, u32[]{:S(2)}, u32[]{:S(2)}) collective-permute-start(bf16[32,10,1,128]{3,0,2,1:T(8,128)(2,1)S(1)} %get-tuple-element.41), channel_id=1, source_target_pairs={{0,1},{1,2},{2,3},{3,4},{4,5},{5,6},{6,7},{8,9},{9,10},{10,11},{11... | collective-permute-start | bytes 245768 | tf_op jit(solution)/shard_map/ppermute | solution.py:16
  34.1 5.6 %collective-permute-start.5 = (bf16[32,1,8,128]{3,0,2,1:T(8,128)(2,1)S(1)}, bf16[32,1,8,128]{3,0,2,1:T(8,128)(2,1)S(1)}, u32[]{:S(2)}, u32[]{:S(2)}) collective-permute-start(bf16[32,1,8,128]{3,0,2,1:T(8,128)(2,1)S(1)} %get-tuple-element.48), channel_id=1, source_target_pairs={{8,0},{16,8},{24,16},{32,24},{40,32},{48,40},{56,48},{64,56},{72,6... | collective-permute-start | bytes 196616 | tf_op jit(solution)/shard_map/ppermute | solution.py:17
  36.0 5.0 %collective-permute-start.4 = (bf16[32,1,8,128]{3,0,2,1:T(8,128)(2,1)S(1)}, bf16[32,1,8,128]{3,0,2,1:T(8,128)(2,1)S(1)}, u32[]{:S(2)}, u32[]{:S(2)}) collective-permute-start(bf16[32,1,8,128]{3,0,2,1:T(8,128)(2,1)S(1)} %get-tuple-element.47), channel_id=1, source_target_pairs={{0,8},{8,16},{16,24},{24,32},{32,40},{40,48},{48,56},{56,64},{64,7... | collective-permute-start | bytes 196616 | tf_op jit(solution)/shard_map/ppermute | solution.py:16
  39.7 8.6 %copy-start.6 = (bf16[32,1,8,128]{3,0,2,1:T(8,128)(2,1)}, bf16[32,1,8,128]{3,0,2,1:T(8,128)(2,1)S(1)}, u32[]{:S(2)}) copy-start(bf16[32,1,8,128]{3,0,2,1:T(8,128)(2,1)S(1)} %collective-permute-done.5) | copy-start | bytes 196612
  41.0 7.4 %copy-start.8 = (bf16[32,1,8,128]{3,0,2,1:T(8,128)(2,1)}, bf16[32,1,8,128]{3,0,2,1:T(8,128)(2,1)S(1)}, u32[]{:S(2)}) copy-start(bf16[32,1,8,128]{3,0,2,1:T(8,128)(2,1)S(1)} %collective-permute-done.4) | copy-start | bytes 196612
  41.7 24.5 %collective-permute-start.7 = (bf16[32,10,1,128]{3,0,2,1:T(8,128)(2,1)}, bf16[32,10,1,128]{3,0,2,1:T(8,128)(2,1)}, u32[]{:S(2)}, u32[]{:S(2)}) collective-permute-start(bf16[32,10,1,128]{3,0,2,1:T(8,128)(2,1)} %get-tuple-element.40), channel_id=1, source_target_pairs={{1,0},{2,1},{3,2},{4,3},{5,4},{6,5},{7,6},{9,8},{10,9},{11,10},{12... | collective-permute-start | bytes 245768 | tf_op jit(solution)/shard_map/ppermute | solution.py:17
  43.0 23.2 %collective-permute-start.6 = (bf16[32,10,1,128]{3,0,2,1:T(8,128)(2,1)}, bf16[32,10,1,128]{3,0,2,1:T(8,128)(2,1)}, u32[]{:S(2)}, u32[]{:S(2)}) collective-permute-start(bf16[32,10,1,128]{3,0,2,1:T(8,128)(2,1)} %get-tuple-element.39), channel_id=1, source_target_pairs={{0,1},{1,2},{2,3},{3,4},{4,5},{5,6},{6,7},{8,9},{9,10},{10,11},{11... | collective-permute-start | bytes 245768 | tf_op jit(solution)/shard_map/ppermute | solution.py:16
  61.4 4.7 %copy-start.29 = (bf16[32,1,1,3,32]{4,0,3,2,1:T(8,128)(2,1)S(1)}, bf16[32,1,1,3,32]{4,0,3,2,1:T(8,128)(2,1)}, u32[]{:S(2)}) copy-start(bf16[32,1,1,3,32]{4,0,3,2,1:T(8,128)(2,1)} %get-tuple-element.73) | copy-start | bytes 18436
  61.4 4.9 %copy-start.7 = (bf16[32,1,8,128]{3,0,2,1:T(8,128)(2,1)S(1)}, bf16[32,1,8,128]{3,0,2,1:T(8,128)(2,1)}, u32[]{:S(2)}) copy-start(bf16[32,1,8,128]{3,0,2,1:T(8,128)(2,1)} %copy-done.6) | copy-start | bytes 196612
  61.4 4.8 %copy-start.9 = (bf16[32,1,8,128]{3,0,2,1:T(8,128)(2,1)S(1)}, bf16[32,1,8,128]{3,0,2,1:T(8,128)(2,1)}, u32[]{:S(2)}) copy-start(bf16[32,1,8,128]{3,0,2,1:T(8,128)(2,1)} %copy-done.8) | copy-start | bytes 196612
  84.0 12.4 %collective-permute-start.9 = (bf16[32,1,8,128]{3,0,2,1:T(8,128)(2,1)}, bf16[32,1,8,128]{3,0,2,1:T(8,128)(2,1)S(1)}, u32[]{:S(2)}, u32[]{:S(2)}) collective-permute-start(bf16[32,1,8,128]{3,0,2,1:T(8,128)(2,1)} %get-tuple-element.46), channel_id=1, source_target_pairs={{8,0},{16,8},{24,16},{32,24},{40,32},{48,40},{56,48},{64,56},{72,6... | collective-permute-start | bytes 196616 | tf_op jit(solution)/shard_map/ppermute | solution.py:17
  85.9 10.5 %collective-permute-start.8 = (bf16[32,1,8,128]{3,0,2,1:T(8,128)(2,1)}, bf16[32,1,8,128]{3,0,2,1:T(8,128)(2,1)S(1)}, u32[]{:S(2)}, u32[]{:S(2)}) collective-permute-start(bf16[32,1,8,128]{3,0,2,1:T(8,128)(2,1)} %get-tuple-element.45), channel_id=1, source_target_pairs={{0,8},{8,16},{16,24},{24,32},{32,40},{40,48},{48,56},{56,64},{64,7... | collective-permute-start | bytes 196616 | tf_op jit(solution)/shard_map/ppermute | solution.py:16
  97.1 7.9 %collective-permute-start.11 = (bf16[32,10,1,128]{3,0,2,1:T(8,128)(2,1)}, bf16[32,10,1,128]{3,0,2,1:T(8,128)(2,1)S(1)}, u32[]{:S(2)}, u32[]{:S(2)}) collective-permute-start(bf16[32,10,1,128]{3,0,2,1:T(8,128)(2,1)} %get-tuple-element.38), channel_id=1, source_target_pairs={{1,0},{2,1},{3,2},{4,3},{5,4},{6,5},{7,6},{9,8},{10,9},{11,10},{12... | collective-permute-start | bytes 245768 | tf_op jit(solution)/shard_map/ppermute | solution.py:17
  98.6 6.4 %collective-permute-start.10 = (bf16[32,10,1,128]{3,0,2,1:T(8,128)(2,1)S(1)}, bf16[32,10,1,128]{3,0,2,1:T(8,128)(2,1)S(1)}, u32[]{:S(2)}, u32[]{:S(2)}) collective-permute-start(bf16[32,10,1,128]{3,0,2,1:T(8,128)(2,1)S(1)} %get-tuple-element.37), channel_id=1, source_target_pairs={{0,1},{1,2},{2,3},{3,4},{4,5},{5,6},{6,7},{8,9},{9,10},{10,11},{11... | collective-permute-start | bytes 245768 | tf_op jit(solution)/shard_map/ppermute | solution.py:16
  118.5 10.4 %collective-permute-start.13 = (bf16[32,1,8,128]{3,0,2,1:T(8,128)(2,1)S(1)}, bf16[32,1,8,128]{3,0,2,1:T(8,128)(2,1)S(1)}, u32[]{:S(2)}, u32[]{:S(2)}) collective-permute-start(bf16[32,1,8,128]{3,0,2,1:T(8,128)(2,1)S(1)} %get-tuple-element.44), channel_id=1, source_target_pairs={{8,0},{16,8},{24,16},{32,24},{40,32},{48,40},{56,48},{64,56},{72,6... | collective-permute-start | bytes 196616 | tf_op jit(solution)/shard_map/ppermute | solution.py:17
  120.4 8.4 %collective-permute-start.12 = (bf16[32,1,8,128]{3,0,2,1:T(8,128)(2,1)S(1)}, bf16[32,1,8,128]{3,0,2,1:T(8,128)(2,1)S(1)}, u32[]{:S(2)}, u32[]{:S(2)}) collective-permute-start(bf16[32,1,8,128]{3,0,2,1:T(8,128)(2,1)S(1)} %get-tuple-element.43), channel_id=1, source_target_pairs={{0,8},{8,16},{16,24},{24,32},{32,40},{40,48},{48,56},{56,64},{64,7... | collective-permute-start | bytes 196616 | tf_op jit(solution)/shard_map/ppermute | solution.py:16
  128.9 166.3 %collective-permute-start.15 = (bf16[32,10,1,128]{3,0,2,1:T(8,128)(2,1)S(1)}, bf16[32,10,1,128]{3,0,2,1:T(8,128)(2,1)S(1)}, u32[]{:S(2)}, u32[]{:S(2)}) collective-permute-start(bf16[32,10,1,128]{3,0,2,1:T(8,128)(2,1)S(1)} %get-tuple-element.36), channel_id=1, source_target_pairs={{1,0},{2,1},{3,2},{4,3},{5,4},{6,5},{7,6},{9,8},{10,9},{11,10},{12... | collective-permute-start | bytes 245768 | tf_op jit(solution)/shard_map/ppermute | solution.py:17
  130.2 165.0 %collective-permute-start.14 = (bf16[32,10,1,128]{3,0,2,1:T(8,128)(2,1)S(1)}, bf16[32,10,1,128]{3,0,2,1:T(8,128)(2,1)S(1)}, u32[]{:S(2)}, u32[]{:S(2)}) collective-permute-start(bf16[32,10,1,128]{3,0,2,1:T(8,128)(2,1)S(1)} %get-tuple-element.35), channel_id=1, source_target_pairs={{0,1},{1,2},{2,3},{3,4},{4,5},{5,6},{6,7},{8,9},{9,10},{10,11},{11... | collective-permute-start | bytes 245768 | tf_op jit(solution)/shard_map/ppermute | solution.py:16
  (35 other events, 61.1 us)
Sparse Core Ops, SparseCore 0:
  129.0 161.5 all-reduce.6
where the time goes:
time: 312 us; the launch traced here: 310 us
  waiting for transfers between devices  159 us (51%)
  starting transfers between devices  47.5 us (15%)
  local copies, waits for them, and re-layouts  41.2 us (13%)
  matrix products  29.3 us (9%)
  other arithmetic  17.8 us (6%)
  between operations  15.2 us (5%)
    psum x1, waiting for transfers between devices, together(): running = lax.psum(ravelled, axis)  156 us
    ppermute x8, starting transfers between devices, padded_2(): before = lax.ppermute(last, axis, up)  33 us
    dot_general x36, matrix products, convolve(): jnp.einsum('ok,kxyz->oxyz', kernel, window, preferred_element_type=jnp.fl...  15.9 us
    ppermute x8, starting transfers between devices, padded_2(): after = lax.ppermute(first, axis, down)  14.4 us
    dot_general x18, matrix products, weight_grad(): jnp.einsum('oxyz,kxyz->ok', upstream, window, preferred_element_type=jnp....  13.4 us
    reshape x2, local copies, waits for them, and re-layouts, expand(): jnp.repeat(jnp.repeat(jnp.repeat(field, factor, axis=-3), factor, axis=-2...  7.38 us
    concatenate x4, other arithmetic, padded_2(): x = jnp.concatenate([before, x, after], axis=dim)  6.97 us
    unnamed x88, local copies, waits for them, and re-layouts  6.91 us
  transfers between devices with their start and end apart: 17, of which 4 were waited for; matrix products, arithmetic and copies ran while one was open for 12% of the time, Pallas kernels for 0%

commit v1 on v0

--- a/solution.py
+++ b/solution.py
@@ -19,11 +19,20 @@
     return x
 
 
-def together(arrays, axis):
-    ravelled, at, outs = (jnp.concatenate([a.reshape(-1) for a in arrays]), 0, [])
-    running = lax.psum(ravelled, axis)
+def together(arrays, axes):
+    devices = 1
+    for axis in axes:
+        devices *= lax.axis_size(axis)
+    flat = jnp.concatenate([a.reshape(-1) for a in arrays])
+    rows = -(-flat.size // (devices * 128))
+    flat = jnp.pad(flat, (0, devices * rows * 128 - flat.size)).astype(jnp.bfloat16)
+    parts = lax.all_to_all(flat.reshape(devices, rows, 128), axes, 0, 0, tiled=True)
+    mine = jnp.sum(parts.astype(jnp.float32), axis=0).astype(jnp.bfloat16)
+    spread = jnp.broadcast_to(mine[None], (devices, rows, 128))
+    summed = lax.all_to_all(spread, axes, 0, 0, tiled=True).reshape(-1).astype(jnp.float32)
+    outs, at = [], 0
     for a in arrays:
-        outs.append(running[at : at + a.size].reshape(a.shape))
+        outs.append(summed[at : at + a.size].reshape(a.shape))
         at += a.size
     return tuple(outs)
 

time: 312 us -> 190 us (0.61)
  waiting for transfers between devices: 159 us -> 8.26 us
  starting transfers between devices: 47.5 us -> 85 us
  between operations: 15.2 us -> 1.84 us
    psum x1 -> x0, waiting for transfers between devices: 156 us -> none  [together(): running = lax.psum(ravelled, axis)]
    all_to_all x0 -> x2, starting transfers between devices: none -> 36.1 us  [the longest x1 28.3 us: together(): lax.all_to_all(flat.reshape(devices, rows, 128), axes, 0, 0, tiled=True)]
    another operation x18, local copies, waits for them, and re-layouts: 1.62 us -> 11.1 us  [convolve(): kernel = weight[:, row_off, col_off].reshape(channels, -1)]
    all_to_all x0 -> x2, waiting for transfers between devices: none -> 6.56 us  [the longest x1 4.4 us: together(): lax.all_to_all(flat.reshape(devices, rows, 128), axes, 0, 0, tiled=True)]
    unnamed x88 -> x98, local copies, waits for them, and re-layouts: 6.91 us -> 4.7 us
  transfers between devices with their start and end apart: 17 -> 18, of which waited for: 4 -> 4; matrix products, arithmetic and copies ran while one was open for 12% -> 25% of each run, Pallas kernels for 0% -> 0%
where the time goes in v1:
time: 190 us; the launch traced here: 188 us
  starting transfers between devices  85 us (45%)
  local copies, waits for them, and re-layouts  44 us (23%)
  matrix products  28.8 us (15%)
  other arithmetic  20.2 us (11%)
  waiting for transfers between devices  8.26 us (4%)
    ppermute x8, starting transfers between devices, padded_2(): before = lax.ppermute(last, axis, up)  34.7 us
    all_to_all x1, starting transfers between devices, together(): lax.all_to_all(flat.reshape(devices, rows, 128), axes, 0, 0, tiled=True)  28.3 us
    dot_general x36, matrix products, convolve(): jnp.einsum('ok,kxyz->oxyz', kernel, window, preferred_element_type=jnp.fl...  16 us
    ppermute x8, starting transfers between devices, padded_2(): after = lax.ppermute(first, axis, down)  14.2 us
    dot_general x18, matrix products, weight_grad(): jnp.einsum('oxyz,kxyz->ok', upstream, window, preferred_element_type=jnp....  12.8 us
    another operation x18, local copies, waits for them, and re-layouts, convolve(): kernel = weight[:, row_off, col_off].reshape(channels, -1)  11.1 us
    all_to_all x1, starting transfers between devices, together(): lax.all_to_all(spread, axes, 0, 0, tiled=True).reshape(-1)  7.77 us
    reshape x2, local copies, waits for them, and re-layouts, expand(): jnp.repeat(jnp.repeat(jnp.repeat(field, factor, axis=-3), factor, axis=-2...  7.29 us
  transfers between devices with their start and end apart: 18, of which 4 were waited for; matrix products, arithmetic and copies ran while one was open for 25% of the time, Pallas kernels for 0%

profile of v1, /device:TPU:1, one launch (start us, length us, event | category | flops | bytes accessed | tf_op | source)
XLA Modules:
  0.0 188.1 jit_solution(8800664745096699252)
XLA Ops:
  3.7 3.3 %collective-permute-start.1 = (bf16[32,1,8,128]{3,0,2,1:T(8,128)(2,1)S(1)}, bf16[32,1,8,128]{3,0,2,1:T(8,128)(2,1)S(1)}, u32[]{:S(2)}, u32[]{:S(2)}) collective-permute-start(bf16[32,1,8,128]{3,0,2,1:T(8,128)(2,1)S(1)} %get-tuple-element.58), channel_id=1, source_target_pairs={{8,0},{16,8},{24,16},{32,24},{40,32},{48,40},{56,48},{64,56},{72,6... | collective-permute-start | bytes 196616 | tf_op jit(solution)/shard_map/ppermute | solution.py:17
  7.0 3.6 %collective-permute-start = (bf16[32,1,8,128]{3,0,2,1:T(8,128)(2,1)S(1)}, bf16[32,1,8,128]{3,0,2,1:T(8,128)(2,1)S(1)}, u32[]{:S(2)}, u32[]{:S(2)}) collective-permute-start(bf16[32,1,8,128]{3,0,2,1:T(8,128)(2,1)S(1)} %get-tuple-element.57), channel_id=1, source_target_pairs={{0,8},{8,16},{16,24},{24,32},{32,40},{40,48},{48,56},{56,64},{64,7... | collective-permute-start | bytes 196616 | tf_op jit(solution)/shard_map/ppermute | solution.py:16
  14.0 4.0 %collective-permute-start.2 = (bf16[32,10,1,128]{3,0,2,1:T(8,128)(2,1)}, bf16[32,10,1,128]{3,0,2,1:T(8,128)(2,1)S(1)}, u32[]{:S(2)}, u32[]{:S(2)}) collective-permute-start(bf16[32,10,1,128]{3,0,2,1:T(8,128)(2,1)} %get-tuple-element.49), channel_id=1, source_target_pairs={{0,1},{1,2},{2,3},{3,4},{4,5},{5,6},{6,7},{8,9},{9,10},{10,11},{11... | collective-permute-start | bytes 245768 | tf_op jit(solution)/shard_map/ppermute | solution.py:16
  26.2 2.3 %broadcast_in_dim.54 = f32[32,8,8,64,2]{0,2,4,3,1:T(8,128)} broadcast(f32[32,8,8,64]{0,2,3,1:T(8,128)S(1)} %bitcast.349), dimensions={0,1,2,3} | broadcast | bytes 1572864 | tf_op jit(solution)/shard_map/broadcast_in_dim | solution.py:82
  28.4 3.6 %copy.281 = f32[32,8,8,128]{3,0,2,1:T(8,128)} copy(f32[32,8,8,128]{0,2,3,1:T(8,128)} %bitcast.343) | data formatting | bytes 2097152 | tf_op jit(solution)/shard_map/reshape | solution.py:82
  33.2 2.3 %broadcast_in_dim.51 = s32[32,8,8,64,2]{0,2,4,3,1:T(8,128)} broadcast(s32[32,8,8,64]{0,2,3,1:T(8,128)S(1)} %bitcast.350), dimensions={0,1,2,3} | broadcast | bytes 1572864 | tf_op jit(solution)/shard_map/broadcast_in_dim | solution.py:82
  35.5 3.6 %copy.279 = s32[32,8,8,128]{3,0,2,1:T(8,128)} copy(s32[32,8,8,128]{0,2,3,1:T(8,128)} %bitcast.344) | data formatting | bytes 2097152 | tf_op jit(solution)/shard_map/reshape | solution.py:82
  44.3 1.5 fusion.20
  52.2 1.9 %collective-permute-start.5 = (bf16[32,1,8,128]{3,0,2,1:T(8,128)(2,1)S(1)}, bf16[32,1,8,128]{3,0,2,1:T(8,128)(2,1)S(1)}, u32[]{:S(2)}, u32[]{:S(2)}) collective-permute-start(bf16[32,1,8,128]{3,0,2,1:T(8,128)(2,1)S(1)} %get-tuple-element.56), channel_id=1, source_target_pairs={{8,0},{16,8},{24,16},{32,24},{40,32},{48,40},{56,48},{64,56},{72,6... | collective-permute-start | bytes 196616 | tf_op jit(solution)/shard_map/ppermute | solution.py:17
  54.1 4.7 %collective-permute-start.4 = (bf16[32,1,8,128]{3,0,2,1:T(8,128)(2,1)S(1)}, bf16[32,1,8,128]{3,0,2,1:T(8,128)(2,1)S(1)}, u32[]{:S(2)}, u32[]{:S(2)}) collective-permute-start(bf16[32,1,8,128]{3,0,2,1:T(8,128)(2,1)S(1)} %get-tuple-element.55), channel_id=1, source_target_pairs={{0,8},{8,16},{16,24},{24,32},{32,40},{40,48},{48,56},{56,64},{64,7... | collective-permute-start | bytes 196616 | tf_op jit(solution)/shard_map/ppermute | solution.py:16
  61.5 4.2 %collective-permute-start.6 = (bf16[32,10,1,128]{3,0,2,1:T(8,128)(2,1)S(1)}, bf16[32,10,1,128]{3,0,2,1:T(8,128)(2,1)S(1)}, u32[]{:S(2)}, u32[]{:S(2)}) collective-permute-start(bf16[32,10,1,128]{3,0,2,1:T(8,128)(2,1)S(1)} %get-tuple-element.47), channel_id=1, source_target_pairs={{0,1},{1,2},{2,3},{3,4},{4,5},{5,6},{6,7},{8,9},{9,10},{10,11},{11... | collective-permute-start | bytes 245768 | tf_op jit(solution)/shard_map/ppermute | solution.py:16
  73.3 1.6 fusion.427
  82.6 1.9 %collective-permute-start.9 = (bf16[32,1,8,128]{3,0,2,1:T(8,128)(2,1)}, bf16[32,1,8,128]{3,0,2,1:T(8,128)(2,1)S(1)}, u32[]{:S(2)}, u32[]{:S(2)}) collective-permute-start(bf16[32,1,8,128]{3,0,2,1:T(8,128)(2,1)} %get-tuple-element.54), channel_id=1, source_target_pairs={{8,0},{16,8},{24,16},{32,24},{40,32},{48,40},{56,48},{64,56},{72,6... | collective-permute-start | bytes 196616 | tf_op jit(solution)/shard_map/ppermute | solution.py:17
  84.5 5.4 %collective-permute-start.8 = (bf16[32,1,8,128]{3,0,2,1:T(8,128)(2,1)}, bf16[32,1,8,128]{3,0,2,1:T(8,128)(2,1)S(1)}, u32[]{:S(2)}, u32[]{:S(2)}) collective-permute-start(bf16[32,1,8,128]{3,0,2,1:T(8,128)(2,1)} %get-tuple-element.53), channel_id=1, source_target_pairs={{0,8},{8,16},{16,24},{24,32},{32,40},{40,48},{48,56},{56,64},{64,7... | collective-permute-start | bytes 196616 | tf_op jit(solution)/shard_map/ppermute | solution.py:16
  98.3 5.3 %collective-permute-start.10 = (bf16[32,10,1,128]{3,0,2,1:T(8,128)(2,1)}, bf16[32,10,1,128]{3,0,2,1:T(8,128)(2,1)}, u32[]{:S(2)}, u32[]{:S(2)}) collective-permute-start(bf16[32,10,1,128]{3,0,2,1:T(8,128)(2,1)} %get-tuple-element.45), channel_id=1, source_target_pairs={{0,1},{1,2},{2,3},{3,4},{4,5},{5,6},{6,7},{8,9},{9,10},{10,11},{11... | collective-permute-start | bytes 245768 | tf_op jit(solution)/shard_map/ppermute | solution.py:16
  104.8 2.4 %fusion.24 = bf16[32,10,10,130]{3,0,2,1:T(8,128)(2,1)S(1)} fusion(bf16[32,10,1,128]{3,0,2,1:T(8,128)(2,1)} %collective-permute-done.11, bf16[32,10,1,128]{3,0,2,1:T(8,128)(2,1)} %collective-permute-done.10, bf16[32,1,8,128]{3,0,2,1:T(8,128)(2,1)} %copy-done.5, bf16[32,8,8,128]{3,0,2,1:T(8,128)(2,1)S(1)} %get-tuple-element.102, ...), kind=kLoop, calls=%fused_computation.32 | loop fusion | flops 7488000 | bytes 1651200 | tf_op jit(solution)/shard_map/concatenate | solution.py:18
  119.7 1.9 %collective-permute-start.13 = (bf16[32,1,8,128]{3,0,2,1:T(8,128)(2,1)S(1)}, bf16[32,1,8,128]{3,0,2,1:T(8,128)(2,1)S(1)}, u32[]{:S(2)}, u32[]{:S(2)}) collective-permute-start(bf16[32,1,8,128]{3,0,2,1:T(8,128)(2,1)S(1)} %get-tuple-element.52), channel_id=1, source_target_pairs={{8,0},{16,8},{24,16},{32,24},{40,32},{48,40},{56,48},{64,56},{72,6... | collective-permute-start | bytes 196616 | tf_op jit(solution)/shard_map/ppermute | solution.py:17
  121.6 3.6 %collective-permute-start.12 = (bf16[32,1,8,128]{3,0,2,1:T(8,128)(2,1)S(1)}, bf16[32,1,8,128]{3,0,2,1:T(8,128)(2,1)S(1)}, u32[]{:S(2)}, u32[]{:S(2)}) collective-permute-start(bf16[32,1,8,128]{3,0,2,1:T(8,128)(2,1)S(1)} %get-tuple-element.51), channel_id=1, source_target_pairs={{0,8},{8,16},{16,24},{24,32},{32,40},{40,48},{48,56},{56,64},{64,7... | collective-permute-start | bytes 196616 | tf_op jit(solution)/shard_map/ppermute | solution.py:16
  128.5 28.3 %all-to-all-start = ((bf16[128,4,128]{2,1,0:T(4,128)(2,1)}), bf16[128,4,128]{2,1,0:T(4,128)(2,1)S(1)}, u32[]{:S(2)}, u32[]{:S(2)}) async-start(bf16[128,4,128]{2,1,0:T(4,128)(2,1)} %bitcast.111), calls=%async_computation | async-start | bytes 262144 | tf_op jit(solution)/shard_map/all_to_all | solution.py:29
  158.2 4.0 %collective-permute-start.14 = (bf16[32,10,1,128]{3,0,2,1:T(8,128)(2,1)S(1)}, bf16[32,10,1,128]{3,0,2,1:T(8,128)(2,1)S(1)}, u32[]{:S(2)}, u32[]{:S(2)}) collective-permute-start(bf16[32,10,1,128]{3,0,2,1:T(8,128)(2,1)S(1)} %get-tuple-element.43), channel_id=1, source_target_pairs={{0,1},{1,2},{2,3},{3,4},{4,5},{5,6},{6,7},{8,9},{9,10},{10,11},{11... | collective-permute-start | bytes 245768 | tf_op jit(solution)/shard_map/ppermute | solution.py:16
  162.2 4.4 %all-to-all-done = bf16[128,4,128]{2,1,0:T(4,128)(2,1)S(1)} async-done(((bf16[128,4,128]{2,1,0:T(4,128)(2,1)}), bf16[128,4,128]{2,1,0:T(4,128)(2,1)S(1)}, u32[]{:S(2)}, u32[]{:S(2)}) %all-to-all-start) | async-done | bytes 131104 | tf_op jit(solution)/shard_map/all_to_all | solution.py:29
  167.5 7.8 %all-to-all-start.1 = ((bf16[128,4,128]{2,1,0:T(4,128)(2,1)}), bf16[128,4,128]{2,1,0:T(4,128)(2,1)S(1)}, u32[]{:S(2)}, u32[]{:S(2)}) async-start(bf16[128,4,128]{2,1,0:T(4,128)(2,1)} %broadcast_in_dim.55), calls=%async_computation.1 | async-start | bytes 262144 | tf_op jit(solution)/shard_map/all_to_all | solution.py:32
  175.3 1.5 select_maximum_fusion
  182.9 2.2 %all-to-all-done.1 = bf16[128,4,128]{2,1,0:T(4,128)(2,1)S(1)} async-done(((bf16[128,4,128]{2,1,0:T(4,128)(2,1)}), bf16[128,4,128]{2,1,0:T(4,128)(2,1)S(1)}, u32[]{:S(2)}, u32[]{:S(2)}) %all-to-all-start.1) | async-done | bytes 131104 | tf_op jit(solution)/shard_map/all_to_all | solution.py:32
  (292 shorter events, 81.0 us)
Async XLA Ops:
  1.7 9.0 %copy-start.3 = (bf16[32,3,3,3,32]{4,0,3,2,1:T(8,128)(2,1)S(1)}, bf16[32,3,3,3,32]{4,0,3,2,1:T(8,128)(2,1)}, u32[]{:S(2)}) copy-start(bf16[32,3,3,3,32]{4,0,3,2,1:T(8,128)(2,1)} %param.12) | copy-start | bytes 165892
  1.7 9.6 %copy-start.4 = (bf16[32,3,3,3,32]{4,0,3,2,1:T(8,128)(2,1)S(1)}, bf16[32,3,3,3,32]{4,0,3,2,1:T(8,128)(2,1)}, u32[]{:S(2)}) copy-start(bf16[32,3,3,3,32]{4,0,3,2,1:T(8,128)(2,1)} %param.10) | copy-start | bytes 165892
  2.2 22.9 %copy-start.13 = (bf16[32,4,4,64]{3,2,1,0:T(4,128)(2,1)S(1)}, bf16[32,4,4,64]{3,2,1,0:T(4,128)(2,1)}, u32[]{:S(2)}) copy-start(bf16[32,4,4,64]{3,2,1,0:T(4,128)(2,1)} %param.14) | copy-start | bytes 196612
  3.7 8.3 %collective-permute-start.1 = (bf16[32,1,8,128]{3,0,2,1:T(8,128)(2,1)S(1)}, bf16[32,1,8,128]{3,0,2,1:T(8,128)(2,1)S(1)}, u32[]{:S(2)}, u32[]{:S(2)}) collective-permute-start(bf16[32,1,8,128]{3,0,2,1:T(8,128)(2,1)S(1)} %get-tuple-element.58), channel_id=1, source_target_pairs={{8,0},{16,8},{24,16},{32,24},{40,32},{48,40},{56,48},{64,56},{72,6... | collective-permute-start | bytes 196616 | tf_op jit(solution)/shard_map/ppermute | solution.py:17
  7.0 5.0 %collective-permute-start = (bf16[32,1,8,128]{3,0,2,1:T(8,128)(2,1)S(1)}, bf16[32,1,8,128]{3,0,2,1:T(8,128)(2,1)S(1)}, u32[]{:S(2)}, u32[]{:S(2)}) collective-permute-start(bf16[32,1,8,128]{3,0,2,1:T(8,128)(2,1)S(1)} %get-tuple-element.57), channel_id=1, source_target_pairs={{0,8},{8,16},{16,24},{24,32},{32,40},{40,48},{48,56},{56,64},{64,7... | collective-permute-start | bytes 196616 | tf_op jit(solution)/shard_map/ppermute | solution.py:16
  12.7 31.6 %collective-permute-start.3 = (bf16[32,10,1,128]{3,0,2,1:T(8,128)(2,1)}, bf16[32,10,1,128]{3,0,2,1:T(8,128)(2,1)S(1)}, u32[]{:S(2)}, u32[]{:S(2)}) collective-permute-start(bf16[32,10,1,128]{3,0,2,1:T(8,128)(2,1)} %get-tuple-element.50), channel_id=1, source_target_pairs={{1,0},{2,1},{3,2},{4,3},{5,4},{6,5},{7,6},{9,8},{10,9},{11,10},{12... | collective-permute-start | bytes 245768 | tf_op jit(solution)/shard_map/ppermute | solution.py:17
  14.0 30.3 %collective-permute-start.2 = (bf16[32,10,1,128]{3,0,2,1:T(8,128)(2,1)}, bf16[32,10,1,128]{3,0,2,1:T(8,128)(2,1)S(1)}, u32[]{:S(2)}, u32[]{:S(2)}) collective-permute-start(bf16[32,10,1,128]{3,0,2,1:T(8,128)(2,1)} %get-tuple-element.49), channel_id=1, source_target_pairs={{0,1},{1,2},{2,3},{3,4},{4,5},{5,6},{6,7},{8,9},{9,10},{10,11},{11... | collective-permute-start | bytes 245768 | tf_op jit(solution)/shard_map/ppermute | solution.py:16
  52.2 6.7 %collective-permute-start.5 = (bf16[32,1,8,128]{3,0,2,1:T(8,128)(2,1)S(1)}, bf16[32,1,8,128]{3,0,2,1:T(8,128)(2,1)S(1)}, u32[]{:S(2)}, u32[]{:S(2)}) collective-permute-start(bf16[32,1,8,128]{3,0,2,1:T(8,128)(2,1)S(1)} %get-tuple-element.56), channel_id=1, source_target_pairs={{8,0},{16,8},{24,16},{32,24},{40,32},{48,40},{56,48},{64,56},{72,6... | collective-permute-start | bytes 196616 | tf_op jit(solution)/shard_map/ppermute | solution.py:17
  54.1 6.0 %collective-permute-start.4 = (bf16[32,1,8,128]{3,0,2,1:T(8,128)(2,1)S(1)}, bf16[32,1,8,128]{3,0,2,1:T(8,128)(2,1)S(1)}, u32[]{:S(2)}, u32[]{:S(2)}) collective-permute-start(bf16[32,1,8,128]{3,0,2,1:T(8,128)(2,1)S(1)} %get-tuple-element.55), channel_id=1, source_target_pairs={{0,8},{8,16},{16,24},{24,32},{32,40},{40,48},{48,56},{56,64},{64,7... | collective-permute-start | bytes 196616 | tf_op jit(solution)/shard_map/ppermute | solution.py:16
  60.2 6.4 %collective-permute-start.7 = (bf16[32,10,1,128]{3,0,2,1:T(8,128)(2,1)S(1)}, bf16[32,10,1,128]{3,0,2,1:T(8,128)(2,1)S(1)}, u32[]{:S(2)}, u32[]{:S(2)}) collective-permute-start(bf16[32,10,1,128]{3,0,2,1:T(8,128)(2,1)S(1)} %get-tuple-element.48), channel_id=1, source_target_pairs={{1,0},{2,1},{3,2},{4,3},{5,4},{6,5},{7,6},{9,8},{10,9},{11,10},{12... | collective-permute-start | bytes 245768 | tf_op jit(solution)/shard_map/ppermute | solution.py:17
  61.5 5.5 %collective-permute-start.6 = (bf16[32,10,1,128]{3,0,2,1:T(8,128)(2,1)S(1)}, bf16[32,10,1,128]{3,0,2,1:T(8,128)(2,1)S(1)}, u32[]{:S(2)}, u32[]{:S(2)}) collective-permute-start(bf16[32,10,1,128]{3,0,2,1:T(8,128)(2,1)S(1)} %get-tuple-element.47), channel_id=1, source_target_pairs={{0,1},{1,2},{2,3},{3,4},{4,5},{5,6},{6,7},{8,9},{9,10},{10,11},{11... | collective-permute-start | bytes 245768 | tf_op jit(solution)/shard_map/ppermute | solution.py:16
  82.6 13.7 %collective-permute-start.9 = (bf16[32,1,8,128]{3,0,2,1:T(8,128)(2,1)}, bf16[32,1,8,128]{3,0,2,1:T(8,128)(2,1)S(1)}, u32[]{:S(2)}, u32[]{:S(2)}) collective-permute-start(bf16[32,1,8,128]{3,0,2,1:T(8,128)(2,1)} %get-tuple-element.54), channel_id=1, source_target_pairs={{8,0},{16,8},{24,16},{32,24},{40,32},{48,40},{56,48},{64,56},{72,6... | collective-permute-start | bytes 196616 | tf_op jit(solution)/shard_map/ppermute | solution.py:17
  84.5 11.8 %collective-permute-start.8 = (bf16[32,1,8,128]{3,0,2,1:T(8,128)(2,1)}, bf16[32,1,8,128]{3,0,2,1:T(8,128)(2,1)S(1)}, u32[]{:S(2)}, u32[]{:S(2)}) collective-permute-start(bf16[32,1,8,128]{3,0,2,1:T(8,128)(2,1)} %get-tuple-element.53), channel_id=1, source_target_pairs={{0,8},{8,16},{16,24},{24,32},{32,40},{40,48},{48,56},{56,64},{64,7... | collective-permute-start | bytes 196616 | tf_op jit(solution)/shard_map/ppermute | solution.py:16
  96.3 7.3 %copy-start.5 = (bf16[32,1,8,128]{3,0,2,1:T(8,128)(2,1)}, bf16[32,1,8,128]{3,0,2,1:T(8,128)(2,1)S(1)}, u32[]{:S(2)}) copy-start(bf16[32,1,8,128]{3,0,2,1:T(8,128)(2,1)S(1)} %collective-permute-done.9) | copy-start | bytes 196612
  97.0 7.8 %collective-permute-start.11 = (bf16[32,10,1,128]{3,0,2,1:T(8,128)(2,1)}, bf16[32,10,1,128]{3,0,2,1:T(8,128)(2,1)}, u32[]{:S(2)}, u32[]{:S(2)}) collective-permute-start(bf16[32,10,1,128]{3,0,2,1:T(8,128)(2,1)} %get-tuple-element.46), channel_id=1, source_target_pairs={{1,0},{2,1},{3,2},{4,3},{5,4},{6,5},{7,6},{9,8},{10,9},{11,10},{12... | collective-permute-start | bytes 245768 | tf_op jit(solution)/shard_map/ppermute | solution.py:17
  98.3 6.5 %collective-permute-start.10 = (bf16[32,10,1,128]{3,0,2,1:T(8,128)(2,1)}, bf16[32,10,1,128]{3,0,2,1:T(8,128)(2,1)}, u32[]{:S(2)}, u32[]{:S(2)}) collective-permute-start(bf16[32,10,1,128]{3,0,2,1:T(8,128)(2,1)} %get-tuple-element.45), channel_id=1, source_target_pairs={{0,1},{1,2},{2,3},{3,4},{4,5},{5,6},{6,7},{8,9},{9,10},{10,11},{11... | collective-permute-start | bytes 245768 | tf_op jit(solution)/shard_map/ppermute | solution.py:16
  119.0 7.9 %copy-start.11 = (bf16[27648]{0:T(1024)(128)(2,1)S(1)}, bf16[27648]{0:T(1024)(128)(2,1)}, u32[]{:S(2)}) copy-start(bf16[27648]{0:T(1024)(128)(2,1)} %reshape.75) | copy-start | bytes 165892
  119.0 7.9 %copy-start.44 = (bf16[32]{0:T(256)(128)(2,1)S(1)}, bf16[32]{0:T(256)(128)(2,1)}, u32[]{:S(2)}) copy-start(bf16[32]{0:T(256)(128)(2,1)} %get-tuple-element.101) | copy-start | bytes 196
  119.7 37.2 %collective-permute-start.13 = (bf16[32,1,8,128]{3,0,2,1:T(8,128)(2,1)S(1)}, bf16[32,1,8,128]{3,0,2,1:T(8,128)(2,1)S(1)}, u32[]{:S(2)}, u32[]{:S(2)}) collective-permute-start(bf16[32,1,8,128]{3,0,2,1:T(8,128)(2,1)S(1)} %get-tuple-element.52), channel_id=1, source_target_pairs={{8,0},{16,8},{24,16},{32,24},{40,32},{48,40},{56,48},{64,56},{72,6... | collective-permute-start | bytes 196616 | tf_op jit(solution)/shard_map/ppermute | solution.py:17
  121.6 35.2 %collective-permute-start.12 = (bf16[32,1,8,128]{3,0,2,1:T(8,128)(2,1)S(1)}, bf16[32,1,8,128]{3,0,2,1:T(8,128)(2,1)S(1)}, u32[]{:S(2)}, u32[]{:S(2)}) collective-permute-start(bf16[32,1,8,128]{3,0,2,1:T(8,128)(2,1)S(1)} %get-tuple-element.51), channel_id=1, source_target_pairs={{0,8},{8,16},{16,24},{24,32},{32,40},{40,48},{48,56},{56,64},{64,7... | collective-permute-start | bytes 196616 | tf_op jit(solution)/shard_map/ppermute | solution.py:16
  128.5 38.1 %all-to-all-start = ((bf16[128,4,128]{2,1,0:T(4,128)(2,1)}), bf16[128,4,128]{2,1,0:T(4,128)(2,1)S(1)}, u32[]{:S(2)}, u32[]{:S(2)}) async-start(bf16[128,4,128]{2,1,0:T(4,128)(2,1)} %bitcast.111), calls=%async_computation | async-start | bytes 262144 | tf_op jit(solution)/shard_map/all_to_all | solution.py:29
  156.9 18.3 %collective-permute-start.15 = (bf16[32,10,1,128]{3,0,2,1:T(8,128)(2,1)S(1)}, bf16[32,10,1,128]{3,0,2,1:T(8,128)(2,1)S(1)}, u32[]{:S(2)}, u32[]{:S(2)}) collective-permute-start(bf16[32,10,1,128]{3,0,2,1:T(8,128)(2,1)S(1)} %get-tuple-element.44), channel_id=1, source_target_pairs={{1,0},{2,1},{3,2},{4,3},{5,4},{6,5},{7,6},{9,8},{10,9},{11,10},{12... | collective-permute-start | bytes 245768 | tf_op jit(solution)/shard_map/ppermute | solution.py:17
  158.2 17.1 %collective-permute-start.14 = (bf16[32,10,1,128]{3,0,2,1:T(8,128)(2,1)S(1)}, bf16[32,10,1,128]{3,0,2,1:T(8,128)(2,1)S(1)}, u32[]{:S(2)}, u32[]{:S(2)}) collective-permute-start(bf16[32,10,1,128]{3,0,2,1:T(8,128)(2,1)S(1)} %get-tuple-element.43), channel_id=1, source_target_pairs={{0,1},{1,2},{2,3},{3,4},{4,5},{5,6},{6,7},{8,9},{9,10},{10,11},{11... | collective-permute-start | bytes 245768 | tf_op jit(solution)/shard_map/ppermute | solution.py:16
  167.5 17.6 %all-to-all-start.1 = ((bf16[128,4,128]{2,1,0:T(4,128)(2,1)}), bf16[128,4,128]{2,1,0:T(4,128)(2,1)S(1)}, u32[]{:S(2)}, u32[]{:S(2)}) async-start(bf16[128,4,128]{2,1,0:T(4,128)(2,1)} %broadcast_in_dim.55), calls=%async_computation.1 | async-start | bytes 262144 | tf_op jit(solution)/shard_map/all_to_all | solution.py:32
  (41 other events, 69.1 us)

commit v2 on v0

v2 whole, which is shorter than its diff:
```python
import math

import jax
import jax.numpy as jnp
from jax import lax
from jax.experimental import pallas as pl
from jax.experimental.pallas import tpu as pltpu
from jax.sharding import PartitionSpec as P

BF = jnp.bfloat16
F32 = jnp.float32
HALO = 4


def shift(v, axis, step):
    devices = lax.axis_size(axis)
    pairs = [(i, i + step) for i in range(devices) if 0 <= i + step < devices]
    return lax.ppermute(v, axis, pairs)


def toeplitz(kernel):
    k = kernel.transpose(3, 0, 1, 2, 4)
    zero = jnp.zeros_like(k[:, :, :, :1])
    lower = jnp.concatenate([k, zero], axis=3)
    upper = jnp.concatenate([zero, k], axis=3)
    chan = kernel.shape[0]
    return jnp.stack([lower, upper], axis=0).reshape(6 * chan, 12 * chan)


def flipped(weight):
    return jnp.flip(weight, (1, 2, 3)).transpose(4, 1, 2, 3, 0)


def section(own, xlow, xhigh, ylow, yhigh, pown, mask, w1, w2, f2, f1, b1, b2,
            out, parts, feat, pool, hid, two, one, ups, acc1, acc2):
    C, Z = 32, 128
    N = out.shape[0]
    H = HALO
    W = N + 2 * H
    Q = N // 2
    PW = Q + 2
    feat[H:H + N, H * C:(H + N) * C, :] = own[...]
    for k in range(H):
        for y in range(N):
            r = slice((H + y) * C, (H + y + 1) * C)
            feat[k, r, :] = xlow[k * N + y]
            feat[H + N + k, r, :] = xhigh[k * N + y]
    for x in range(W):
        for k in range(H):
            feat[x, k * C:(k + 1) * C, :] = ylow[x * H + k]
            feat[x, (H + N + k) * C:(H + N + k + 1) * C, :] = yhigh[x * H + k]
    pool[1:1 + Q, C:(1 + Q) * C, :] = pown[...]
    for y in range(Q):
        r = slice((1 + y) * C, (2 + y) * C)
        pool[0, r, :] = xlow[H * N + y]
        pool[1 + Q, r, :] = xhigh[H * N + y]
    for x in range(PW):
        pool[x, 0:C, :] = ylow[W * H + x]
        pool[x, (1 + Q) * C:(2 + Q) * C, :] = yhigh[W * H + x]
    row = lax.broadcasted_iota(jnp.int32, (Z, 2 * Z), 0)
    col = lax.broadcasted_iota(jnp.int32, (Z, 2 * Z), 1)
    spread = jnp.where(row == col // 2, 1.0, 0.0).astype(BF)
    for x in range(PW):
        ups[x] = jnp.dot(pool[x], spread, preferred_element_type=F32)

    lane = lax.broadcasted_iota(jnp.int32, (C, Z), 1)
    at_start = lane == 0
    at_end = lane == Z - 1
    odd = (lane % 2).astype(F32)

    def after(v):
        return jnp.where(at_start, 0.0, pltpu.roll(v, 1, 1))

    def before(v):
        return jnp.where(at_end, 0.0, pltpu.roll(v, Z - 1, 1))

    def conv(src, weight, width, write):
        def trip(i, carry):
            x = 2 * i
            for j in range(width // 2):
                y = 2 * j
                r = slice(y * C, (y + 4) * C)
                rows = [src[x + d, r, :] for d in range(4)]
                tile = jnp.concatenate(
                    [jnp.concatenate([rows[d], rows[d + 1]], axis=1) for d in range(3)], axis=0)
                got = jnp.dot(weight[...], tile, preferred_element_type=F32)
                for xo in range(2):
                    for yo in range(2):
                        g = got[yo * 3 * C:(yo + 1) * 3 * C, xo * Z:(xo + 1) * Z]
                        v = g[C:2 * C] + after(g[0:C]) + before(g[2 * C:])
                        write(i, j, xo, yo, v)
            return carry
        lax.fori_loop(0, width // 2, trip, 0)

    def mask_of(i, j, xo, yo, reach):
        bx = (2 * i + xo + 8 - reach) >> 3
        by = (2 * j + yo + 8 - reach) >> 3
        return mask[bx][by:by + 1, :]

    def cell(y):
        return slice(y * C, (y + 1) * C)

    def write_hidden(i, j, xo, yo, v):
        m = mask_of(i, j, xo, yo, H - 1)
        hid[2 * i + xo, cell(2 * j + yo), :] = (jnp.maximum(v + b1[...], 0.0) * m).astype(BF)

    def write_two(i, j, xo, yo, v):
        m = mask_of(i, j, xo, yo, H - 2)
        grad = ups[i, cell(j), 0:Z]
        pick = ups[i, cell(j), Z:2 * Z]
        live = (pick == odd + float(4 * xo + 2 * yo)) & (v + b2[...] > 0.0)
        two[2 * i + xo, cell(2 * j + yo), :] = jnp.where(live, grad * m, 0.0).astype(BF)

    def write_one(i, j, xo, yo, v):
        h = hid[2 * i + xo + 2, cell(2 * j + yo + 2), :].astype(F32)
        one[2 * i + xo, cell(2 * j + yo), :] = jnp.where(h > 0.0, v, 0.0).astype(BF)

    def write_out(i, j, xo, yo, v):
        m = mask_of(i, j, xo, yo, 0)
        out[2 * i + xo, cell(2 * j + yo), :] = (v * m).astype(BF)

    conv(feat, w1, W - 2, write_hidden)
    conv(hid, w2, W - 4, write_two)
    conv(two, f2, W - 6, write_one)
    conv(one, f1, W - 8, write_out)

    def weight_grad(src, off_s, delta, off_d, acc):
        def trip(x, sums):
            total, bias = sums
            lefts, rights = [], []
            for y in range(N):
                d = delta[x + off_d, cell(y + off_d), :].astype(F32)
                bias = bias + d
                rights.append(jnp.concatenate([before(d), d, after(d)], axis=0).astype(BF))
            right = jnp.concatenate(rights, axis=1)
            left = jnp.concatenate(
                [jnp.concatenate(
                    [src[x + off_s + a, (y + off_s) * C:(y + off_s + 3) * C, :] for y in range(N)],
                    axis=1) for a in range(3)], axis=0)
            got = lax.dot_general(left, right, (((1,), (1,)), ((), ())), preferred_element_type=F32)
            acc[...] += got
            return total, bias
        acc[...] = jnp.zeros_like(acc)
        _, bias = lax.fori_loop(0, N, trip, (0, jnp.zeros((C, Z), F32)))
        return jnp.broadcast_to(jnp.sum(bias, axis=1, keepdims=True), (C, Z))

    bias2 = weight_grad(hid, H - 2, two, H - 2, acc2)
    bias1 = weight_grad(feat, H - 1, one, H - 3, acc1)
    rows9 = 9 * C
    pad = jnp.zeros((rows9, Z - 3 * C), F32)
    parts[0:rows9, :] = jnp.concatenate([acc1[...], pad], axis=1).astype(BF)
    parts[rows9:2 * rows9, :] = jnp.concatenate([acc2[...], pad], axis=1).astype(BF)
    parts[2 * rows9:2 * rows9 + C, :] = bias1.astype(BF)
    parts[2 * rows9 + C:2 * rows9 + 2 * C, :] = bias2.astype(BF)


def body(features, occupancy, weight_one, bias_one, weight_two, bias_two, grad_pooled, pool_choice):
    C, nx, ny, Z = features.shape
    qx, qy = nx // 2, ny // 2
    H = HALO
    axes = ("gx", "gy")
    devices = lax.axis_size("gx") * lax.axis_size("gy")
    flags = jnp.pad(occupancy, ((1, 1), (1, 1), (0, 0)))
    window = lax.dynamic_slice(
        flags, (lax.axis_index("gx"), lax.axis_index("gy"), jnp.int32(0)), (3, 3, occupancy.shape[2]))
    mask = jnp.repeat(window, 8, axis=2).astype(F32)
    own = features.transpose(1, 2, 0, 3) * mask[1, 1].astype(BF)
    mask = jnp.pad(mask, ((0, 0), (0, 5), (0, 0)))
    pown = jnp.concatenate([grad_pooled, pool_choice.astype(BF)], axis=3).transpose(1, 2, 0, 3)

    def msg(cells, pooled):
        return jnp.concatenate([cells.reshape(-1, C, Z), pooled.reshape(-1, C, Z)], axis=0)

    xlow = shift(msg(own[nx - H:], pown[qx - 1:]), "gx", 1)
    xhigh = shift(msg(own[:H], pown[:1]), "gx", -1)

    def side(ys, qs):
        def pieces(m):
            return m[:H * ny].reshape(H, ny, C, Z)[:, ys], m[H * ny:].reshape(1, qy, C, Z)[:, qs]
        lc, lp = pieces(xlow)
        hc, hp = pieces(xhigh)
        return msg(jnp.concatenate([lc, own[:, ys], hc], axis=0),
                   jnp.concatenate([lp, pown[:, qs], hp], axis=0))

    ylow = shift(side(slice(ny - H, ny), slice(qy - 1, qy)), "gy", 1)
    yhigh = shift(side(slice(0, H), slice(0, 1)), "gy", -1)

    w = nx + 2 * H
    out, parts = pl.pallas_call(
        section,
        out_shape=(jax.ShapeDtypeStruct((nx, ny * C, Z), BF),
                   jax.ShapeDtypeStruct((20 * C, Z), BF)),
        scratch_shapes=[
            pltpu.VMEM((w, w * C, Z), BF),
            pltpu.VMEM((qx + 2, (qy + 2) * C, Z), BF),
            pltpu.VMEM((w - 2, (w - 2) * C, Z), BF),
            pltpu.VMEM((w - 4, (w - 4) * C, Z), BF),
            pltpu.VMEM((w - 6, (w - 6) * C, Z), BF),
            pltpu.VMEM((qx + 2, (qy + 2) * C, 2 * Z), F32),
            pltpu.VMEM((9 * C, 3 * C), F32),
            pltpu.VMEM((9 * C, 3 * C), F32),
        ],
        compiler_params=pltpu.CompilerParams(vmem_limit_bytes=40 << 20),
        name="section",
    )(own.reshape(nx, ny * C, Z), xlow, xhigh, ylow, yhigh, pown.reshape(qx, qy * C, Z), mask,
      toeplitz(weight_one), toeplitz(weight_two), toeplitz(flipped(weight_two)),
      toeplitz(flipped(weight_one)),
      jnp.broadcast_to(bias_one[:, None], (C, Z)), jnp.broadcast_to(bias_two[:, None], (C, Z)))

    rows = 20 * C // devices
    got = lax.all_to_all(parts.reshape(devices, rows, Z), axes, 0, 0, tiled=True)
    mine = jnp.sum(got.astype(F32), axis=0).astype(BF)
    spread = jnp.broadcast_to(mine[None], (devices, rows, Z))
    summed = lax.all_to_all(spread, axes, 0, 0, tiled=True).reshape(20 * C, Z).astype(F32)
    cells = nx * lax.axis_size("gx") * ny * lax.axis_size("gy") * Z
    summed = summed * (1.0 / math.sqrt(cells))

    def unpack(block):
        return block[:, :3 * C].reshape(3, 3, C, 3, C).transpose(4, 0, 1, 3, 2)

    grad_input = out.reshape(nx, ny, C, Z).transpose(2, 0, 1, 3)
    return (grad_input, unpack(summed[:9 * C]), summed[18 * C:19 * C, 0],
            unpack(summed[9 * C:18 * C]), summed[19 * C:, 0])


def solution(mesh):
    cell = P(None, "gx", "gy", None)
    return jax.shard_map(
        body,
        mesh=mesh,
        in_specs=(cell, P(), P(), P(), P(), P(), cell, cell),
        out_specs=(cell, P(), P(), P(), P()),
        check_vma=False,
    )
```

time: 312 us -> 105 us (0.34)
  waiting for transfers between devices: 159 us -> 13.7 us
  starting transfers between devices: 47.5 us -> 16.4 us
  matrix products: 29.3 us -> 0 us
  blocking collectives: 0 us -> 26.1 us
  local copies, waits for them, and re-layouts: 41.2 us -> 22.1 us
  Pallas kernels: 0 us -> 18.7 us
  between operations: 15.2 us -> 1.11 us
  other arithmetic: 17.8 us -> 6.73 us
    psum x1 -> x0, waiting for transfers between devices: 156 us -> none  [together(): running = lax.psum(ravelled, axis)]
    ppermute x16 -> x4, starting transfers between devices: 47.5 us -> 12.1 us  [shift(): return lax.ppermute(v, axis, pairs)]
    dot_general x54 -> x0, matrix products: 29.3 us -> none  [the longest x36 15.9 us: convolve(): jnp.einsum('ok,kxyz->oxyz', kernel, window, preferred_element_type=jnp.fl...]
    all_to_all x0 -> x1, blocking collectives: none -> 26.1 us  [body(): lax.all_to_all(parts.reshape(devices, rows, Z), axes, 0, 0, tiled=True)]
    pallas_call x0 -> x1, Pallas kernels: none -> 18.7 us  [body(): pl.pallas_call(section, out_shape=(jax.ShapeDtypeStruct((nx, ny * C, Z),...]
    all_to_all x0 -> x1, waiting for transfers between devices: none -> 10 us  [body(): lax.all_to_all(spread, axes, 0, 0, tiled=True).reshape(20 * C, Z)]
    concatenate x8 -> x6, other arithmetic: 10.4 us -> 4.09 us  [the longest x4 3.24 us: msg(): jnp.concatenate([cells.reshape(-1, C, Z), pooled.reshape(-1, C, Z)], axis=0)]
    broadcast_in_dim x7 -> x4, local copies, waits for them, and re-layouts: 6.27 us -> 0.96 us  [the longest x1 0.74 us: body(): spread = jnp.broadcast_to(mine[None], (devices, rows, Z))]
  transfers between devices with their start and end apart: 17 -> 5, of which waited for: 4 -> 3; matrix products, arithmetic and copies ran while one was open for 12% -> 13% of each run, Pallas kernels for 0% -> 0%
where the time goes in v2:
time: 105 us
  blocking collectives  26.1 us (25%)
  local copies, waits for them, and re-layouts  22.1 us (21%)
  Pallas kernels  18.7 us (18%)
  starting transfers between devices  16.4 us (16%)
  waiting for transfers between devices  13.7 us (13%)
  other arithmetic  6.73 us (6%)
  between operations  1.11 us (1%)
    all_to_all x1, blocking collectives, body(): lax.all_to_all(parts.reshape(devices, rows, Z), axes, 0, 0, tiled=True)  26.1 us
    pallas_call x1, Pallas kernels, body(): pl.pallas_call(section, out_shape=(jax.ShapeDtypeStruct((nx, ny * C, Z),...  18.7 us
    ppermute x4, starting transfers between devices, shift(): return lax.ppermute(v, axis, pairs)  12.1 us
    all_to_all x1, waiting for transfers between devices, body(): lax.all_to_all(spread, axes, 0, 0, tiled=True).reshape(20 * C, Z)  10 us
    unnamed x25, local copies, waits for them, and re-layouts  7.41 us
    another operation x8, local copies, waits for them, and re-layouts, toeplitz(): return jnp.stack([lower, upper], axis=0).reshape(6 * chan, 12 * chan)  5.14 us
    all_to_all x1, starting transfers between devices, body(): lax.all_to_all(spread, axes, 0, 0, tiled=True).reshape(20 * C, Z)  4.25 us
    ppermute x4, waiting for transfers between devices, shift(): return lax.ppermute(v, axis, pairs)  3.72 us
  transfers between devices with their start and end apart: 5, of which 3 were waited for; matrix products, arithmetic and copies ran while one was open for 13% of the time, Pallas kernels for 0%

profile of v2, /device:TPU:1, one launch (start us, length us, event | category | flops | bytes accessed | tf_op | source)
XLA Modules:
  0.0 104.8 jit_solution(3380928228566996665)
XLA Ops:
  1.6 1.1 %multiply_bitcast_fusion = bf16[8,8,32,128]{3,1,0,2:T(8,128)(2,1)S(1)} fusion(bf16[32,8,8,128]{3,2,1,0:T(8,128)(2,1)} %param.8, bf16[128]{0:T(256)(128)(2,1)S(1)} %fusion.1), kind=kLoop, calls=%fused_computation.10 | loop fusion | flops 262144 | bytes 1048832 | tf_op jit(solution)/shard_map/mul | solution.py:167
  3.7 0.9 copy-done.5
  5.5 4.9 %collective-permute-start = (bf16[36,32,128]{2,1,0:T(8,128)(2,1)}, bf16[36,32,128]{2,1,0:T(8,128)(2,1)S(1)}, u32[]{:S(2)}, u32[]{:S(2)}) collective-permute-start(bf16[36,32,128]{2,1,0:T(8,128)(2,1)} %pad_maximum_fusion.8), channel_id=1, source_target_pairs={{0,8},{8,16},{16,24},{24,32},{32,40},{40,48},{48,56},{56,64},{64,7... | collective-permute-start | bytes 884744 | tf_op jit(solution)/shard_map/ppermute | solution.py:18
  11.3 1.9 %collective-permute-start.1 = (bf16[36,32,128]{2,1,0:T(8,128)(2,1)}, bf16[36,32,128]{2,1,0:T(8,128)(2,1)S(1)}, u32[]{:S(2)}, u32[]{:S(2)}) collective-permute-start(bf16[36,32,128]{2,1,0:T(8,128)(2,1)} %pad_maximum_fusion.9), channel_id=1, source_target_pairs={{8,0},{16,8},{24,16},{32,24},{40,32},{48,40},{56,48},{64,56},{72,6... | collective-permute-start | bytes 884744 | tf_op jit(solution)/shard_map/ppermute | solution.py:18
  14.3 0.8 copy-done.2
  17.4 2.2 %collective-permute-done.1.xhigh = bf16[36,32,128]{2,1,0:T(8,128)(2,1)S(1)} collective-permute-done((bf16[36,32,128]{2,1,0:T(8,128)(2,1)}, bf16[36,32,128]{2,1,0:T(8,128)(2,1)S(1)}, u32[]{:S(2)}, u32[]{:S(2)}) %collective-permute-start.1) | collective-permute-done | bytes 294944 | tf_op jit(solution)/shard_map/ppermute | solution.py:18
  21.0 0.9 pad_maximum_fusion.5
  21.9 1.3 %collective-permute-start.3 = (bf16[70,32,128]{2,1,0:T(8,128)(2,1)}, bf16[70,32,128]{2,1,0:T(8,128)(2,1)S(1)}, u32[]{:S(2)}, u32[]{:S(2)}) collective-permute-start(bf16[70,32,128]{2,1,0:T(8,128)(2,1)} %pad_maximum_fusion.5), channel_id=1, source_target_pairs={{1,0},{2,1},{3,2},{4,3},{5,4},{6,5},{7,6},{9,8},{10,9},{11,10},{12... | collective-permute-start | bytes 1720328 | tf_op jit(solution)/shard_map/ppermute | solution.py:18
  23.5 0.9 pad_maximum_fusion.4
  24.4 4.0 %collective-permute-start.2 = (bf16[70,32,128]{2,1,0:T(8,128)(2,1)}, bf16[70,32,128]{2,1,0:T(8,128)(2,1)S(1)}, u32[]{:S(2)}, u32[]{:S(2)}) collective-permute-start(bf16[70,32,128]{2,1,0:T(8,128)(2,1)} %pad_maximum_fusion.4), channel_id=1, source_target_pairs={{0,1},{1,2},{2,3},{3,4},{4,5},{5,6},{6,7},{8,9},{9,10},{10,11},{11... | collective-permute-start | bytes 1720328 | tf_op jit(solution)/shard_map/ppermute | solution.py:18
  28.6 1.1 %copy.70 = bf16[2,3,32,3,4,32]{5,4,3,2,1,0:T(4,128)(2,1)} copy(bf16[2,3,32,3,4,32]{2,5,1,4,3,0:T(8,128)(2,1)S(1)} %pad_maximum_fusion.3) | data formatting | bytes 294912 | tf_op jit(solution)/shard_map/stack | solution.py:27
  29.7 1.5 %reshape.112.f1 = bf16[192,384]{1,0:T(8,128)(2,1)S(1)} reshape(bf16[2,3,32,3,4,32]{5,4,3,2,1,0:T(4,128)(2,1)} %copy.70) | data formatting | bytes 294912 | tf_op jit(solution)/shard_map/reshape | solution.py:27
  32.2 1.2 %pad_bitcast_fusion.5 = (bf16[1,3,32,3,4,32]{5,2,1,4,3,0:T(8,128)(2,1)S(1)}, bf16[1,3,32,3,4,32]{5,2,1,4,3,0:T(8,128)(2,1)S(1)}) fusion(bf16[3,32,3,3,32]{4,1,0,3,2:T(8,128)(2,1)} %bitcast.76), kind=kLoop, calls=%fused_computation.18 | loop fusion | bytes 202752 | tf_op jit(solution)/shard_map/stack | solution.py:27
  33.5 1.1 %copy.68 = bf16[2,3,32,3,4,32]{5,4,3,2,1,0:T(4,128)(2,1)} copy(bf16[2,3,32,3,4,32]{5,2,1,4,3,0:T(8,128)(2,1)S(1)} %pad_maximum_fusion.1) | data formatting | bytes 294912 | tf_op jit(solution)/shard_map/stack | solution.py:27
  34.6 1.5 %reshape.110.w2 = bf16[192,384]{1,0:T(8,128)(2,1)S(1)} reshape(bf16[2,3,32,3,4,32]{5,4,3,2,1,0:T(4,128)(2,1)} %copy.68) | data formatting | bytes 294912 | tf_op jit(solution)/shard_map/reshape | solution.py:27
  36.1 1.6 %collective-permute-done.2.ylow = bf16[70,32,128]{2,1,0:T(8,128)(2,1)S(1)} collective-permute-done((bf16[70,32,128]{2,1,0:T(8,128)(2,1)}, bf16[70,32,128]{2,1,0:T(8,128)(2,1)S(1)}, u32[]{:S(2)}, u32[]{:S(2)}) %collective-permute-start.2) | collective-permute-done | bytes 573472 | tf_op jit(solution)/shard_map/ppermute | solution.py:18
  39.0 18.7 %section.1 = (bf16[8,256,128]{2,1,0:T(8,128)(2,1)S(1)}, bf16[640,128]{1,0:T(8,128)(2,1)S(1)}) custom-call(bf16[8,256,128]{2,1,0:T(8,128)(2,1)S(1)} %bitcast.62, bf16[36,32,128]{2,1,0:T(8,128)(2,1)S(1)} %collective-permute-done.xlow, bf16[36,32,128]{2,1,0:T(8,128)(2,1)S(1)} %collective-permute-done.1.xhigh, ...), custom_call_target="tpu_custom_call" | custom-call | tf_op jit(solution)/shard_map/section/pallas_call | solution.py:189
  58.4 1.0 reshape.114
  59.4 26.1 %all_to_all.10 = bf16[128,5,128]{2,1,0:T(8,128)(2,1)S(1)} all-to-all(bf16[128,5,128]{2,1,0:T(8,128)(2,1)S(1)} %reshape.114), channel_id=1, replica_groups=mesh['gx'=16,'gy'=8] {'gx','gy'}, dimensions={0} | all-to-all | bytes 327680 | tf_op jit(solution)/shard_map/all_to_all | solution.py:211
  86.4 4.2 %all-to-all-start.1 = ((bf16[128,5,128]{2,1,0:T(8,128)(2,1)}), bf16[128,5,128]{2,1,0:T(8,128)(2,1)S(1)}, u32[]{:S(2)}, u32[]{:S(2)}) async-start(bf16[128,5,128]{2,1,0:T(8,128)(2,1)} %broadcast_in_dim.11), calls=%async_computation.1 | async-start | bytes 524288 | tf_op jit(solution)/shard_map/all_to_all | solution.py:214
  90.6 1.0 copy.80
  91.6 10.0 %all-to-all-done.1 = bf16[128,5,128]{2,1,0:T(8,128)(2,1)S(1)} async-done(((bf16[128,5,128]{2,1,0:T(8,128)(2,1)}), bf16[128,5,128]{2,1,0:T(8,128)(2,1)S(1)}, u32[]{:S(2)}, u32[]{:S(2)}) %all-to-all-start.1) | async-done | bytes 163872 | tf_op jit(solution)/shard_map/all_to_all | solution.py:214
  102.6 1.0 copy.72
  103.9 1.0 copy.73
  (75 shorter events, 13.9 us)
Async XLA Ops:
  2.7 0.9 copy-start.6
  3.6 0.9 copy-start.5
  5.5 11.7 %collective-permute-start = (bf16[36,32,128]{2,1,0:T(8,128)(2,1)}, bf16[36,32,128]{2,1,0:T(8,128)(2,1)S(1)}, u32[]{:S(2)}, u32[]{:S(2)}) collective-permute-start(bf16[36,32,128]{2,1,0:T(8,128)(2,1)} %pad_maximum_fusion.8), channel_id=1, source_target_pairs={{0,8},{8,16},{16,24},{24,32},{32,40},{40,48},{48,56},{56,64},{64,7... | collective-permute-start | bytes 884744 | tf_op jit(solution)/shard_map/ppermute | solution.py:18
  11.3 8.2 %collective-permute-start.1 = (bf16[36,32,128]{2,1,0:T(8,128)(2,1)}, bf16[36,32,128]{2,1,0:T(8,128)(2,1)S(1)}, u32[]{:S(2)}, u32[]{:S(2)}) collective-permute-start(bf16[36,32,128]{2,1,0:T(8,128)(2,1)} %pad_maximum_fusion.9), channel_id=1, source_target_pairs={{8,0},{16,8},{24,16},{32,24},{40,32},{48,40},{56,48},{64,56},{72,6... | collective-permute-start | bytes 884744 | tf_op jit(solution)/shard_map/ppermute | solution.py:18
  13.2 0.9 copy-start.4
  14.2 0.9 copy-start.2
  21.9 14.2 %collective-permute-start.3 = (bf16[70,32,128]{2,1,0:T(8,128)(2,1)}, bf16[70,32,128]{2,1,0:T(8,128)(2,1)S(1)}, u32[]{:S(2)}, u32[]{:S(2)}) collective-permute-start(bf16[70,32,128]{2,1,0:T(8,128)(2,1)} %pad_maximum_fusion.5), channel_id=1, source_target_pairs={{1,0},{2,1},{3,2},{4,3},{5,4},{6,5},{7,6},{9,8},{10,9},{11,10},{12... | collective-permute-start | bytes 1720328 | tf_op jit(solution)/shard_map/ppermute | solution.py:18
  23.5 4.9 %copy-start.1 = (bf16[1,3,32,3,4,32]{2,5,1,4,3,0:T(8,128)(2,1)S(1)}, bf16[1,3,32,3,4,32]{2,5,1,4,3,0:T(8,128)(2,1)}, u32[]{:S(2)}) copy-start(bf16[1,3,32,3,4,32]{2,5,1,4,3,0:T(8,128)(2,1)} %get-tuple-element.32) | copy-start | bytes 221188
  24.4 13.3 %collective-permute-start.2 = (bf16[70,32,128]{2,1,0:T(8,128)(2,1)}, bf16[70,32,128]{2,1,0:T(8,128)(2,1)S(1)}, u32[]{:S(2)}, u32[]{:S(2)}) collective-permute-start(bf16[70,32,128]{2,1,0:T(8,128)(2,1)} %pad_maximum_fusion.4), channel_id=1, source_target_pairs={{0,1},{1,2},{2,3},{3,4},{4,5},{5,6},{6,7},{8,9},{9,10},{10,11},{11... | collective-permute-start | bytes 1720328 | tf_op jit(solution)/shard_map/ppermute | solution.py:18
  29.7 1.6 %copy-start.3 = (bf16[32,3,3,3,32]{4,0,3,2,1:T(8,128)(2,1)S(1)}, bf16[32,3,3,3,32]{4,0,3,2,1:T(8,128)(2,1)}, u32[]{:S(2)}) copy-start(bf16[32,3,3,3,32]{4,0,3,2,1:T(8,128)(2,1)} %param.10) | copy-start | bytes 165892
  37.7 0.7 copy-start.7
  38.3 0.7 copy-start.8
  57.7 0.7 copy-start
  86.4 15.3 %all-to-all-start.1 = ((bf16[128,5,128]{2,1,0:T(8,128)(2,1)}), bf16[128,5,128]{2,1,0:T(8,128)(2,1)S(1)}, u32[]{:S(2)}, u32[]{:S(2)}) async-start(bf16[128,5,128]{2,1,0:T(8,128)(2,1)} %broadcast_in_dim.11), calls=%async_computation.1 | async-start | bytes 524288 | tf_op jit(solution)/shard_map/all_to_all | solution.py:214

commit v3 on v2

v3 whole, which is shorter than its diff:
```python
import math

import jax
import jax.numpy as jnp
from jax import lax
from jax.experimental import pallas as pl
from jax.experimental.pallas import tpu as pltpu
from jax.sharding import PartitionSpec as P

BF = jnp.bfloat16
F32 = jnp.float32
C, Z, N, H = 32, 128, 8, 4
W = N + 2 * H
Q = N // 2
ROWS = 8


def call(kernel, outs, scratch=(), name=None):
    return pl.pallas_call(
        kernel,
        out_shape=tuple(jax.ShapeDtypeStruct(s, d) for s, d in outs),
        scratch_shapes=[pltpu.VMEM(s, d) for s, d in scratch],
        compiler_params=pltpu.CompilerParams(vmem_limit_bytes=40 << 20),
        name=name,
    )


def shift(v, axis, step):
    devices = lax.axis_size(axis)
    pairs = [(i, i + step) for i in range(devices) if 0 <= i + step < devices]
    return lax.ppermute(v, axis, pairs)


def cell(y, n=1):
    return slice(y * C, (y + n) * C)


def prepare(w1, w2, b1, b2, t1, t2, f2, f1, c1, c2):
    zero = jnp.zeros((C, C), F32)
    for src, plain, flip in ((w1, t1, f1), (w2, t2, f2)):
        for a in range(3):
            for c in range(3):
                rows = slice(c * C, (c + 1) * C)
                high = slice((3 + c) * C, (4 + c) * C)
                cols = slice(a * 4 * C, (a + 1) * 4 * C)
                line = jnp.concatenate(
                    [src[a * 9 + b * 3 + c].astype(F32) for b in range(3)] + [zero], axis=1)
                plain[rows, cols] = line.astype(BF)
                plain[high, cols] = pltpu.roll(line, C, 1).astype(BF)
                tall = jnp.concatenate(
                    [src[(2 - a) * 9 + (2 - b) * 3 + 2 - c].astype(F32) for b in range(3)] + [zero],
                    axis=0)
                line = jnp.transpose(tall)
                flip[rows, cols] = line.astype(BF)
                flip[high, cols] = pltpu.roll(line, C, 1).astype(BF)
    for src, dst in ((b1, c1), (b2, c2)):
        dst[...] = jnp.transpose(jnp.broadcast_to(src[...], (Z, C)))


def pack_y(own, pown, mlow, mhigh):
    for x in range(N):
        for k in range(H):
            mlow[x * H + k] = own[x, cell(N - H + k), :]
            mhigh[x * H + k] = own[x, cell(k), :]
    for x in range(Q):
        mlow[N * H + x] = pown[x, cell(Q - 1), :]
        mhigh[N * H + x] = pown[x, cell(0), :]


def pack_x(own, pown, ylow, yhigh, feat, pool, mlow, mhigh):
    for x in range(N):
        feat[x, cell(H, N), :] = own[x]
        for k in range(H):
            feat[x, cell(k), :] = ylow[x * H + k]
            feat[x, cell(H + N + k), :] = yhigh[x * H + k]
    for x in range(Q):
        pool[x, cell(1, Q), :] = pown[x]
        pool[x, cell(0), :] = ylow[N * H + x]
        pool[x, cell(Q + 1), :] = yhigh[N * H + x]
    for k in range(H):
        for y in range(W):
            mlow[k * W + y] = feat[N - H + k, cell(y), :]
            mhigh[k * W + y] = feat[k, cell(y), :]
    for y in range(Q + 2):
        mlow[H * W + y] = pool[Q - 1, cell(y), :]
        mhigh[H * W + y] = pool[0, cell(y), :]


def after(v):
    lane = lax.broadcasted_iota(jnp.int32, v.shape, 1)
    return jnp.where(lane == 0, 0.0, pltpu.roll(v, 1, 1))


def before(v):
    lane = lax.broadcasted_iota(jnp.int32, v.shape, 1)
    return jnp.where(lane == Z - 1, 0.0, pltpu.roll(v, Z - 1, 1))


def spreader():
    row = lax.broadcasted_iota(jnp.int32, (Z, 2 * Z), 0)
    col = lax.broadcasted_iota(jnp.int32, (Z, 2 * Z), 1)
    return jnp.where(row == col // 2, 1.0, 0.0).astype(BF)


def conv_pair(src, x, weight, width, write, i):
    for j in range(width // 2):
        rows = [src[x + d, cell(2 * j, 4), :] for d in range(4)]
        tile = jnp.concatenate(
            [jnp.concatenate([rows[d], rows[d + 1]], axis=1) for d in range(3)], axis=0)
        got = jnp.dot(weight[...], tile, preferred_element_type=F32)
        for xo in range(2):
            for yo in range(2):
                g = got[yo * 3 * C:(yo + 1) * 3 * C, xo * Z:(xo + 1) * Z]
                v = g[C:2 * C] + after(g[0:C]) + before(g[2 * C:])
                write(i, j, xo, yo, v)


def writers(mask, b1, b2, ups, hid, two, one, at):
    lane = lax.broadcasted_iota(jnp.int32, (C, Z), 1)
    odd = (lane % 2).astype(F32)

    def mask_of(i, j, xo, yo, reach):
        bx = (2 * i + xo + N - reach) >> 3
        by = (2 * j + yo + N - reach) >> 3
        return mask[bx][by:by + 1, :]

    def write_hidden(i, j, xo, yo, v):
        m = mask_of(i, j, xo, yo, H - 1)
        hid[2 * i + xo - at[0], cell(2 * j + yo), :] = (
            jnp.maximum(v + b1[...], 0.0) * m).astype(BF)

    def write_two(i, j, xo, yo, v):
        m = mask_of(i, j, xo, yo, H - 2)
        grad = ups[i - at[3], cell(j), 0:Z]
        pick = ups[i - at[3], cell(j), Z:2 * Z]
        live = (pick == odd + float(4 * xo + 2 * yo)) & (v + b2[...] > 0.0)
        two[2 * i + xo - at[1], cell(2 * j + yo), :] = jnp.where(live, grad * m, 0.0).astype(BF)

    def write_one(i, j, xo, yo, v):
        h = hid[2 * i + xo + 2 - at[0], cell(2 * j + yo + 2), :].astype(F32)
        one[2 * i + xo - at[2], cell(2 * j + yo), :] = jnp.where(h > 0.0, v, 0.0).astype(BF)

    return write_hidden, write_two, write_one


def middle(feat, pool, mask, t1, t2, f2, b1, b2, hid, two, one, ups):
    spread = spreader()
    for p in range(2):
        ups[p] = jnp.dot(pool[1 + p], spread, preferred_element_type=F32)
    write_hidden, write_two, write_one = writers(mask, b1, b2, ups, hid, two, one, (4, 4, 4, 2))

    def trip(t, carry):
        conv_pair(feat, 2 * t, t1, W - 2, write_hidden, t + 2)
        return carry
    lax.fori_loop(0, 3, trip, 0)
    for i in (2, 3):
        conv_pair(hid, 2 * i - 4, t2, W - 4, write_two, i)
    conv_pair(two, 0, f2, W - 6, write_one, 2)


def outer(mfeat, mpool, xlow, xhigh, mhid, mtwo, mone, mask, t1, t2, f2, b1, b2,
          one, parts, feat, hid, two, ups, acc1, acc2):
    for x in range(N):
        feat[H + x] = mfeat[x]
    for k in range(H):
        for y in range(W):
            feat[k, cell(y), :] = xlow[k * W + y]
            feat[H + N + k, cell(y), :] = xhigh[k * W + y]
    for x in range(6):
        hid[4 + x] = mhid[x]
    for x in range(4):
        two[4 + x] = mtwo[x]
    for x in range(2):
        one[4 + x] = mone[x]
    spread = spreader()
    for y in range(Q + 2):
        ups[0, cell(y), :] = jnp.dot(xlow[H * W + y], spread, preferred_element_type=F32)
        ups[Q + 1, cell(y), :] = jnp.dot(xhigh[H * W + y], spread, preferred_element_type=F32)
    ups[1] = jnp.dot(mpool[0], spread, preferred_element_type=F32)
    ups[Q] = jnp.dot(mpool[Q - 1], spread, preferred_element_type=F32)
    write_hidden, write_two, write_one = writers(mask, b1, b2, ups, hid, two, one, (0, 0, 0, 0))

    def rim(src, weight, width, write):
        half = width // 2

        def trip(t, carry):
            for k in range(2):
                i = t * (half - 2) + k
                conv_pair(src, 2 * i, weight, width, write, i)
            return carry
        lax.fori_loop(0, 2, trip, 0)

    rim(feat, t1, W - 2, write_hidden)
    rim(hid, t2, W - 4, write_two)
    rim(two, f2, W - 6, write_one)

    def term(x, bias, src, off_s, delta, off_d, acc):
        rights = []
        for y in range(N):
            d = delta[x + off_d, cell(y + off_d), :].astype(F32)
            bias = bias + d
            rights.append(jnp.concatenate([before(d), d, after(d)], axis=0).astype(BF))
        left = jnp.concatenate(
            [jnp.concatenate([src[x + off_s + a, cell(y + off_s, 3), :] for y in range(N)], axis=1)
             for a in range(3)], axis=0)
        acc[...] += lax.dot_general(left, jnp.concatenate(rights, axis=1), (((1,), (1,)), ((), ())),
                                    preferred_element_type=F32)
        return bias

    def trip(x, sums):
        s2 = term(x, sums[1], hid, H - 2, two, H - 2, acc2)
        s1 = term(x, sums[0], feat, H - 1, one, H - 3, acc1)
        return s1, s2

    acc1[...] = jnp.zeros_like(acc1)
    acc2[...] = jnp.zeros_like(acc2)
    none = jnp.zeros((C, Z), F32)
    sums = lax.fori_loop(0, N, trip, (none, none))
    rows9 = 9 * C
    pad = jnp.zeros((rows9, Z - 3 * C), F32)
    for k, acc in enumerate((acc1, acc2)):
        parts[k * rows9:(k + 1) * rows9, :] = jnp.concatenate([acc[...], pad], axis=1).astype(BF)
        total = jnp.sum(sums[k], axis=1, keepdims=True)
        parts[2 * rows9 + k * C:2 * rows9 + (k + 1) * C, :] = jnp.broadcast_to(
            total, (C, Z)).astype(BF)
    rest = parts.shape[0] - 20 * C
    parts[20 * C:, :] = jnp.zeros((rest, Z), BF)


def final(one, mask, f1, out):
    def write_out(i, j, xo, yo, v):
        out[2 * i + xo, cell(2 * j + yo), :] = (v * mask[1][1:2, :]).astype(BF)

    def trip(t, carry):
        for k in range(2):
            conv_pair(one, 4 * t + 2 * k, f1, N, write_out, 2 * t + k)
        return carry
    lax.fori_loop(0, N // 4, trip, 0)


def body(features, occupancy, weight_one, bias_one, weight_two, bias_two, grad_pooled, pool_choice):
    axes = ("gx", "gy")
    devices = lax.axis_size("gx") * lax.axis_size("gy")
    flags = jnp.pad(occupancy, ((1, 1), (1, 1), (0, 0)))
    window = lax.dynamic_slice(
        flags, (lax.axis_index("gx"), lax.axis_index("gy"), jnp.int32(0)), (3, 3, occupancy.shape[2]))
    mask = jnp.repeat(window, 8, axis=2).astype(F32)
    own = (features * mask[1, 1].astype(BF)).transpose(1, 2, 0, 3).reshape(N, N * C, Z)
    mask = jnp.pad(mask, ((0, 0), (0, 5), (0, 0)))
    pown = jnp.concatenate([grad_pooled, pool_choice.astype(BF)], axis=3)
    pown = pown.transpose(1, 2, 0, 3).reshape(Q, Q * C, Z)

    ymsg = N * H + Q
    mlow, mhigh = call(pack_y, [((ymsg, C, Z), BF)] * 2, name="pack_y")(own, pown)
    ylow = shift(mlow, "gy", 1)
    yhigh = shift(mhigh, "gy", -1)

    def blocks(weight):
        return weight.transpose(1, 2, 3, 0, 4).reshape(27, C, C)

    t1, t2, f2, f1, b1, b2 = call(
        prepare, [((6 * C, 12 * C), BF)] * 4 + [((C, Z), F32)] * 2, name="prepare")(
            blocks(weight_one), blocks(weight_two), bias_one.reshape(1, C), bias_two.reshape(1, C))

    own, pown, t1 = lax.optimization_barrier((own, pown, t1))
    xmsg = W * H + Q + 2
    mfeat, mpool, mlow, mhigh = call(
        pack_x, [((N, W * C, Z), BF), ((Q, (Q + 2) * C, Z), BF)] + [((xmsg, C, Z), BF)] * 2,
        name="pack_x")(own, pown, ylow, yhigh)
    xlow = shift(mlow, "gx", 1)
    xhigh = shift(mhigh, "gx", -1)

    mhid, mtwo, mone = call(
        middle,
        [((6, (W - 2) * C, Z), BF), ((4, (W - 4) * C, Z), BF), ((2, (W - 6) * C, Z), BF)],
        [((2, (Q + 2) * C, 2 * Z), F32)], name="middle")(mfeat, mpool, mask, t1, t2, f2, b1, b2)

    one, parts = call(
        outer, [((W - 6, (W - 6) * C, Z), BF), ((devices * ROWS, Z), BF)],
        [((W, W * C, Z), BF), ((W - 2, (W - 2) * C, Z), BF), ((W - 4, (W - 4) * C, Z), BF),
         ((Q + 2, (Q + 2) * C, 2 * Z), F32), ((9 * C, 3 * C), F32), ((9 * C, 3 * C), F32)],
        name="outer")(mfeat, mpool, xlow, xhigh, mhid, mtwo, mone, mask, t1, t2, f2, b1, b2)

    got = lax.all_to_all(parts.reshape(devices, ROWS, Z), axes, 0, 0, tiled=True)
    out, = call(final, [((N, N * C, Z), BF)], name="final")(one, mask, f1)
    mine = jnp.sum(got.astype(F32), axis=0).astype(BF)
    spread = jnp.broadcast_to(mine[None], (devices, ROWS, Z))
    summed = lax.all_to_all(spread, axes, 0, 0, tiled=True).reshape(devices * ROWS, Z).astype(F32)
    cells = N * lax.axis_size("gx") * N * lax.axis_size("gy") * Z
    summed = summed * (1.0 / math.sqrt(cells))

    def unpack(block):
        return block[:, :3 * C].reshape(3, 3, C, 3, C).transpose(4, 0, 1, 3, 2)

    grad_input = out.reshape(N, N, C, Z).transpose(2, 0, 1, 3)
    return (grad_input, unpack(summed[:9 * C]), summed[18 * C:19 * C, 0],
            unpack(summed[9 * C:18 * C]), summed[19 * C:20 * C, 0])


def solution(mesh):
    cells = P(None, "gx", "gy", None)
    return jax.shard_map(
        body,
        mesh=mesh,
        in_specs=(cells, P(), P(), P(), P(), P(), cells, cells),
        out_specs=(cells, P(), P(), P(), P()),
        check_vma=False,
    )
```

time: 105 us -> 86.4 us (0.82)
  local copies, waits for them, and re-layouts: 22.1 us -> 6.02 us
  waiting for transfers between devices: 13.7 us -> 20.7 us
  other arithmetic: 6.73 us -> 2.19 us
  blocking collectives: 26.1 us -> 23.2 us
  Pallas kernels: 18.7 us -> 16.3 us
    ppermute x4, waiting for transfers between devices: 3.72 us -> 12 us  [shift(): return lax.ppermute(v, axis, pairs)]
    another operation x10 -> x0, local copies, waits for them, and re-layouts: 5.17 us -> none  [the longest x8 5.14 us: toeplitz(): return jnp.stack([lower, upper], axis=0).reshape(6 * chan, 12 * chan)]
    unnamed x25 -> x14, local copies, waits for them, and re-layouts: 7.41 us -> 2.57 us
    reshape x9 -> x1, local copies, waits for them, and re-layouts: 5.72 us -> 1 us  [body(): grad_input = out.reshape(N, N, C, Z).transpose(2, 0, 1, 3)]
    concatenate x6 -> x0, other arithmetic: 4.09 us -> none  [the longest x4 3.24 us: msg(): jnp.concatenate([cells.reshape(-1, C, Z), pooled.reshape(-1, C, Z)], axis=0)]
    all_to_all x1, blocking collectives: 26.1 us -> 23.2 us  [body(): lax.all_to_all(parts.reshape(devices, ROWS, Z), axes, 0, 0, tiled=True)]
    pallas_call x1 -> x6, Pallas kernels: 18.7 us -> 16.3 us  [the longest x1 10.2 us: body(): call(outer, [((W - 6, (W - 6) * C, Z), BF), ((devices * ROWS, Z), BF)], [...]
    all_to_all x1, waiting for transfers between devices: 10 us -> 8.68 us  [body(): lax.all_to_all(spread, axes, 0, 0, tiled=True).reshape(devices * ROWS, Z)]
  transfers between devices with their start and end apart: 5 -> 5, of which waited for: 3 -> 5; matrix products, arithmetic and copies ran while one was open for 13% -> 1% of each run, Pallas kernels for 0% -> 7%
where the time goes in v3:
time: 86.4 us; the launch traced here: 86.1 us
  blocking collectives  23.2 us (27%)
  waiting for transfers between devices  20.7 us (24%)
  starting transfers between devices  16.8 us (19%)
  Pallas kernels  16.3 us (19%)
  local copies, waits for them, and re-layouts  6.02 us (7%)
  other arithmetic  2.19 us (3%)
  between operations  0.87 us (1%)
    all_to_all x1, blocking collectives, body(): lax.all_to_all(parts.reshape(devices, ROWS, Z), axes, 0, 0, tiled=True)  23.2 us
    ppermute x4, starting transfers between devices, shift(): return lax.ppermute(v, axis, pairs)  12.5 us
    ppermute x4, waiting for transfers between devices, shift(): return lax.ppermute(v, axis, pairs)  12 us
    pallas_call x1, Pallas kernels, body(): call(outer, [((W - 6, (W - 6) * C, Z), BF), ((devices * ROWS, Z), BF)], [...  10.2 us
    all_to_all x1, waiting for transfers between devices, body(): lax.all_to_all(spread, axes, 0, 0, tiled=True).reshape(devices * ROWS, Z)  8.68 us
    all_to_all x1, starting transfers between devices, body(): lax.all_to_all(spread, axes, 0, 0, tiled=True).reshape(devices * ROWS, Z)  4.25 us
    pallas_call x1, Pallas kernels, body(): call(middle, [((6, (W - 2) * C, Z), BF), ((4, (W - 4) * C, Z), BF), ((2,...  3.34 us
    unnamed x14, local copies, waits for them, and re-layouts  2.57 us
  transfers between devices with their start and end apart: 5, of which 5 were waited for; matrix products, arithmetic and copies ran while one was open for 1% of the time, Pallas kernels for 7%

profile of v3, /device:TPU:1, one launch (start us, length us, event | category | flops | bytes accessed | tf_op | source)
XLA Modules:
  0.0 86.1 jit_solution(5307952503853916122)
XLA Ops:
  0.6 0.7 fusion
  1.6 1.1 %convert_element_type.29 = bf16[32,4,4,64]{3,2,1,0:T(4,128)(2,1)S(1)} convert(s32[32,4,4,64]{3,2,1,0:T(4,128)} %param.15) | non-fusion elementwise | flops 32768 | bytes 196608 | tf_op jit(solution)/shard_map/convert_element_type | solution.py:250
  3.0 0.3 copy.21
  3.4 4.1 %collective-permute-start = (bf16[36,32,128]{2,1,0:T(8,128)(2,1)S(1)}, bf16[36,32,128]{2,1,0:T(8,128)(2,1)S(1)}, u32[]{:S(2)}, u32[]{:S(2)}) collective-permute-start(bf16[36,32,128]{2,1,0:T(8,128)(2,1)S(1)} %get-tuple-element.28), channel_id=1, source_target_pairs={{0,1},{1,2},{2,3},{3,4},{4,5},{5,6},{6,7},{8,9},{9,10},{10,11},{11... | collective-permute-start | bytes 884744 | tf_op jit(solution)/shard_map/ppermute | solution.py:31
  7.5 1.3 %collective-permute-start.1 = (bf16[36,32,128]{2,1,0:T(8,128)(2,1)S(1)}, bf16[36,32,128]{2,1,0:T(8,128)(2,1)S(1)}, u32[]{:S(2)}, u32[]{:S(2)}) collective-permute-start(bf16[36,32,128]{2,1,0:T(8,128)(2,1)S(1)} %get-tuple-element.29), channel_id=1, source_target_pairs={{1,0},{2,1},{3,2},{4,3},{5,4},{6,5},{7,6},{9,8},{10,9},{11,10},{12... | collective-permute-start | bytes 884744 | tf_op jit(solution)/shard_map/ppermute | solution.py:31
  8.8 0.6 copy-done.2
  9.4 1.3 %prepare.1 = (bf16[192,384]{1,0:T(8,128)(2,1)S(1)}, bf16[192,384]{1,0:T(8,128)(2,1)S(1)}, bf16[192,384]{1,0:T(8,128)(2,1)S(1)}, bf16[192,384]{1,0:T(8,128)(2,1)S...) custom-call(bf16[27,32,32]{2,1,0:T(8,128)(2,1)S(1)} %bitcast.33, bf16[27,32,32]{2,1,0:T(8,128)(2,1)S(1)} %bitcast.34, ...), custom_call_target="tpu_custom_call" | custom-call | tf_op jit(solution)/shard_map/prepare/pallas_call | solution.py:261
  10.7 2.4 %collective-permute-done.ylow = bf16[36,32,128]{2,1,0:T(8,128)(2,1)S(1)} collective-permute-done((bf16[36,32,128]{2,1,0:T(8,128)(2,1)S(1)}, bf16[36,32,128]{2,1,0:T(8,128)(2,1)S(1)}, u32[]{:S(2)}, u32[]{:S(2)}) %collective-permute-start) | collective-permute-done | bytes 294944 | tf_op jit(solution)/shard_map/ppermute | solution.py:31
  13.1 3.8 %collective-permute-done.1.yhigh = bf16[36,32,128]{2,1,0:T(8,128)(2,1)S(1)} collective-permute-done((bf16[36,32,128]{2,1,0:T(8,128)(2,1)S(1)}, bf16[36,32,128]{2,1,0:T(8,128)(2,1)S(1)}, u32[]{:S(2)}, u32[]{:S(2)}) %collective-permute-start.1) | collective-permute-done | bytes 294944 | tf_op jit(solution)/shard_map/ppermute | solution.py:31
  17.1 5.2 %collective-permute-start.2 = (bf16[70,32,128]{2,1,0:T(8,128)(2,1)S(1)}, bf16[70,32,128]{2,1,0:T(8,128)(2,1)S(1)}, u32[]{:S(2)}, u32[]{:S(2)}) collective-permute-start(bf16[70,32,128]{2,1,0:T(8,128)(2,1)S(1)} %get-tuple-element.32), channel_id=1, source_target_pairs={{0,8},{8,16},{16,24},{24,32},{32,40},{40,48},{48,56},{56,64},{64,7... | collective-permute-start | bytes 1720328 | tf_op jit(solution)/shard_map/ppermute | solution.py:31
  22.4 1.9 %collective-permute-start.3 = (bf16[70,32,128]{2,1,0:T(8,128)(2,1)S(1)}, bf16[70,32,128]{2,1,0:T(8,128)(2,1)S(1)}, u32[]{:S(2)}, u32[]{:S(2)}) collective-permute-start(bf16[70,32,128]{2,1,0:T(8,128)(2,1)S(1)} %get-tuple-element.33), channel_id=1, source_target_pairs={{8,0},{16,8},{24,16},{32,24},{40,32},{48,40},{56,48},{64,56},{72,6... | collective-permute-start | bytes 1720328 | tf_op jit(solution)/shard_map/ppermute | solution.py:31
  24.3 3.3 %middle.1 = (bf16[6,448,128]{2,1,0:T(8,128)(2,1)S(1)}, bf16[4,384,128]{2,1,0:T(8,128)(2,1)S(1)}, bf16[2,320,128]{2,1,0:T(8,128)(2,1)S(1)}) custom-call(bf16[8,512,128]{2,1,0:T(8,128)(2,1)S(1)} %get-tuple-element.30.feat.mfeat, bf16[4,192,128]{2,1,0:T(8,128)(2,1)S(1)} %get-tuple-element.31.pool.mpool, f32[3,8,128]{2,1,0:T(8,128)S(1)} %pad.9.mask, ...), custom_call_target="tpu_custom_call" | custom-call | tf_op jit(solution)/shard_map/middle/pallas_call | solution.py:273
  27.7 1.3 %collective-permute-done.2.xlow = bf16[70,32,128]{2,1,0:T(8,128)(2,1)S(1)} collective-permute-done((bf16[70,32,128]{2,1,0:T(8,128)(2,1)S(1)}, bf16[70,32,128]{2,1,0:T(8,128)(2,1)S(1)}, u32[]{:S(2)}, u32[]{:S(2)}) %collective-permute-start.2) | collective-permute-done | bytes 573472 | tf_op jit(solution)/shard_map/ppermute | solution.py:31
  29.0 4.4 %collective-permute-done.3.xhigh = bf16[70,32,128]{2,1,0:T(8,128)(2,1)S(1)} collective-permute-done((bf16[70,32,128]{2,1,0:T(8,128)(2,1)S(1)}, bf16[70,32,128]{2,1,0:T(8,128)(2,1)S(1)}, u32[]{:S(2)}, u32[]{:S(2)}) %collective-permute-start.3) | collective-permute-done | bytes 573472 | tf_op jit(solution)/shard_map/ppermute | solution.py:31
  33.4 10.2 %outer.1 = (bf16[10,320,128]{2,1,0:T(8,128)(2,1)S(1)}, bf16[1024,128]{1,0:T(8,128)(2,1)S(1)}) custom-call(bf16[8,512,128]{2,1,0:T(8,128)(2,1)S(1)} %get-tuple-element.30.feat.mfeat, bf16[4,192,128]{2,1,0:T(8,128)(2,1)S(1)} %get-tuple-element.31.pool.mpool, bf16[70,32,128]{2,1,0:T(8,128)(2,1)S(1)} %collective-permute-done.2.xlow, ...), custom_call_target="tpu_custom_call" | custom-call | tf_op jit(solution)/shard_map/outer/pallas_call | solution.py:278
  43.6 23.2 %all_to_all.10 = bf16[128,8,128]{2,1,0:T(8,128)(2,1)S(1)} all-to-all(bf16[128,8,128]{2,1,0:T(8,128)(2,1)S(1)} %bitcast.32), channel_id=1, replica_groups=mesh['gx'=16,'gy'=8] {'gx','gy'}, dimensions={0} | all-to-all | bytes 524288 | tf_op jit(solution)/shard_map/all_to_all | solution.py:284
  67.0 0.7 broadcast_in_dim.5
  67.7 4.2 %all-to-all-start.1 = ((bf16[128,8,128]{2,1,0:T(8,128)(2,1)}), bf16[128,8,128]{2,1,0:T(8,128)(2,1)S(1)}, u32[]{:S(2)}, u32[]{:S(2)}) async-start(bf16[128,8,128]{2,1,0:T(8,128)(2,1)} %broadcast_in_dim.5), calls=%async_computation.1 | async-start | bytes 524288 | tf_op jit(solution)/shard_map/all_to_all | solution.py:288
  72.0 1.3 %final.1 = bf16[8,256,128]{2,1,0:T(8,128)(2,1)S(1)} custom-call(bf16[10,320,128]{2,1,0:T(8,128)(2,1)S(1)} %get-tuple-element.42.one, f32[3,8,128]{2,1,0:T(8,128)S(1)} %pad.9.mask, bf16[192,384]{1,0:T(8,128)(2,1)S(1)} %get-tuple-element.43.f1), custom_call_target="tpu_custom_call" | custom-call | tf_op jit(solution)/shard_map/final/pallas_call | solution.py:285
  73.3 1.0 %copy.27 = bf16[8,8,32,128]{3,1,0,2:T(8,128)(2,1)} copy(bf16[8,8,32,128]{3,2,1,0:T(8,128)(2,1)S(1)} %bitcast.29) | data formatting | bytes 1048576 | tf_op jit(solution)/shard_map/reshape | solution.py:295
  74.3 8.7 %all-to-all-done.1 = bf16[128,8,128]{2,1,0:T(8,128)(2,1)S(1)} async-done(((bf16[128,8,128]{2,1,0:T(8,128)(2,1)}), bf16[128,8,128]{2,1,0:T(8,128)(2,1)S(1)}, u32[]{:S(2)}, u32[]{:S(2)}) %all-to-all-start.1) | async-done | bytes 262176 | tf_op jit(solution)/shard_map/all_to_all | solution.py:288
  83.0 0.6 slice_reduce_fusion
  83.9 1.0 %copy.25 = f32[32,3,3,3,32]{4,0,3,2,1:T(8,128)} copy(f32[32,3,3,3,32]{0,3,4,2,1:T(4,128)S(1)} %bitcast.37) | data formatting | bytes 221184
  85.1 1.0 %copy.24 = f32[32,3,3,3,32]{4,0,3,2,1:T(8,128)} copy(f32[32,3,3,3,32]{0,3,4,2,1:T(4,128)S(1)} %bitcast.38) | data formatting | bytes 221184
  (25 shorter events, 1.4 us)
Async XLA Ops:
  1.4 1.2 %copy-start.5 = (bf16[32,4,4,64]{3,2,1,0:T(4,128)(2,1)S(1)}, bf16[32,4,4,64]{3,2,1,0:T(4,128)(2,1)}, u32[]{:S(2)}) copy-start(bf16[32,4,4,64]{3,2,1,0:T(4,128)(2,1)} %param.14) | copy-start | bytes 196612
  1.6 1.3 %copy-start.4 = (bf16[32,8,8,128]{3,2,1,0:T(8,128)(2,1)S(1)}, bf16[32,8,8,128]{3,2,1,0:T(8,128)(2,1)}, u32[]{:S(2)}) copy-start(bf16[32,8,8,128]{3,2,1,0:T(8,128)(2,1)} %param.8) | copy-start | bytes 1572868
  3.3 5.5 %copy-start = (bf16[32,3,3,3,32]{4,0,3,2,1:T(8,128)(2,1)S(1)}, bf16[32,3,3,3,32]{4,0,3,2,1:T(8,128)(2,1)}, u32[]{:S(2)}) copy-start(bf16[32,3,3,3,32]{4,0,3,2,1:T(8,128)(2,1)} %param.10) | copy-start | bytes 165892
  3.3 5.5 %copy-start.1 = (bf16[32,3,3,3,32]{4,0,3,2,1:T(8,128)(2,1)S(1)}, bf16[32,3,3,3,32]{4,0,3,2,1:T(8,128)(2,1)}, u32[]{:S(2)}) copy-start(bf16[32,3,3,3,32]{4,0,3,2,1:T(8,128)(2,1)} %param.12) | copy-start | bytes 165892
  3.4 9.8 %collective-permute-start = (bf16[36,32,128]{2,1,0:T(8,128)(2,1)S(1)}, bf16[36,32,128]{2,1,0:T(8,128)(2,1)S(1)}, u32[]{:S(2)}, u32[]{:S(2)}) collective-permute-start(bf16[36,32,128]{2,1,0:T(8,128)(2,1)S(1)} %get-tuple-element.28), channel_id=1, source_target_pairs={{0,1},{1,2},{2,3},{3,4},{4,5},{5,6},{6,7},{8,9},{9,10},{10,11},{11... | collective-permute-start | bytes 884744 | tf_op jit(solution)/shard_map/ppermute | solution.py:31
  7.5 9.5 %collective-permute-start.1 = (bf16[36,32,128]{2,1,0:T(8,128)(2,1)S(1)}, bf16[36,32,128]{2,1,0:T(8,128)(2,1)S(1)}, u32[]{:S(2)}, u32[]{:S(2)}) collective-permute-start(bf16[36,32,128]{2,1,0:T(8,128)(2,1)S(1)} %get-tuple-element.29), channel_id=1, source_target_pairs={{1,0},{2,1},{3,2},{4,3},{5,4},{6,5},{7,6},{9,8},{10,9},{11,10},{12... | collective-permute-start | bytes 884744 | tf_op jit(solution)/shard_map/ppermute | solution.py:31
  8.8 0.7 copy-start.2
  8.8 0.7 copy-start.3
  17.1 11.9 %collective-permute-start.2 = (bf16[70,32,128]{2,1,0:T(8,128)(2,1)S(1)}, bf16[70,32,128]{2,1,0:T(8,128)(2,1)S(1)}, u32[]{:S(2)}, u32[]{:S(2)}) collective-permute-start(bf16[70,32,128]{2,1,0:T(8,128)(2,1)S(1)} %get-tuple-element.32), channel_id=1, source_target_pairs={{0,8},{8,16},{16,24},{24,32},{32,40},{40,48},{48,56},{56,64},{64,7... | collective-permute-start | bytes 1720328 | tf_op jit(solution)/shard_map/ppermute | solution.py:31
  22.4 11.0 %collective-permute-start.3 = (bf16[70,32,128]{2,1,0:T(8,128)(2,1)S(1)}, bf16[70,32,128]{2,1,0:T(8,128)(2,1)S(1)}, u32[]{:S(2)}, u32[]{:S(2)}) collective-permute-start(bf16[70,32,128]{2,1,0:T(8,128)(2,1)S(1)} %get-tuple-element.33), channel_id=1, source_target_pairs={{8,0},{16,8},{24,16},{32,24},{40,32},{48,40},{56,48},{64,56},{72,6... | collective-permute-start | bytes 1720328 | tf_op jit(solution)/shard_map/ppermute | solution.py:31
  67.7 15.3 %all-to-all-start.1 = ((bf16[128,8,128]{2,1,0:T(8,128)(2,1)}), bf16[128,8,128]{2,1,0:T(8,128)(2,1)S(1)}, u32[]{:S(2)}, u32[]{:S(2)}) async-start(bf16[128,8,128]{2,1,0:T(8,128)(2,1)} %broadcast_in_dim.5), calls=%async_computation.1 | async-start | bytes 524288 | tf_op jit(solution)/shard_map/all_to_all | solution.py:288

commit v4 on v3

--- a/solution.py
+++ b/solution.py
@@ -13,6 +13,7 @@
 W = N + 2 * H
 Q = N // 2
 ROWS = 8
+CELLS = 128 * 64 * 128
 
 
 def call(kernel, outs, scratch=(), name=None):
@@ -102,9 +103,9 @@
     return jnp.where(row == col // 2, 1.0, 0.0).astype(BF)
 
 
-def conv_pair(src, x, weight, width, write, i):
+def conv_pair(rows_at, x, weight, width, write, i):
     for j in range(width // 2):
-        rows = [src[x + d, cell(2 * j, 4), :] for d in range(4)]
+        rows = [rows_at(x + d, 2 * j, 4) for d in range(4)]
         tile = jnp.concatenate(
             [jnp.concatenate([rows[d], rows[d + 1]], axis=1) for d in range(3)], axis=0)
         got = jnp.dot(weight[...], tile, preferred_element_type=F32)
@@ -115,7 +116,13 @@
                 write(i, j, xo, yo, v)
 
 
-def writers(mask, b1, b2, ups, hid, two, one, at):
+def planes(ref, first=0):
+    def rows_at(x, y, n=1):
+        return ref[x - first, cell(y, n), :]
+    return rows_at
+
+
+def writers(mask, b1, b2, ups_at, hid_at, hid_put, two_put, one_put):
     lane = lax.broadcasted_iota(jnp.int32, (C, Z), 1)
     odd = (lane % 2).astype(F32)
 
@@ -126,116 +133,147 @@
 
     def write_hidden(i, j, xo, yo, v):
         m = mask_of(i, j, xo, yo, H - 1)
-        hid[2 * i + xo - at[0], cell(2 * j + yo), :] = (
-            jnp.maximum(v + b1[...], 0.0) * m).astype(BF)
+        hid_put(2 * i + xo, 2 * j + yo, (jnp.maximum(v + b1[...], 0.0) * m).astype(BF))
 
     def write_two(i, j, xo, yo, v):
         m = mask_of(i, j, xo, yo, H - 2)
-        grad = ups[i - at[3], cell(j), 0:Z]
-        pick = ups[i - at[3], cell(j), Z:2 * Z]
+        grad, pick = ups_at(i, j)
         live = (pick == odd + float(4 * xo + 2 * yo)) & (v + b2[...] > 0.0)
-        two[2 * i + xo - at[1], cell(2 * j + yo), :] = jnp.where(live, grad * m, 0.0).astype(BF)
+        two_put(2 * i + xo, 2 * j + yo, jnp.where(live, grad * m, 0.0).astype(BF))
 
     def write_one(i, j, xo, yo, v):
-        h = hid[2 * i + xo + 2 - at[0], cell(2 * j + yo + 2), :].astype(F32)
-        one[2 * i + xo - at[2], cell(2 * j + yo), :] = jnp.where(h > 0.0, v, 0.0).astype(BF)
+        h = hid_at(2 * i + xo + 2, 2 * j + yo + 2).astype(F32)
+        one_put(2 * i + xo, 2 * j + yo, jnp.where(h > 0.0, v, 0.0).astype(BF))
 
     return write_hidden, write_two, write_one
 
 
-def middle(feat, pool, mask, t1, t2, f2, b1, b2, hid, two, one, ups):
+def putter(ref, index):
+    def put(x, y, v):
+        ref[index(x), cell(y), :] = v
+    return put
+
+
+def upstream(ups, index):
+    def ups_at(i, j):
+        return ups[index(i), cell(j), 0:Z], ups[index(i), cell(j), Z:2 * Z]
+    return ups_at
+
+
+def term(x, bias, src_at, off_s, delta_at, off_d, acc):
+    rights = []
+    for y in range(N):
+        d = delta_at(x + off_d, y + off_d).astype(F32)
+        bias[...] += d
+        rights.append(jnp.concatenate([before(d), d, after(d)], axis=0).astype(BF))
+    left = jnp.concatenate(
+        [jnp.concatenate([src_at(x + off_s + a, y + off_s, 3) for y in range(N)], axis=1)
+         for a in range(3)], axis=0)
+    acc[...] += lax.dot_general(left, jnp.concatenate(rights, axis=1), (((1,), (1,)), ((), ())),
+                                preferred_element_type=F32)
+
+
+def middle(feat, pool, mask, t1, t2, f2, b1, b2, hid, two, one, acc1, acc2, s1, s2, ups):
     spread = spreader()
     for p in range(2):
         ups[p] = jnp.dot(pool[1 + p], spread, preferred_element_type=F32)
-    write_hidden, write_two, write_one = writers(mask, b1, b2, ups, hid, two, one, (4, 4, 4, 2))
-
-    def trip(t, carry):
-        conv_pair(feat, 2 * t, t1, W - 2, write_hidden, t + 2)
-        return carry
-    lax.fori_loop(0, 3, trip, 0)
+    feat_at, hid_at, two_at, one_at = planes(feat, 4), planes(hid, 4), planes(two, 4), planes(one, 4)
+    mid = lambda x: x - 4
+    write_hidden, write_two, write_one = writers(
+        mask, b1, b2, upstream(ups, lambda i: i - 2), hid_at,
+        putter(hid, mid), putter(two, mid), putter(one, mid))
+    for ref in (acc1, acc2, s1, s2):
+        ref[...] = jnp.zeros_like(ref)
+    for i in (2, 3, 4):
+        conv_pair(feat_at, 2 * i, t1, W - 2, write_hidden, i)
     for i in (2, 3):
-        conv_pair(hid, 2 * i - 4, t2, W - 4, write_two, i)
-    conv_pair(two, 0, f2, W - 6, write_one, 2)
-
-
-def outer(mfeat, mpool, xlow, xhigh, mhid, mtwo, mone, mask, t1, t2, f2, b1, b2,
-          one, parts, feat, hid, two, ups, acc1, acc2):
-    for x in range(N):
-        feat[H + x] = mfeat[x]
-    for k in range(H):
-        for y in range(W):
-            feat[k, cell(y), :] = xlow[k * W + y]
-            feat[H + N + k, cell(y), :] = xhigh[k * W + y]
-    for x in range(6):
-        hid[4 + x] = mhid[x]
-    for x in range(4):
-        two[4 + x] = mtwo[x]
-    for x in range(2):
-        one[4 + x] = mone[x]
+        conv_pair(hid_at, 2 * i, t2, W - 4, write_two, i)
+    conv_pair(two_at, 4, f2, W - 6, write_one, 2)
+    for x in range(2, 6):
+        term(x, s2, hid_at, H - 2, two_at, H - 2, acc2)
+    for x in range(3, 5):
+        term(x, s1, feat_at, H - 1, one_at, H - 3, acc1)
+
+
+def outer(mfeat, mpool, xlow, xhigh, mhid, mtwo, mone, macc1, macc2, ms1, ms2, mask,
+          t1, t2, f2, b1, b2, one, parts, hid, two, ups, acc1, acc2, s1, s2):
+    def feat_at(x, y, n=1):
+        if H <= x < H + N:
+            return mfeat[x - H, cell(y, n), :]
+        ref, k = (xlow, x) if x < H else (xhigh, x - H - N)
+        return ref[k * W + y:k * W + y + n].reshape(n * C, Z)
+
     spread = spreader()
     for y in range(Q + 2):
         ups[0, cell(y), :] = jnp.dot(xlow[H * W + y], spread, preferred_element_type=F32)
-        ups[Q + 1, cell(y), :] = jnp.dot(xhigh[H * W + y], spread, preferred_element_type=F32)
+        ups[3, cell(y), :] = jnp.dot(xhigh[H * W + y], spread, preferred_element_type=F32)
     ups[1] = jnp.dot(mpool[0], spread, preferred_element_type=F32)
-    ups[Q] = jnp.dot(mpool[Q - 1], spread, preferred_element_type=F32)
-    write_hidden, write_two, write_one = writers(mask, b1, b2, ups, hid, two, one, (0, 0, 0, 0))
-
-    def rim(src, weight, width, write):
-        half = width // 2
-
-        def trip(t, carry):
-            for k in range(2):
-                i = t * (half - 2) + k
-                conv_pair(src, 2 * i, weight, width, write, i)
-            return carry
-        lax.fori_loop(0, 2, trip, 0)
-
-    rim(feat, t1, W - 2, write_hidden)
-    rim(hid, t2, W - 4, write_two)
-    rim(two, f2, W - 6, write_one)
-
-    def term(x, bias, src, off_s, delta, off_d, acc):
-        rights = []
-        for y in range(N):
-            d = delta[x + off_d, cell(y + off_d), :].astype(F32)
-            bias = bias + d
-            rights.append(jnp.concatenate([before(d), d, after(d)], axis=0).astype(BF))
-        left = jnp.concatenate(
-            [jnp.concatenate([src[x + off_s + a, cell(y + off_s, 3), :] for y in range(N)], axis=1)
-             for a in range(3)], axis=0)
-        acc[...] += lax.dot_general(left, jnp.concatenate(rights, axis=1), (((1,), (1,)), ((), ())),
-                                    preferred_element_type=F32)
-        return bias
-
-    def trip(x, sums):
-        s2 = term(x, sums[1], hid, H - 2, two, H - 2, acc2)
-        s1 = term(x, sums[0], feat, H - 1, one, H - 3, acc1)
-        return s1, s2
-
-    acc1[...] = jnp.zeros_like(acc1)
-    acc2[...] = jnp.zeros_like(acc2)
-    none = jnp.zeros((C, Z), F32)
-    sums = lax.fori_loop(0, N, trip, (none, none))
+    ups[2] = jnp.dot(mpool[Q - 1], spread, preferred_element_type=F32)
+
+    def merged(ref, mid, count):
+        def rows_at(x, y, n=1):
+            if 4 <= x < 4 + count:
+                return mid[x - 4, cell(y, n), :]
+            return ref[x if x < 4 else x - count, cell(y, n), :]
+        return rows_at
+
+    hid_at, two_at = merged(hid, mhid, 6), merged(two, mtwo, 4)
+    one_at = planes(one)
+    for x in range(2):
+        one[4 + x] = mone[x]
+    write_hidden, write_two, write_one = writers(
+        mask, b1, b2, upstream(ups, lambda i: i if i < 2 else i - 2), hid_at,
+        putter(hid, lambda x: x if x < 4 else x - 6),
+        putter(two, lambda x: x if x < 4 else x - 4), putter(one, lambda x: x))
+    acc1[...] = macc1[...]
+    acc2[...] = macc2[...]
+    s1[...] = ms1[...]
+    s2[...] = ms2[...]
+    for i in (0, 1, 5, 6):
+        conv_pair(feat_at, 2 * i, t1, W - 2, write_hidden, i)
+    for i in (0, 1, 4, 5):
+        conv_pair(hid_at, 2 * i, t2, W - 4, write_two, i)
+    for i in (0, 1, 3, 4):
+        conv_pair(two_at, 2 * i, f2, W - 6, write_one, i)
+    for x in (0, 1, 6, 7):
+        term(x, s2, hid_at, H - 2, two_at, H - 2, acc2)
+    for x in (0, 1, 2, 5, 6, 7):
+        term(x, s1, feat_at, H - 1, one_at, H - 3, acc1)
     rows9 = 9 * C
     pad = jnp.zeros((rows9, Z - 3 * C), F32)
-    for k, acc in enumerate((acc1, acc2)):
+    for k, (acc, sums) in enumerate(((acc1, s1), (acc2, s2))):
         parts[k * rows9:(k + 1) * rows9, :] = jnp.concatenate([acc[...], pad], axis=1).astype(BF)
-        total = jnp.sum(sums[k], axis=1, keepdims=True)
+        total = jnp.sum(sums[...], axis=1, keepdims=True)
         parts[2 * rows9 + k * C:2 * rows9 + (k + 1) * C, :] = jnp.broadcast_to(
             total, (C, Z)).astype(BF)
     rest = parts.shape[0] - 20 * C
     parts[20 * C:, :] = jnp.zeros((rest, Z), BF)
 
 
+def add_up(got, out):
+    total = jnp.sum(got[...].astype(F32), axis=0, keepdims=True).astype(BF)
+    out[...] = jnp.broadcast_to(total, out.shape)
+
+
+def unpack(summed, w1, w2, b1, b2):
+    scale = 1.0 / math.sqrt(CELLS)
+    rows9 = 9 * C
+    for k, (w, b) in enumerate(((w1, b1), (w2, b2))):
+        for n in range(9):
+            rows = slice(k * rows9 + n * C, k * rows9 + (n + 1) * C)
+            block = jnp.transpose(summed[rows, :].astype(F32) * scale)
+            for c in range(3):
+                w[n * 3 + c] = block[c * C:(c + 1) * C, :]
+        rows = slice(2 * rows9 + k * C, 2 * rows9 + (k + 1) * C)
+        b[...] = jnp.transpose(summed[rows, :].astype(F32) * scale)[0:1, :]
+
+
 def final(one, mask, f1, out):
     def write_out(i, j, xo, yo, v):
         out[2 * i + xo, cell(2 * j + yo), :] = (v * mask[1][1:2, :]).astype(BF)
 
-    def trip(t, carry):
-        for k in range(2):
-            conv_pair(one, 4 * t + 2 * k, f1, N, write_out, 2 * t + k)
-        return carry
-    lax.fori_loop(0, N // 4, trip, 0)
+    for i in range(N // 2):
+        conv_pair(planes(one), 2 * i, f1, N, write_out, i)
 
 
 def body(features, occupancy, weight_one, bias_one, weight_two, bias_two, grad_pooled, pool_choice):
@@ -270,31 +308,31 @@
     xlow = shift(mlow, "gx", 1)
     xhigh = shift(mhigh, "gx", -1)
 
-    mhid, mtwo, mone = call(
+    grads = [((9 * C, 3 * C), F32)] * 2 + [((C, Z), F32)] * 2
+    mids = call(
         middle,
-        [((6, (W - 2) * C, Z), BF), ((4, (W - 4) * C, Z), BF), ((2, (W - 6) * C, Z), BF)],
+        [((6, (W - 2) * C, Z), BF), ((4, (W - 4) * C, Z), BF), ((2, (W - 6) * C, Z), BF)] + grads,
         [((2, (Q + 2) * C, 2 * Z), F32)], name="middle")(mfeat, mpool, mask, t1, t2, f2, b1, b2)
 
     one, parts = call(
         outer, [((W - 6, (W - 6) * C, Z), BF), ((devices * ROWS, Z), BF)],
-        [((W, W * C, Z), BF), ((W - 2, (W - 2) * C, Z), BF), ((W - 4, (W - 4) * C, Z), BF),
-         ((Q + 2, (Q + 2) * C, 2 * Z), F32), ((9 * C, 3 * C), F32), ((9 * C, 3 * C), F32)],
-        name="outer")(mfeat, mpool, xlow, xhigh, mhid, mtwo, mone, mask, t1, t2, f2, b1, b2)
-
-    got = lax.all_to_all(parts.reshape(devices, ROWS, Z), axes, 0, 0, tiled=True)
+        [((8, (W - 2) * C, Z), BF), ((8, (W - 4) * C, Z), BF),
+         ((4, (Q + 2) * C, 2 * Z), F32)] + grads,
+        name="outer")(mfeat, mpool, xlow, xhigh, *mids, mask, t1, t2, f2, b1, b2)
+
+    block = (devices, ROWS, Z)
+    got = lax.all_to_all(parts.reshape(block), axes, 0, 0, tiled=True)
     out, = call(final, [((N, N * C, Z), BF)], name="final")(one, mask, f1)
-    mine = jnp.sum(got.astype(F32), axis=0).astype(BF)
-    spread = jnp.broadcast_to(mine[None], (devices, ROWS, Z))
-    summed = lax.all_to_all(spread, axes, 0, 0, tiled=True).reshape(devices * ROWS, Z).astype(F32)
-    cells = N * lax.axis_size("gx") * N * lax.axis_size("gy") * Z
-    summed = summed * (1.0 / math.sqrt(cells))
-
-    def unpack(block):
-        return block[:, :3 * C].reshape(3, 3, C, 3, C).transpose(4, 0, 1, 3, 2)
+    mine, = call(add_up, [(block, BF)], name="add_up")(got)
+    summed = lax.all_to_all(mine, axes, 0, 0, tiled=True).reshape(devices * ROWS, Z)
+    gw1, gw2, gb1, gb2 = call(
+        unpack, [((27, C, C), F32)] * 2 + [((1, C), F32)] * 2, name="unpack")(summed)
+
+    def weights(g):
+        return g.reshape(3, 3, 3, C, C).transpose(3, 0, 1, 2, 4)
 
     grad_input = out.reshape(N, N, C, Z).transpose(2, 0, 1, 3)
-    return (grad_input, unpack(summed[:9 * C]), summed[18 * C:19 * C, 0],
-            unpack(summed[9 * C:18 * C]), summed[19 * C:20 * C, 0])
+    return grad_input, weights(gw1), gb1.reshape(C), weights(gw2), gb2.reshape(C)
 
 
 def solution(mesh):

time: 86.4 us -> 80.1 us (0.927)
  local copies, waits for them, and re-layouts: 6.02 us -> 2.23 us
  Pallas kernels: 16.3 us -> 13.7 us
    pallas_call x1, Pallas kernels: 10.2 us -> 5.83 us  [body(): call(outer, [((W - 6, (W - 6) * C, Z), BF), ((devices * ROWS, Z), BF)], [...]
    pallas_call x0 -> x2, Pallas kernels: none -> 1.97 us  [the longest x1 1.12 us: body(): call(unpack, [((27, C, C), F32)] * 2 + [((1, C), F32)] * 2, name='unpack')]
    unnamed x14 -> x12, local copies, waits for them, and re-layouts: 2.57 us -> 0.66 us
where the time goes in v4:
time: 80.1 us; the launch traced here: 79.7 us
  blocking collectives  23.2 us (29%)
  waiting for transfers between devices  20.9 us (26%)
  starting transfers between devices  16.8 us (21%)
  Pallas kernels  13.7 us (17%)
  local copies, waits for them, and re-layouts  2.23 us (3%)
  other arithmetic  2.01 us (3%)
  between operations  0.84 us (1%)
    all_to_all x1, blocking collectives, body(): got = lax.all_to_all(parts.reshape(block), axes, 0, 0, tiled=True)  23.2 us
    ppermute x4, starting transfers between devices, shift(): return lax.ppermute(v, axis, pairs)  12.5 us
    ppermute x4, waiting for transfers between devices, shift(): return lax.ppermute(v, axis, pairs)  12 us
    all_to_all x1, waiting for transfers between devices, body(): lax.all_to_all(mine, axes, 0, 0, tiled=True).reshape(devices * ROWS, Z)  8.94 us
    pallas_call x1, Pallas kernels, body(): call(outer, [((W - 6, (W - 6) * C, Z), BF), ((devices * ROWS, Z), BF)], [...  5.83 us
    all_to_all x1, starting transfers between devices, body(): lax.all_to_all(mine, axes, 0, 0, tiled=True).reshape(devices * ROWS, Z)  4.25 us
    pallas_call x1, Pallas kernels, body(): call(middle, [((6, (W - 2) * C, Z), BF), ((4, (W - 4) * C, Z), BF), ((2,...  3.35 us
  transfers between devices with their start and end apart: 5, of which 5 were waited for; matrix products, arithmetic and copies ran while one was open for 1% of the time, Pallas kernels for 7%

profile of v4, /device:TPU:1, one launch (start us, length us, event | category | flops | bytes accessed | tf_op | source)
XLA Modules:
  0.0 79.7 jit_solution(10498013149528492265)
XLA Ops:
  0.6 0.7 fusion
  1.6 1.1 %convert_element_type.23 = bf16[32,4,4,64]{3,2,1,0:T(4,128)(2,1)S(1)} convert(s32[32,4,4,64]{3,2,1,0:T(4,128)} %param.15) | non-fusion elementwise | flops 32768 | bytes 196608 | tf_op jit(solution)/shard_map/convert_element_type | solution.py:288
  2.7 0.2 maximum_bitcast_fusion
  3.0 0.3 copy.16
  3.4 4.1 %collective-permute-start = (bf16[36,32,128]{2,1,0:T(8,128)(2,1)S(1)}, bf16[36,32,128]{2,1,0:T(8,128)(2,1)S(1)}, u32[]{:S(2)}, u32[]{:S(2)}) collective-permute-start(bf16[36,32,128]{2,1,0:T(8,128)(2,1)S(1)} %get-tuple-element.36), channel_id=1, source_target_pairs={{0,1},{1,2},{2,3},{3,4},{4,5},{5,6},{6,7},{8,9},{9,10},{10,11},{11... | collective-permute-start | bytes 884744 | tf_op jit(solution)/shard_map/ppermute | solution.py:32
  7.5 1.3 %collective-permute-start.1 = (bf16[36,32,128]{2,1,0:T(8,128)(2,1)S(1)}, bf16[36,32,128]{2,1,0:T(8,128)(2,1)S(1)}, u32[]{:S(2)}, u32[]{:S(2)}) collective-permute-start(bf16[36,32,128]{2,1,0:T(8,128)(2,1)S(1)} %get-tuple-element.37), channel_id=1, source_target_pairs={{1,0},{2,1},{3,2},{4,3},{5,4},{6,5},{7,6},{9,8},{10,9},{11,10},{12... | collective-permute-start | bytes 884744 | tf_op jit(solution)/shard_map/ppermute | solution.py:32
  8.8 0.6 copy-done.2
  9.4 1.3 %prepare.1 = (bf16[192,384]{1,0:T(8,128)(2,1)S(1)}, bf16[192,384]{1,0:T(8,128)(2,1)S(1)}, bf16[192,384]{1,0:T(8,128)(2,1)S(1)}, bf16[192,384]{1,0:T(8,128)(2,1)S...) custom-call(bf16[27,32,32]{2,1,0:T(8,128)(2,1)S(1)} %bitcast.39, bf16[27,32,32]{2,1,0:T(8,128)(2,1)S(1)} %bitcast.40, ...), custom_call_target="tpu_custom_call" | custom-call | tf_op jit(solution)/shard_map/prepare/pallas_call | solution.py:299
  10.7 2.4 %collective-permute-done.ylow = bf16[36,32,128]{2,1,0:T(8,128)(2,1)S(1)} collective-permute-done((bf16[36,32,128]{2,1,0:T(8,128)(2,1)S(1)}, bf16[36,32,128]{2,1,0:T(8,128)(2,1)S(1)}, u32[]{:S(2)}, u32[]{:S(2)}) %collective-permute-start) | collective-permute-done | bytes 294944 | tf_op jit(solution)/shard_map/ppermute | solution.py:32
  13.1 3.8 %collective-permute-done.1.yhigh = bf16[36,32,128]{2,1,0:T(8,128)(2,1)S(1)} collective-permute-done((bf16[36,32,128]{2,1,0:T(8,128)(2,1)S(1)}, bf16[36,32,128]{2,1,0:T(8,128)(2,1)S(1)}, u32[]{:S(2)}, u32[]{:S(2)}) %collective-permute-start.1) | collective-permute-done | bytes 294944 | tf_op jit(solution)/shard_map/ppermute | solution.py:32
  17.0 0.2 pack_x.1
  17.1 5.2 %collective-permute-start.2 = (bf16[70,32,128]{2,1,0:T(8,128)(2,1)S(1)}, bf16[70,32,128]{2,1,0:T(8,128)(2,1)S(1)}, u32[]{:S(2)}, u32[]{:S(2)}) collective-permute-start(bf16[70,32,128]{2,1,0:T(8,128)(2,1)S(1)} %get-tuple-element.40), channel_id=1, source_target_pairs={{0,8},{8,16},{16,24},{24,32},{32,40},{40,48},{48,56},{56,64},{64,7... | collective-permute-start | bytes 1720328 | tf_op jit(solution)/shard_map/ppermute | solution.py:32
  22.4 1.9 %collective-permute-start.3 = (bf16[70,32,128]{2,1,0:T(8,128)(2,1)S(1)}, bf16[70,32,128]{2,1,0:T(8,128)(2,1)S(1)}, u32[]{:S(2)}, u32[]{:S(2)}) collective-permute-start(bf16[70,32,128]{2,1,0:T(8,128)(2,1)S(1)} %get-tuple-element.41), channel_id=1, source_target_pairs={{8,0},{16,8},{24,16},{32,24},{40,32},{48,40},{56,48},{64,56},{72,6... | collective-permute-start | bytes 1720328 | tf_op jit(solution)/shard_map/ppermute | solution.py:32
  24.3 3.4 %middle.1 = (bf16[6,448,128]{2,1,0:T(8,128)(2,1)S(1)}, bf16[4,384,128]{2,1,0:T(8,128)(2,1)S(1)}, bf16[2,320,128]{2,1,0:T(8,128)(2,1)S(1)}, f32[288,96]{1,0:T(8,1...) custom-call(bf16[8,512,128]{2,1,0:T(8,128)(2,1)S(1)} %get-tuple-element.38.feat.mfeat, ...), custom_call_target="tpu_custom_call" | custom-call | tf_op jit(solution)/shard_map/middle/pallas_call | solution.py:312
  27.7 1.3 %collective-permute-done.2.xlow = bf16[70,32,128]{2,1,0:T(8,128)(2,1)S(1)} collective-permute-done((bf16[70,32,128]{2,1,0:T(8,128)(2,1)S(1)}, bf16[70,32,128]{2,1,0:T(8,128)(2,1)S(1)}, u32[]{:S(2)}, u32[]{:S(2)}) %collective-permute-start.2) | collective-permute-done | bytes 573472 | tf_op jit(solution)/shard_map/ppermute | solution.py:32
  29.0 4.4 %collective-permute-done.3.xhigh = bf16[70,32,128]{2,1,0:T(8,128)(2,1)S(1)} collective-permute-done((bf16[70,32,128]{2,1,0:T(8,128)(2,1)S(1)}, bf16[70,32,128]{2,1,0:T(8,128)(2,1)S(1)}, u32[]{:S(2)}, u32[]{:S(2)}) %collective-permute-start.3) | collective-permute-done | bytes 573472 | tf_op jit(solution)/shard_map/ppermute | solution.py:32
  33.4 5.8 %outer.1 = (bf16[10,320,128]{2,1,0:T(8,128)(2,1)S(1)}, bf16[1024,128]{1,0:T(8,128)(2,1)S(1)}) custom-call(bf16[8,512,128]{2,1,0:T(8,128)(2,1)S(1)} %get-tuple-element.38.feat.mfeat, bf16[4,192,128]{2,1,0:T(8,128)(2,1)S(1)} %get-tuple-element.39.pool.mpool, bf16[70,32,128]{2,1,0:T(8,128)(2,1)S(1)} %collective-permute-done.2.xlow, ...), custom_call_target="tpu_custom_call" | custom-call | tf_op jit(solution)/shard_map/outer/pallas_call | solution.py:317
  39.2 23.2 %all_to_all.10.got = bf16[128,8,128]{2,1,0:T(8,128)(2,1)S(1)} all-to-all(bf16[128,8,128]{2,1,0:T(8,128)(2,1)S(1)} %bitcast.38), channel_id=1, replica_groups=mesh['gx'=16,'gy'=8] {'gx','gy'}, dimensions={0} | all-to-all | bytes 524288 | tf_op jit(solution)/shard_map/all_to_all | solution.py:324
  62.5 0.9 %add_up.1 = bf16[128,8,128]{2,1,0:T(8,128)(2,1)} custom-call(bf16[128,8,128]{2,1,0:T(8,128)(2,1)S(1)} %all_to_all.10.got), custom_call_target="tpu_custom_call" | custom-call | tf_op jit(solution)/shard_map/add_up/pallas_call | solution.py:326
  63.3 4.2 %all-to-all-start.1 = ((bf16[128,8,128]{2,1,0:T(8,128)(2,1)}), bf16[128,8,128]{2,1,0:T(8,128)(2,1)S(1)}, u32[]{:S(2)}, u32[]{:S(2)}) async-start(bf16[128,8,128]{2,1,0:T(8,128)(2,1)} %add_up.1), calls=%async_computation.1 | async-start | bytes 524288 | tf_op jit(solution)/shard_map/all_to_all | solution.py:327
  67.6 1.1 %final.1 = bf16[8,256,128]{2,1,0:T(8,128)(2,1)S(1)} custom-call(bf16[10,320,128]{2,1,0:T(8,128)(2,1)S(1)} %get-tuple-element.54.one, f32[3,8,128]{2,1,0:T(8,128)S(1)} %pad.9.mask, bf16[192,384]{1,0:T(8,128)(2,1)S(1)} %get-tuple-element.55.f1), custom_call_target="tpu_custom_call" | custom-call | tf_op jit(solution)/shard_map/final/pallas_call | solution.py:325
  68.7 1.0 %copy.20 = bf16[8,8,32,128]{3,1,0,2:T(8,128)(2,1)} copy(bf16[8,8,32,128]{3,2,1,0:T(8,128)(2,1)S(1)} %bitcast.34) | data formatting | bytes 1048576 | tf_op jit(solution)/shard_map/reshape | solution.py:334
  69.7 8.9 %all-to-all-done.1 = bf16[128,8,128]{2,1,0:T(8,128)(2,1)S(1)} async-done(((bf16[128,8,128]{2,1,0:T(8,128)(2,1)}), bf16[128,8,128]{2,1,0:T(8,128)(2,1)S(1)}, u32[]{:S(2)}, u32[]{:S(2)}) %all-to-all-start.1) | async-done | bytes 262176 | tf_op jit(solution)/shard_map/all_to_all | solution.py:327
  78.6 1.1 %unpack.1 = (f32[27,32,32]{2,1,0:T(8,128)}, f32[27,32,32]{2,1,0:T(8,128)}, f32[1,32]{1,0:T(1,128)}, f32[1,32]{1,0:T(1,128)}) custom-call(bf16[1024,128]{1,0:T(8,128)(2,1)S(1)} %bitcast.37), custom_call_target="tpu_custom_call" | custom-call | tf_op jit(solution)/shard_map/unpack/pallas_call | solution.py:328
  (18 shorter events, 0.4 us)
Async XLA Ops:
  1.4 1.2 %copy-start.5 = (bf16[32,4,4,64]{3,2,1,0:T(4,128)(2,1)S(1)}, bf16[32,4,4,64]{3,2,1,0:T(4,128)(2,1)}, u32[]{:S(2)}) copy-start(bf16[32,4,4,64]{3,2,1,0:T(4,128)(2,1)} %param.14) | copy-start | bytes 196612
  1.6 1.3 %copy-start.4 = (bf16[32,8,8,128]{3,2,1,0:T(8,128)(2,1)S(1)}, bf16[32,8,8,128]{3,2,1,0:T(8,128)(2,1)}, u32[]{:S(2)}) copy-start(bf16[32,8,8,128]{3,2,1,0:T(8,128)(2,1)} %param.8) | copy-start | bytes 1572868
  3.3 5.5 %copy-start = (bf16[32,3,3,3,32]{4,0,3,2,1:T(8,128)(2,1)S(1)}, bf16[32,3,3,3,32]{4,0,3,2,1:T(8,128)(2,1)}, u32[]{:S(2)}) copy-start(bf16[32,3,3,3,32]{4,0,3,2,1:T(8,128)(2,1)} %param.10) | copy-start | bytes 165892
  3.3 5.5 %copy-start.1 = (bf16[32,3,3,3,32]{4,0,3,2,1:T(8,128)(2,1)S(1)}, bf16[32,3,3,3,32]{4,0,3,2,1:T(8,128)(2,1)}, u32[]{:S(2)}) copy-start(bf16[32,3,3,3,32]{4,0,3,2,1:T(8,128)(2,1)} %param.12) | copy-start | bytes 165892
  3.4 9.8 %collective-permute-start = (bf16[36,32,128]{2,1,0:T(8,128)(2,1)S(1)}, bf16[36,32,128]{2,1,0:T(8,128)(2,1)S(1)}, u32[]{:S(2)}, u32[]{:S(2)}) collective-permute-start(bf16[36,32,128]{2,1,0:T(8,128)(2,1)S(1)} %get-tuple-element.36), channel_id=1, source_target_pairs={{0,1},{1,2},{2,3},{3,4},{4,5},{5,6},{6,7},{8,9},{9,10},{10,11},{11... | collective-permute-start | bytes 884744 | tf_op jit(solution)/shard_map/ppermute | solution.py:32
  7.5 9.5 %collective-permute-start.1 = (bf16[36,32,128]{2,1,0:T(8,128)(2,1)S(1)}, bf16[36,32,128]{2,1,0:T(8,128)(2,1)S(1)}, u32[]{:S(2)}, u32[]{:S(2)}) collective-permute-start(bf16[36,32,128]{2,1,0:T(8,128)(2,1)S(1)} %get-tuple-element.37), channel_id=1, source_target_pairs={{1,0},{2,1},{3,2},{4,3},{5,4},{6,5},{7,6},{9,8},{10,9},{11,10},{12... | collective-permute-start | bytes 884744 | tf_op jit(solution)/shard_map/ppermute | solution.py:32
  8.8 0.7 copy-start.2
  8.8 0.7 copy-start.3
  17.1 11.9 %collective-permute-start.2 = (bf16[70,32,128]{2,1,0:T(8,128)(2,1)S(1)}, bf16[70,32,128]{2,1,0:T(8,128)(2,1)S(1)}, u32[]{:S(2)}, u32[]{:S(2)}) collective-permute-start(bf16[70,32,128]{2,1,0:T(8,128)(2,1)S(1)} %get-tuple-element.40), channel_id=1, source_target_pairs={{0,8},{8,16},{16,24},{24,32},{32,40},{40,48},{48,56},{56,64},{64,7... | collective-permute-start | bytes 1720328 | tf_op jit(solution)/shard_map/ppermute | solution.py:32
  22.4 11.0 %collective-permute-start.3 = (bf16[70,32,128]{2,1,0:T(8,128)(2,1)S(1)}, bf16[70,32,128]{2,1,0:T(8,128)(2,1)S(1)}, u32[]{:S(2)}, u32[]{:S(2)}) collective-permute-start(bf16[70,32,128]{2,1,0:T(8,128)(2,1)S(1)} %get-tuple-element.41), channel_id=1, source_target_pairs={{8,0},{16,8},{24,16},{32,24},{40,32},{48,40},{56,48},{64,56},{72,6... | collective-permute-start | bytes 1720328 | tf_op jit(solution)/shard_map/ppermute | solution.py:32
  63.3 15.3 %all-to-all-start.1 = ((bf16[128,8,128]{2,1,0:T(8,128)(2,1)}), bf16[128,8,128]{2,1,0:T(8,128)(2,1)S(1)}, u32[]{:S(2)}, u32[]{:S(2)}) async-start(bf16[128,8,128]{2,1,0:T(8,128)(2,1)} %add_up.1), calls=%async_computation.1 | async-start | bytes 524288 | tf_op jit(solution)/shard_map/all_to_all | solution.py:327

commit v5 on v4

--- a/solution.py
+++ b/solution.py
@@ -6,6 +6,7 @@
 from jax.experimental import pallas as pl
 from jax.experimental.pallas import tpu as pltpu
 from jax.sharding import PartitionSpec as P
+
 
 BF = jnp.bfloat16
 F32 = jnp.float32
@@ -16,13 +17,12 @@
 CELLS = 128 * 64 * 128
 
 
-def call(kernel, outs, scratch=(), name=None):
+def call(kernel, outs, scratch=()):
     return pl.pallas_call(
         kernel,
         out_shape=tuple(jax.ShapeDtypeStruct(s, d) for s, d in outs),
         scratch_shapes=[pltpu.VMEM(s, d) for s, d in scratch],
         compiler_params=pltpu.CompilerParams(vmem_limit_bytes=40 << 20),
-        name=name,
     )
 
 
@@ -58,17 +58,23 @@
         dst[...] = jnp.transpose(jnp.broadcast_to(src[...], (Z, C)))
 
 
-def pack_y(own, pown, mlow, mhigh):
+def pack_faces(own, pown, ylow, yhigh, xlow, xhigh):
     for x in range(N):
         for k in range(H):
-            mlow[x * H + k] = own[x, cell(N - H + k), :]
-            mhigh[x * H + k] = own[x, cell(k), :]
-    for x in range(Q):
-        mlow[N * H + x] = pown[x, cell(Q - 1), :]
-        mhigh[N * H + x] = pown[x, cell(0), :]
-
-
-def pack_x(own, pown, ylow, yhigh, feat, pool, mlow, mhigh):
+            ylow[x * H + k] = own[x, cell(N - H + k), :]
+            yhigh[x * H + k] = own[x, cell(k), :]
+    for k in range(H):
+        for y in range(N):
+            xlow[k * N + y] = own[N - H + k, cell(y), :]
+            xhigh[k * N + y] = own[k, cell(y), :]
+    for q in range(Q):
+        ylow[N * H + q] = pown[q, cell(Q - 1), :]
+        yhigh[N * H + q] = pown[q, cell(0), :]
+        xlow[N * H + q] = pown[Q - 1, cell(q), :]
+        xhigh[N * H + q] = pown[0, cell(q), :]
+
+
+def pack_corners(own, pown, ylow, yhigh, feat, pool, clow, chigh):
     for x in range(N):
         feat[x, cell(H, N), :] = own[x]
         for k in range(H):
@@ -78,13 +84,16 @@
         pool[x, cell(1, Q), :] = pown[x]
         pool[x, cell(0), :] = ylow[N * H + x]
         pool[x, cell(Q + 1), :] = yhigh[N * H + x]
-    for k in range(H):
-        for y in range(W):
-            mlow[k * W + y] = feat[N - H + k, cell(y), :]
-            mhigh[k * W + y] = feat[k, cell(y), :]
-    for y in range(Q + 2):
-        mlow[H * W + y] = pool[Q - 1, cell(y), :]
-        mhigh[H * W + y] = pool[0, cell(y), :]
+    for x in range(H):
+        for k in range(H):
+            clow[x * N + k] = ylow[(N - H + x) * H + k]
+            clow[x * N + H + k] = yhigh[(N - H + x) * H + k]
+            chigh[x * N + k] = ylow[x * H + k]
+            chigh[x * N + H + k] = yhigh[x * H + k]
+    clow[N * H] = ylow[N * H + Q - 1]
+    clow[N * H + 1] = yhigh[N * H + Q - 1]
+    chigh[N * H] = ylow[N * H]
+    chigh[N * H + 1] = yhigh[N * H]
 
 
 def after(v):
@@ -119,6 +128,7 @@
 def planes(ref, first=0):
     def rows_at(x, y, n=1):
         return ref[x - first, cell(y, n), :]
+
     return rows_at
 
 
@@ -151,12 +161,14 @@
 def putter(ref, index):
     def put(x, y, v):
         ref[index(x), cell(y), :] = v
+
     return put
 
 
 def upstream(ups, index):
     def ups_at(i, j):
         return ups[index(i), cell(j), 0:Z], ups[index(i), cell(j), Z:2 * Z]
+
     return ups_at
 
 
@@ -195,18 +207,28 @@
         term(x, s1, feat_at, H - 1, one_at, H - 3, acc1)
 
 
-def outer(mfeat, mpool, xlow, xhigh, mhid, mtwo, mone, macc1, macc2, ms1, ms2, mask,
+def outer(mfeat, mpool, xlow, xhigh, clow, chigh, mhid, mtwo, mone, macc1, macc2, ms1, ms2, mask,
           t1, t2, f2, b1, b2, one, parts, hid, two, ups, acc1, acc2, s1, s2):
     def feat_at(x, y, n=1):
         if H <= x < H + N:
             return mfeat[x - H, cell(y, n), :]
-        ref, k = (xlow, x) if x < H else (xhigh, x - H - N)
-        return ref[k * W + y:k * W + y + n].reshape(n * C, Z)
+        side, corner, k = (xlow, clow, x) if x < H else (xhigh, chigh, x - H - N)
+        cells = []
+        for v in range(y, y + n):
+            if H <= v < H + N:
+                cells.append(side[k * N + v - H])
+            else:
+                cells.append(corner[k * N + (v if v < H else v - N)])
+        return jnp.concatenate(cells, axis=0)
 
     spread = spreader()
-    for y in range(Q + 2):
-        ups[0, cell(y), :] = jnp.dot(xlow[H * W + y], spread, preferred_element_type=F32)
-        ups[3, cell(y), :] = jnp.dot(xhigh[H * W + y], spread, preferred_element_type=F32)
+    for row, side, corner in ((0, xlow, clow), (3, xhigh, chigh)):
+        for y in range(Q + 2):
+            if 1 <= y <= Q:
+                given = side[N * H + y - 1]
+            else:
+                given = corner[N * H + (y > 0)]
+            ups[row, cell(y), :] = jnp.dot(given, spread, preferred_element_type=F32)
     ups[1] = jnp.dot(mpool[0], spread, preferred_element_type=F32)
     ups[2] = jnp.dot(mpool[Q - 1], spread, preferred_element_type=F32)
 
@@ -215,6 +237,7 @@
             if 4 <= x < 4 + count:
                 return mid[x - 4, cell(y, n), :]
             return ref[x if x < 4 else x - count, cell(y, n), :]
+
         return rows_at
 
     hid_at, two_at = merged(hid, mhid, 6), merged(two, mtwo, 4)
@@ -276,7 +299,7 @@
         conv_pair(planes(one), 2 * i, f1, N, write_out, i)
 
 
-def body(features, occupancy, weight_one, bias_one, weight_two, bias_two, grad_pooled, pool_choice):
+def steps(features, occupancy, weight_one, bias_one, weight_two, bias_two, grad_pooled, pool_choice):
     axes = ("gx", "gy")
     devices = lax.axis_size("gx") * lax.axis_size("gy")
     flags = jnp.pad(occupancy, ((1, 1), (1, 1), (0, 0)))
@@ -288,45 +311,46 @@
     pown = jnp.concatenate([grad_pooled, pool_choice.astype(BF)], axis=3)
     pown = pown.transpose(1, 2, 0, 3).reshape(Q, Q * C, Z)
 
-    ymsg = N * H + Q
-    mlow, mhigh = call(pack_y, [((ymsg, C, Z), BF)] * 2, name="pack_y")(own, pown)
-    ylow = shift(mlow, "gy", 1)
-    yhigh = shift(mhigh, "gy", -1)
+    face = ((N * H + Q, C, Z), BF)
+    ydown, yup, xdown, xup = call(pack_faces, [face] * 4)(own, pown)
+    ylow = shift(ydown, "gy", 1)
+    yhigh = shift(yup, "gy", -1)
+    xlow = shift(xdown, "gx", 1)
+    xhigh = shift(xup, "gx", -1)
 
     def blocks(weight):
         return weight.transpose(1, 2, 3, 0, 4).reshape(27, C, C)
 
     t1, t2, f2, f1, b1, b2 = call(
-        prepare, [((6 * C, 12 * C), BF)] * 4 + [((C, Z), F32)] * 2, name="prepare")(
-            blocks(weight_one), blocks(weight_two), bias_one.reshape(1, C), bias_two.reshape(1, C))
+        prepare, [((6 * C, 12 * C), BF)] * 4 + [((C, Z), F32)] * 2)(
+            blocks(weight_one), blocks(weight_two),
+            bias_one.reshape(1, C), bias_two.reshape(1, C))
 
     own, pown, t1 = lax.optimization_barrier((own, pown, t1))
-    xmsg = W * H + Q + 2
-    mfeat, mpool, mlow, mhigh = call(
-        pack_x, [((N, W * C, Z), BF), ((Q, (Q + 2) * C, Z), BF)] + [((xmsg, C, Z), BF)] * 2,
-        name="pack_x")(own, pown, ylow, yhigh)
-    xlow = shift(mlow, "gx", 1)
-    xhigh = shift(mhigh, "gx", -1)
+    mfeat, mpool, cdown, cup = call(
+        pack_corners,
+        [((N, W * C, Z), BF), ((Q, (Q + 2) * C, Z), BF)] + [((N * H + 2, C, Z), BF)] * 2)(own, pown, ylow, yhigh)
+    clow = shift(cdown, "gx", 1)
+    chigh = shift(cup, "gx", -1)
 
     grads = [((9 * C, 3 * C), F32)] * 2 + [((C, Z), F32)] * 2
     mids = call(
         middle,
         [((6, (W - 2) * C, Z), BF), ((4, (W - 4) * C, Z), BF), ((2, (W - 6) * C, Z), BF)] + grads,
-        [((2, (Q + 2) * C, 2 * Z), F32)], name="middle")(mfeat, mpool, mask, t1, t2, f2, b1, b2)
+        [((2, (Q + 2) * C, 2 * Z), F32)])(mfeat, mpool, mask, t1, t2, f2, b1, b2)
 
     one, parts = call(
         outer, [((W - 6, (W - 6) * C, Z), BF), ((devices * ROWS, Z), BF)],
         [((8, (W - 2) * C, Z), BF), ((8, (W - 4) * C, Z), BF),
-         ((4, (Q + 2) * C, 2 * Z), F32)] + grads,
-        name="outer")(mfeat, mpool, xlow, xhigh, *mids, mask, t1, t2, f2, b1, b2)
+         ((4, (Q + 2) * C, 2 * Z), F32)] + grads)(mfeat, mpool, xlow, xhigh, clow, chigh, *mids, mask, t1, t2, f2, b1, b2)
 
     block = (devices, ROWS, Z)
     got = lax.all_to_all(parts.reshape(block), axes, 0, 0, tiled=True)
-    out, = call(final, [((N, N * C, Z), BF)], name="final")(one, mask, f1)
-    mine, = call(add_up, [(block, BF)], name="add_up")(got)
+    out, = call(final, [((N, N * C, Z), BF)])(one, mask, f1)
+    mine, = call(add_up, [(block, BF)])(got)
     summed = lax.all_to_all(mine, axes, 0, 0, tiled=True).reshape(devices * ROWS, Z)
     gw1, gw2, gb1, gb2 = call(
-        unpack, [((27, C, C), F32)] * 2 + [((1, C), F32)] * 2, name="unpack")(summed)
+        unpack, [((27, C, C), F32)] * 2 + [((1, C), F32)] * 2)(summed)
 
     def weights(g):
         return g.reshape(3, 3, 3, C, C).transpose(3, 0, 1, 2, 4)
@@ -338,7 +362,7 @@
 def solution(mesh):
     cells = P(None, "gx", "gy", None)
     return jax.shard_map(
-        body,
+        steps,
         mesh=mesh,
         in_specs=(cells, P(), P(), P(), P(), P(), cells, cells),
         out_specs=(cells, P(), P(), P(), P()),

time: 80.1 us -> 78.8 us (0.984)
  waiting for transfers between devices: 20.9 us -> 11.5 us
  starting transfers between devices: 16.8 us -> 23 us
  blocking collectives: 23.2 us -> 25.1 us
    ppermute x4 -> x6, waiting for transfers between devices: 12 us -> 2.56 us  [shift(): return lax.ppermute(v, axis, pairs)]
    ppermute x4 -> x6, starting transfers between devices: 12.5 us -> 18.7 us  [shift(): return lax.ppermute(v, axis, pairs)]
    all_to_all x1, blocking collectives: 23.2 us -> 25.1 us  [steps(): got = lax.all_to_all(parts.reshape(block), axes, 0, 0, tiled=True)]
  transfers between devices with their start and end apart: 5 -> 7, of which waited for: 5 -> 2; matrix products, arithmetic and copies ran while one was open for 1% -> 1% of each run, Pallas kernels for 7% -> 7%
where the time goes in v5:
time: 78.8 us; the launch traced here: 78.4 us
  blocking collectives  25.1 us (32%)
  starting transfers between devices  23 us (29%)
  Pallas kernels  13.7 us (17%)
  waiting for transfers between devices  11.5 us (15%)
  local copies, waits for them, and re-layouts  2.23 us (3%)
  other arithmetic  2.01 us (3%)
  between operations  0.9 us (1%)
    all_to_all x1, blocking collectives, steps(): got = lax.all_to_all(parts.reshape(block), axes, 0, 0, tiled=True)  25.1 us
    ppermute x6, starting transfers between devices, shift(): return lax.ppermute(v, axis, pairs)  18.7 us
    all_to_all x1, waiting for transfers between devices, steps(): lax.all_to_all(mine, axes, 0, 0, tiled=True).reshape(devices * ROWS, Z)  8.94 us
    pallas_call x1, Pallas kernels, steps(): call(outer, [((W - 6, (W - 6) * C, Z), BF), ((devices * ROWS, Z), BF)], [...  5.79 us
    all_to_all x1, starting transfers between devices, steps(): lax.all_to_all(mine, axes, 0, 0, tiled=True).reshape(devices * ROWS, Z)  4.25 us
    pallas_call x1, Pallas kernels, steps(): call(middle, [((6, (W - 2) * C, Z), BF), ((4, (W - 4) * C, Z), BF), ((2,...  3.35 us
    ppermute x6, waiting for transfers between devices, shift(): return lax.ppermute(v, axis, pairs)  2.56 us
  transfers between devices with their start and end apart: 7, of which 2 were waited for; matrix products, arithmetic and copies ran while one was open for 1% of the time, Pallas kernels for 7%

profile of v5, /device:TPU:1, one launch (start us, length us, event | category | flops | bytes accessed | tf_op | source)
XLA Modules:
  0.0 78.4 jit_solution(7041035895617716029)
XLA Ops:
  0.6 0.7 fusion
  1.6 1.1 %convert_element_type.23 = bf16[32,4,4,64]{3,2,1,0:T(4,128)(2,1)S(1)} convert(s32[32,4,4,64]{3,2,1,0:T(4,128)} %param.15) | non-fusion elementwise | flops 32768 | bytes 196608 | tf_op jit(solution)/shard_map/convert_element_type | solution.py:311
  2.7 0.2 maximum_bitcast_fusion
  3.0 0.3 copy.16
  3.3 0.1 shard_map.120
  3.4 4.1 %collective-permute-start = (bf16[36,32,128]{2,1,0:T(8,128)(2,1)S(1)}, bf16[36,32,128]{2,1,0:T(8,128)(2,1)S(1)}, u32[]{:S(2)}, u32[]{:S(2)}) collective-permute-start(bf16[36,32,128]{2,1,0:T(8,128)(2,1)S(1)} %get-tuple-element.38), channel_id=1, source_target_pairs={{0,1},{1,2},{2,3},{3,4},{4,5},{5,6},{6,7},{8,9},{9,10},{10,11},{11... | collective-permute-start | bytes 884744 | tf_op jit(solution)/shard_map/ppermute | solution.py:32
  7.5 1.3 %collective-permute-start.1 = (bf16[36,32,128]{2,1,0:T(8,128)(2,1)S(1)}, bf16[36,32,128]{2,1,0:T(8,128)(2,1)S(1)}, u32[]{:S(2)}, u32[]{:S(2)}) collective-permute-start(bf16[36,32,128]{2,1,0:T(8,128)(2,1)S(1)} %get-tuple-element.39), channel_id=1, source_target_pairs={{1,0},{2,1},{3,2},{4,3},{5,4},{6,5},{7,6},{9,8},{10,9},{11,10},{12... | collective-permute-start | bytes 884744 | tf_op jit(solution)/shard_map/ppermute | solution.py:32
  8.8 4.4 %collective-permute-start.2 = (bf16[36,32,128]{2,1,0:T(8,128)(2,1)S(1)}, bf16[36,32,128]{2,1,0:T(8,128)(2,1)S(1)}, u32[]{:S(2)}, u32[]{:S(2)}) collective-permute-start(bf16[36,32,128]{2,1,0:T(8,128)(2,1)S(1)} %get-tuple-element.42), channel_id=1, source_target_pairs={{0,8},{8,16},{16,24},{24,32},{32,40},{40,48},{48,56},{56,64},{64,7... | collective-permute-start | bytes 884744 | tf_op jit(solution)/shard_map/ppermute | solution.py:32
  13.2 1.9 %collective-permute-start.3 = (bf16[36,32,128]{2,1,0:T(8,128)(2,1)S(1)}, bf16[36,32,128]{2,1,0:T(8,128)(2,1)S(1)}, u32[]{:S(2)}, u32[]{:S(2)}) collective-permute-start(bf16[36,32,128]{2,1,0:T(8,128)(2,1)S(1)} %get-tuple-element.43), channel_id=1, source_target_pairs={{8,0},{16,8},{24,16},{32,24},{40,32},{48,40},{56,48},{64,56},{72,6... | collective-permute-start | bytes 884744 | tf_op jit(solution)/shard_map/ppermute | solution.py:32
  15.2 0.6 copy-done.2
  15.8 1.3 %shard_map.119 = (bf16[192,384]{1,0:T(8,128)(2,1)S(1)}, bf16[192,384]{1,0:T(8,128)(2,1)S(1)}, bf16[192,384]{1,0:T(8,128)(2,1)S(1)}, bf16[192,384]{1,0:T(8,128)(2...) custom-call(bf16[27,32,32]{2,1,0:T(8,128)(2,1)S(1)} %bitcast.39, bf16[27,32,32]{2,1,0:T(8,128)(2,1)S(1)} %bitcast.40, ...), custom_call_target="tpu_custom_call" | custom-call | tf_op jit(solution)/shard_map/pallas_call | solution.py:324
  17.1 0.1 shard_map.121
  17.3 5.1 %collective-permute-start.4 = (bf16[34,32,128]{2,1,0:T(8,128)(2,1)S(1)}, bf16[34,32,128]{2,1,0:T(8,128)(2,1)S(1)}, u32[]{:S(2)}, u32[]{:S(2)}) collective-permute-start(bf16[34,32,128]{2,1,0:T(8,128)(2,1)S(1)} %get-tuple-element.44), channel_id=1, source_target_pairs={{0,8},{8,16},{16,24},{24,32},{32,40},{40,48},{48,56},{56,64},{64,7... | collective-permute-start | bytes 835592 | tf_op jit(solution)/shard_map/ppermute | solution.py:32
  22.4 1.9 %collective-permute-start.5 = (bf16[34,32,128]{2,1,0:T(8,128)(2,1)S(1)}, bf16[34,32,128]{2,1,0:T(8,128)(2,1)S(1)}, u32[]{:S(2)}, u32[]{:S(2)}) collective-permute-start(bf16[34,32,128]{2,1,0:T(8,128)(2,1)S(1)} %get-tuple-element.45), channel_id=1, source_target_pairs={{8,0},{16,8},{24,16},{32,24},{40,32},{48,40},{56,48},{64,56},{72,6... | collective-permute-start | bytes 835592 | tf_op jit(solution)/shard_map/ppermute | solution.py:32
  24.4 3.4 %shard_map.122 = (bf16[6,448,128]{2,1,0:T(8,128)(2,1)S(1)}, bf16[4,384,128]{2,1,0:T(8,128)(2,1)S(1)}, bf16[2,320,128]{2,1,0:T(8,128)(2,1)S(1)}, f32[288,96]{1,0:...) custom-call(bf16[8,512,128]{2,1,0:T(8,128)(2,1)S(1)} %get-tuple-element.40.feat.mfeat, ...), custom_call_target="tpu_custom_call" | custom-call | tf_op jit(solution)/shard_map/pallas_call | solution.py:337
  27.7 2.5 %collective-permute-done.5.chigh = bf16[34,32,128]{2,1,0:T(8,128)(2,1)S(1)} collective-permute-done((bf16[34,32,128]{2,1,0:T(8,128)(2,1)S(1)}, bf16[34,32,128]{2,1,0:T(8,128)(2,1)S(1)}, u32[]{:S(2)}, u32[]{:S(2)}) %collective-permute-start.5) | collective-permute-done | bytes 278560 | tf_op jit(solution)/shard_map/ppermute | solution.py:32
  30.3 5.8 %shard_map.123 = (bf16[10,320,128]{2,1,0:T(8,128)(2,1)S(1)}, bf16[1024,128]{1,0:T(8,128)(2,1)S(1)}) custom-call(bf16[8,512,128]{2,1,0:T(8,128)(2,1)S(1)} %get-tuple-element.40.feat.mfeat, bf16[4,192,128]{2,1,0:T(8,128)(2,1)S(1)} %get-tuple-element.41.pool.mpool, bf16[36,32,128]{2,1,0:T(8,128)(2,1)S(1)} %collective-permute-done.2.xlow, ...), custom_call_target="tpu_custom_call" | custom-call | tf_op jit(solution)/shard_map/pallas_call | solution.py:342
  36.1 25.1 %all_to_all.10.got = bf16[128,8,128]{2,1,0:T(8,128)(2,1)S(1)} all-to-all(bf16[128,8,128]{2,1,0:T(8,128)(2,1)S(1)} %bitcast.38), channel_id=1, replica_groups=mesh['gx'=16,'gy'=8] {'gx','gy'}, dimensions={0} | all-to-all | bytes 524288 | tf_op jit(solution)/shard_map/all_to_all | solution.py:348
  61.1 0.9 %shard_map.125 = bf16[128,8,128]{2,1,0:T(8,128)(2,1)} custom-call(bf16[128,8,128]{2,1,0:T(8,128)(2,1)S(1)} %all_to_all.10.got), custom_call_target="tpu_custom_call" | custom-call | tf_op jit(solution)/shard_map/pallas_call | solution.py:350
  62.0 4.2 %all-to-all-start.1 = ((bf16[128,8,128]{2,1,0:T(8,128)(2,1)}), bf16[128,8,128]{2,1,0:T(8,128)(2,1)S(1)}, u32[]{:S(2)}, u32[]{:S(2)}) async-start(bf16[128,8,128]{2,1,0:T(8,128)(2,1)} %shard_map.125), calls=%async_computation.1 | async-start | bytes 524288 | tf_op jit(solution)/shard_map/all_to_all | solution.py:351
  66.3 1.1 %shard_map.124 = bf16[8,256,128]{2,1,0:T(8,128)(2,1)S(1)} custom-call(bf16[10,320,128]{2,1,0:T(8,128)(2,1)S(1)} %get-tuple-element.58.one, f32[3,8,128]{2,1,0:T(8,128)S(1)} %pad.9.mask, bf16[192,384]{1,0:T(8,128)(2,1)S(1)} %get-tuple-element.59.f1), custom_call_target="tpu_custom_call" | custom-call | tf_op jit(solution)/shard_map/pallas_call | solution.py:349
  67.3 1.0 %copy.20 = bf16[8,8,32,128]{3,1,0,2:T(8,128)(2,1)} copy(bf16[8,8,32,128]{3,2,1,0:T(8,128)(2,1)S(1)} %bitcast.34) | data formatting | bytes 1048576 | tf_op jit(solution)/shard_map/reshape | solution.py:358
  68.3 8.9 %all-to-all-done.1 = bf16[128,8,128]{2,1,0:T(8,128)(2,1)S(1)} async-done(((bf16[128,8,128]{2,1,0:T(8,128)(2,1)}), bf16[128,8,128]{2,1,0:T(8,128)(2,1)S(1)}, u32[]{:S(2)}, u32[]{:S(2)}) %all-to-all-start.1) | async-done | bytes 262176 | tf_op jit(solution)/shard_map/all_to_all | solution.py:351
  77.3 1.1 %shard_map.126 = (f32[27,32,32]{2,1,0:T(8,128)}, f32[27,32,32]{2,1,0:T(8,128)}, f32[1,32]{1,0:T(1,128)}, f32[1,32]{1,0:T(1,128)}) custom-call(bf16[1024,128]{1,0:T(8,128)(2,1)S(1)} %bitcast.37), custom_call_target="tpu_custom_call" | custom-call | tf_op jit(solution)/shard_map/pallas_call | solution.py:352
  (22 shorter events, 0.3 us)
Async XLA Ops:
  1.4 1.2 %copy-start.5 = (bf16[32,4,4,64]{3,2,1,0:T(4,128)(2,1)S(1)}, bf16[32,4,4,64]{3,2,1,0:T(4,128)(2,1)}, u32[]{:S(2)}) copy-start(bf16[32,4,4,64]{3,2,1,0:T(4,128)(2,1)} %param.14) | copy-start | bytes 196612
  1.6 1.3 %copy-start.4 = (bf16[32,8,8,128]{3,2,1,0:T(8,128)(2,1)S(1)}, bf16[32,8,8,128]{3,2,1,0:T(8,128)(2,1)}, u32[]{:S(2)}) copy-start(bf16[32,8,8,128]{3,2,1,0:T(8,128)(2,1)} %param.8) | copy-start | bytes 1572868
  3.3 11.9 %copy-start = (bf16[32,3,3,3,32]{4,0,3,2,1:T(8,128)(2,1)S(1)}, bf16[32,3,3,3,32]{4,0,3,2,1:T(8,128)(2,1)}, u32[]{:S(2)}) copy-start(bf16[32,3,3,3,32]{4,0,3,2,1:T(8,128)(2,1)} %param.10) | copy-start | bytes 165892
  3.3 11.9 %copy-start.1 = (bf16[32,3,3,3,32]{4,0,3,2,1:T(8,128)(2,1)S(1)}, bf16[32,3,3,3,32]{4,0,3,2,1:T(8,128)(2,1)}, u32[]{:S(2)}) copy-start(bf16[32,3,3,3,32]{4,0,3,2,1:T(8,128)(2,1)} %param.12) | copy-start | bytes 165892
  3.4 13.7 %collective-permute-start = (bf16[36,32,128]{2,1,0:T(8,128)(2,1)S(1)}, bf16[36,32,128]{2,1,0:T(8,128)(2,1)S(1)}, u32[]{:S(2)}, u32[]{:S(2)}) collective-permute-start(bf16[36,32,128]{2,1,0:T(8,128)(2,1)S(1)} %get-tuple-element.38), channel_id=1, source_target_pairs={{0,1},{1,2},{2,3},{3,4},{4,5},{5,6},{6,7},{8,9},{9,10},{10,11},{11... | collective-permute-start | bytes 884744 | tf_op jit(solution)/shard_map/ppermute | solution.py:32
  7.5 9.6 %collective-permute-start.1 = (bf16[36,32,128]{2,1,0:T(8,128)(2,1)S(1)}, bf16[36,32,128]{2,1,0:T(8,128)(2,1)S(1)}, u32[]{:S(2)}, u32[]{:S(2)}) collective-permute-start(bf16[36,32,128]{2,1,0:T(8,128)(2,1)S(1)} %get-tuple-element.39), channel_id=1, source_target_pairs={{1,0},{2,1},{3,2},{4,3},{5,4},{6,5},{7,6},{9,8},{10,9},{11,10},{12... | collective-permute-start | bytes 884744 | tf_op jit(solution)/shard_map/ppermute | solution.py:32
  8.8 18.9 %collective-permute-start.2 = (bf16[36,32,128]{2,1,0:T(8,128)(2,1)S(1)}, bf16[36,32,128]{2,1,0:T(8,128)(2,1)S(1)}, u32[]{:S(2)}, u32[]{:S(2)}) collective-permute-start(bf16[36,32,128]{2,1,0:T(8,128)(2,1)S(1)} %get-tuple-element.42), channel_id=1, source_target_pairs={{0,8},{8,16},{16,24},{24,32},{32,40},{40,48},{48,56},{56,64},{64,7... | collective-permute-start | bytes 884744 | tf_op jit(solution)/shard_map/ppermute | solution.py:32
  13.2 14.5 %collective-permute-start.3 = (bf16[36,32,128]{2,1,0:T(8,128)(2,1)S(1)}, bf16[36,32,128]{2,1,0:T(8,128)(2,1)S(1)}, u32[]{:S(2)}, u32[]{:S(2)}) collective-permute-start(bf16[36,32,128]{2,1,0:T(8,128)(2,1)S(1)} %get-tuple-element.43), channel_id=1, source_target_pairs={{8,0},{16,8},{24,16},{32,24},{40,32},{48,40},{56,48},{64,56},{72,6... | collective-permute-start | bytes 884744 | tf_op jit(solution)/shard_map/ppermute | solution.py:32
  15.2 0.7 copy-start.2
  15.2 0.7 copy-start.3
  17.3 10.5 %collective-permute-start.4 = (bf16[34,32,128]{2,1,0:T(8,128)(2,1)S(1)}, bf16[34,32,128]{2,1,0:T(8,128)(2,1)S(1)}, u32[]{:S(2)}, u32[]{:S(2)}) collective-permute-start(bf16[34,32,128]{2,1,0:T(8,128)(2,1)S(1)} %get-tuple-element.44), channel_id=1, source_target_pairs={{0,8},{8,16},{16,24},{24,32},{32,40},{40,48},{48,56},{56,64},{64,7... | collective-permute-start | bytes 835592 | tf_op jit(solution)/shard_map/ppermute | solution.py:32
  22.4 7.9 %collective-permute-start.5 = (bf16[34,32,128]{2,1,0:T(8,128)(2,1)S(1)}, bf16[34,32,128]{2,1,0:T(8,128)(2,1)S(1)}, u32[]{:S(2)}, u32[]{:S(2)}) collective-permute-start(bf16[34,32,128]{2,1,0:T(8,128)(2,1)S(1)} %get-tuple-element.45), channel_id=1, source_target_pairs={{8,0},{16,8},{24,16},{32,24},{40,32},{48,40},{56,48},{64,56},{72,6... | collective-permute-start | bytes 835592 | tf_op jit(solution)/shard_map/ppermute | solution.py:32
  62.0 15.3 %all-to-all-start.1 = ((bf16[128,8,128]{2,1,0:T(8,128)(2,1)}), bf16[128,8,128]{2,1,0:T(8,128)(2,1)S(1)}, u32[]{:S(2)}, u32[]{:S(2)}) async-start(bf16[128,8,128]{2,1,0:T(8,128)(2,1)} %shard_map.125), calls=%async_computation.1 | async-start | bytes 524288 | tf_op jit(solution)/shard_map/all_to_all | solution.py:351

commit v6 on v5

--- a/solution.py
+++ b/solution.py
@@ -30,6 +30,17 @@
     devices = lax.axis_size(axis)
     pairs = [(i, i + step) for i in range(devices) if 0 <= i + step < devices]
     return lax.ppermute(v, axis, pairs)
+
+
+def swap(v, axis, first):
+    pairs = []
+    for i in range(first, lax.axis_size(axis) - 1, 2):
+        pairs += [(i, i + 1), (i + 1, i)]
+    return lax.ppermute(v, axis, pairs)
+
+
+def odd_place():
+    return lax.axis_index("gx") % 2
 
 
 def cell(y, n=1):
@@ -58,23 +69,34 @@
         dst[...] = jnp.transpose(jnp.broadcast_to(src[...], (Z, C)))
 
 
-def pack_faces(own, pown, ylow, yhigh, xlow, xhigh):
+def pack_faces(own, pown, ylow, yhigh, near, far):
+    odd = odd_place()
     for x in range(N):
         for k in range(H):
             ylow[x * H + k] = own[x, cell(N - H + k), :]
             yhigh[x * H + k] = own[x, cell(k), :]
-    for k in range(H):
-        for y in range(N):
-            xlow[k * N + y] = own[N - H + k, cell(y), :]
-            xhigh[k * N + y] = own[k, cell(y), :]
     for q in range(Q):
         ylow[N * H + q] = pown[q, cell(Q - 1), :]
         yhigh[N * H + q] = pown[q, cell(0), :]
-        xlow[N * H + q] = pown[Q - 1, cell(q), :]
-        xhigh[N * H + q] = pown[0, cell(q), :]
-
-
-def pack_corners(own, pown, ylow, yhigh, feat, pool, clow, chigh):
+    for ref, low in ((near, odd), (far, 1 - odd)):
+        for k in range(H):
+            for y in range(N):
+                ref[k * N + y] = own[(N - H) * (1 - low) + k, cell(y), :]
+        for q in range(Q):
+            ref[N * H + q] = pown[(Q - 1) * (1 - low), cell(q), :]
+
+
+def pack_corners(own, pown, ylow, yhigh, feat, pool, near, far):
+    odd = odd_place()
+    for ref, low in ((near, odd), (far, 1 - odd)):
+        for x in range(H):
+            for k in range(H):
+                at = ((N - H) * (1 - low) + x) * H + k
+                ref[x * N + k] = ylow[at]
+                ref[x * N + H + k] = yhigh[at]
+        at = N * H + (Q - 1) * (1 - low)
+        ref[N * H] = ylow[at]
+        ref[N * H + 1] = yhigh[at]
     for x in range(N):
         feat[x, cell(H, N), :] = own[x]
         for k in range(H):
@@ -84,16 +106,6 @@
         pool[x, cell(1, Q), :] = pown[x]
         pool[x, cell(0), :] = ylow[N * H + x]
         pool[x, cell(Q + 1), :] = yhigh[N * H + x]
-    for x in range(H):
-        for k in range(H):
-            clow[x * N + k] = ylow[(N - H + x) * H + k]
-            clow[x * N + H + k] = yhigh[(N - H + x) * H + k]
-            chigh[x * N + k] = ylow[x * H + k]
-            chigh[x * N + H + k] = yhigh[x * H + k]
-    clow[N * H] = ylow[N * H + Q - 1]
-    clow[N * H + 1] = yhigh[N * H + Q - 1]
-    chigh[N * H] = ylow[N * H]
-    chigh[N * H + 1] = yhigh[N * H]
 
 
 def after(v):
@@ -207,8 +219,20 @@
         term(x, s1, feat_at, H - 1, one_at, H - 3, acc1)
 
 
-def outer(mfeat, mpool, xlow, xhigh, clow, chigh, mhid, mtwo, mone, macc1, macc2, ms1, ms2, mask,
-          t1, t2, f2, b1, b2, one, parts, hid, two, ups, acc1, acc2, s1, s2):
+def outer(mfeat, mpool, xnear, xfar, cnear, cfar, mhid, mtwo, mone, macc1, macc2, ms1, ms2, mask,
+          t1, t2, f2, b1, b2, one, parts, xlow, xhigh, clow, chigh, hid, two, ups, acc1, acc2, s1, s2):
+    odd = odd_place()
+
+    @pl.when(odd == 0)
+    def _():
+        xlow[...], xhigh[...] = xfar[...], xnear[...]
+        clow[...], chigh[...] = cfar[...], cnear[...]
+
+    @pl.when(odd == 1)
+    def _():
+        xlow[...], xhigh[...] = xnear[...], xfar[...]
+        clow[...], chigh[...] = cnear[...], cfar[...]
+
     def feat_at(x, y, n=1):
         if H <= x < H + N:
             return mfeat[x - H, cell(y, n), :]
@@ -312,11 +336,11 @@
     pown = pown.transpose(1, 2, 0, 3).reshape(Q, Q * C, Z)
 
     face = ((N * H + Q, C, Z), BF)
-    ydown, yup, xdown, xup = call(pack_faces, [face] * 4)(own, pown)
+    ydown, yup, near, far = call(pack_faces, [face] * 4)(own, pown)
     ylow = shift(ydown, "gy", 1)
     yhigh = shift(yup, "gy", -1)
-    xlow = shift(xdown, "gx", 1)
-    xhigh = shift(xup, "gx", -1)
+    xfar = swap(far, "gx", 1)
+    xnear = swap(near, "gx", 0)
 
     def blocks(weight):
         return weight.transpose(1, 2, 3, 0, 4).reshape(27, C, C)
@@ -327,11 +351,12 @@
             bias_one.reshape(1, C), bias_two.reshape(1, C))
 
     own, pown, t1 = lax.optimization_barrier((own, pown, t1))
-    mfeat, mpool, cdown, cup = call(
+    corner = ((N * H + 2, C, Z), BF)
+    mfeat, mpool, near, far = call(
         pack_corners,
-        [((N, W * C, Z), BF), ((Q, (Q + 2) * C, Z), BF)] + [((N * H + 2, C, Z), BF)] * 2)(own, pown, ylow, yhigh)
-    clow = shift(cdown, "gx", 1)
-    chigh = shift(cup, "gx", -1)
+        [((N, W * C, Z), BF), ((Q, (Q + 2) * C, Z), BF)] + [corner] * 2)(own, pown, ylow, yhigh)
+    cfar = swap(far, "gx", 1)
+    cnear = swap(near, "gx", 0)
 
     grads = [((9 * C, 3 * C), F32)] * 2 + [((C, Z), F32)] * 2
     mids = call(
@@ -341,8 +366,8 @@
 
     one, parts = call(
         outer, [((W - 6, (W - 6) * C, Z), BF), ((devices * ROWS, Z), BF)],
-        [((8, (W - 2) * C, Z), BF), ((8, (W - 4) * C, Z), BF),
-         ((4, (Q + 2) * C, 2 * Z), F32)] + grads)(mfeat, mpool, xlow, xhigh, clow, chigh, *mids, mask, t1, t2, f2, b1, b2)
+        [face, face, corner, corner, ((8, (W - 2) * C, Z), BF), ((8, (W - 4) * C, Z), BF),
+         ((4, (Q + 2) * C, 2 * Z), F32)] + grads)(mfeat, mpool, xnear, xfar, cnear, cfar, *mids, mask, t1, t2, f2, b1, b2)
 
     block = (devices, ROWS, Z)
     got = lax.all_to_all(parts.reshape(block), axes, 0, 0, tiled=True)

time: 78.8 us -> 74.1 us (0.940)
  starting transfers between devices: 23 us -> 19.4 us
  blocking collectives: 25.1 us -> 23.7 us
    ppermute x6 -> x2, starting transfers between devices: 18.7 us -> 5.37 us  [shift(): return lax.ppermute(v, axis, pairs)]
    ppermute x0 -> x4, starting transfers between devices: none -> 9.81 us  [swap(): return lax.ppermute(v, axis, pairs)]
    all_to_all x1, blocking collectives: 25.1 us -> 23.7 us  [steps(): got = lax.all_to_all(parts.reshape(block), axes, 0, 0, tiled=True)]
    ppermute x0 -> x4, waiting for transfers between devices: none -> 1.01 us  [swap(): return lax.ppermute(v, axis, pairs)]
    ppermute x6 -> x2, waiting for transfers between devices: 2.56 us -> 1.77 us  [shift(): return lax.ppermute(v, axis, pairs)]
  transfers between devices with their start and end apart: 7 -> 7, of which waited for: 2 -> 3; matrix products, arithmetic and copies ran while one was open for 1% -> 1% of each run, Pallas kernels for 7% -> 8%
where the time goes in v6:
time: 74.1 us; the launch traced here: 73.7 us
  blocking collectives  23.7 us (32%)
  starting transfers between devices  19.4 us (26%)
  Pallas kernels  13.8 us (19%)
  waiting for transfers between devices  11.7 us (16%)
  local copies, waits for them, and re-layouts  2.23 us (3%)
  other arithmetic  2.01 us (3%)
  between operations  0.87 us (1%)
    all_to_all x1, blocking collectives, steps(): got = lax.all_to_all(parts.reshape(block), axes, 0, 0, tiled=True)  23.7 us
    ppermute x4, starting transfers between devices, swap(): return lax.ppermute(v, axis, pairs)  9.81 us
    all_to_all x1, waiting for transfers between devices, steps(): lax.all_to_all(mine, axes, 0, 0, tiled=True).reshape(devices * ROWS, Z)  8.94 us
    pallas_call x1, Pallas kernels, steps(): call(outer, [((W - 6, (W - 6) * C, Z), BF), ((devices * ROWS, Z), BF)], [...  5.89 us
    ppermute x2, starting transfers between devices, shift(): return lax.ppermute(v, axis, pairs)  5.37 us
    all_to_all x1, starting transfers between devices, steps(): lax.all_to_all(mine, axes, 0, 0, tiled=True).reshape(devices * ROWS, Z)  4.25 us
    pallas_call x1, Pallas kernels, steps(): call(middle, [((6, (W - 2) * C, Z), BF), ((4, (W - 4) * C, Z), BF), ((2,...  3.35 us
    ppermute x2, waiting for transfers between devices, shift(): return lax.ppermute(v, axis, pairs)  1.77 us
  transfers between devices with their start and end apart: 7, of which 3 were waited for; matrix products, arithmetic and copies ran while one was open for 1% of the time, Pallas kernels for 8%

profile of v6, /device:TPU:1, one launch (start us, length us, event | category | flops | bytes accessed | tf_op | source)
XLA Modules:
  0.0 73.7 jit_solution(7249645436420174022)
XLA Ops:
  0.6 0.7 fusion
  1.6 1.1 %convert_element_type.23 = bf16[32,4,4,64]{3,2,1,0:T(4,128)(2,1)S(1)} convert(s32[32,4,4,64]{3,2,1,0:T(4,128)} %param.15) | non-fusion elementwise | flops 32768 | bytes 196608 | tf_op jit(solution)/shard_map/convert_element_type | solution.py:335
  2.7 0.2 maximum_bitcast_fusion
  3.0 0.3 copy.16
  3.4 4.1 %collective-permute-start = (bf16[36,32,128]{2,1,0:T(8,128)(2,1)S(1)}, bf16[36,32,128]{2,1,0:T(8,128)(2,1)S(1)}, u32[]{:S(2)}, u32[]{:S(2)}) collective-permute-start(bf16[36,32,128]{2,1,0:T(8,128)(2,1)S(1)} %get-tuple-element.38), channel_id=1, source_target_pairs={{0,1},{1,2},{2,3},{3,4},{4,5},{5,6},{6,7},{8,9},{9,10},{10,11},{11... | collective-permute-start | bytes 884744 | tf_op jit(solution)/shard_map/ppermute | solution.py:32
  7.5 1.3 %collective-permute-start.1 = (bf16[36,32,128]{2,1,0:T(8,128)(2,1)S(1)}, bf16[36,32,128]{2,1,0:T(8,128)(2,1)S(1)}, u32[]{:S(2)}, u32[]{:S(2)}) collective-permute-start(bf16[36,32,128]{2,1,0:T(8,128)(2,1)S(1)} %get-tuple-element.39), channel_id=1, source_target_pairs={{1,0},{2,1},{3,2},{4,3},{5,4},{6,5},{7,6},{9,8},{10,9},{11,10},{12... | collective-permute-start | bytes 884744 | tf_op jit(solution)/shard_map/ppermute | solution.py:32
  8.8 1.0 %collective-permute-start.2 = (bf16[36,32,128]{2,1,0:T(8,128)(2,1)S(1)}, bf16[36,32,128]{2,1,0:T(8,128)(2,1)S(1)}, u32[]{:S(2)}, u32[]{:S(2)}) collective-permute-start(bf16[36,32,128]{2,1,0:T(8,128)(2,1)S(1)} %get-tuple-element.42), channel_id=1, source_target_pairs={{0,8},{8,0},{16,24},{24,16},{32,40},{40,32},{48,56},{56,48},{64,72... | collective-permute-start | bytes 884744 | tf_op jit(solution)/shard_map/ppermute | solution.py:39
  9.8 3.5 %collective-permute-start.3 = (bf16[36,32,128]{2,1,0:T(8,128)(2,1)S(1)}, bf16[36,32,128]{2,1,0:T(8,128)(2,1)S(1)}, u32[]{:S(2)}, u32[]{:S(2)}) collective-permute-start(bf16[36,32,128]{2,1,0:T(8,128)(2,1)S(1)} %get-tuple-element.43), channel_id=1, source_target_pairs={{8,16},{16,8},{24,32},{32,24},{40,48},{48,40},{56,64},{64,56},{72,... | collective-permute-start | bytes 884744 | tf_op jit(solution)/shard_map/ppermute | solution.py:39
  13.3 0.6 copy-done.2
  14.0 1.3 %shard_map.119 = (bf16[192,384]{1,0:T(8,128)(2,1)S(1)}, bf16[192,384]{1,0:T(8,128)(2,1)S(1)}, bf16[192,384]{1,0:T(8,128)(2,1)S(1)}, bf16[192,384]{1,0:T(8,128)(2...) custom-call(bf16[27,32,32]{2,1,0:T(8,128)(2,1)S(1)} %bitcast.39, bf16[27,32,32]{2,1,0:T(8,128)(2,1)S(1)} %bitcast.40, ...), custom_call_target="tpu_custom_call" | custom-call | tf_op jit(solution)/shard_map/pallas_call | solution.py:348
  15.2 1.8 %collective-permute-done.1.yhigh = bf16[36,32,128]{2,1,0:T(8,128)(2,1)S(1)} collective-permute-done((bf16[36,32,128]{2,1,0:T(8,128)(2,1)S(1)}, bf16[36,32,128]{2,1,0:T(8,128)(2,1)S(1)}, u32[]{:S(2)}, u32[]{:S(2)}) %collective-permute-start.1) | collective-permute-done | bytes 294944 | tf_op jit(solution)/shard_map/ppermute | solution.py:32
  17.0 0.1 shard_map.121
  17.1 1.9 %collective-permute-start.4 = (bf16[34,32,128]{2,1,0:T(8,128)(2,1)S(1)}, bf16[34,32,128]{2,1,0:T(8,128)(2,1)S(1)}, u32[]{:S(2)}, u32[]{:S(2)}) collective-permute-start(bf16[34,32,128]{2,1,0:T(8,128)(2,1)S(1)} %get-tuple-element.44), channel_id=1, source_target_pairs={{0,8},{8,0},{16,24},{24,16},{32,40},{40,32},{48,56},{56,48},{64,72... | collective-permute-start | bytes 835592 | tf_op jit(solution)/shard_map/ppermute | solution.py:39
  19.0 3.4 %collective-permute-start.5 = (bf16[34,32,128]{2,1,0:T(8,128)(2,1)S(1)}, bf16[34,32,128]{2,1,0:T(8,128)(2,1)S(1)}, u32[]{:S(2)}, u32[]{:S(2)}) collective-permute-start(bf16[34,32,128]{2,1,0:T(8,128)(2,1)S(1)} %get-tuple-element.45), channel_id=1, source_target_pairs={{8,16},{16,8},{24,32},{32,24},{40,48},{48,40},{56,64},{64,56},{72,... | collective-permute-start | bytes 835592 | tf_op jit(solution)/shard_map/ppermute | solution.py:39
  22.5 3.4 %shard_map.122 = (bf16[6,448,128]{2,1,0:T(8,128)(2,1)S(1)}, bf16[4,384,128]{2,1,0:T(8,128)(2,1)S(1)}, bf16[2,320,128]{2,1,0:T(8,128)(2,1)S(1)}, f32[288,96]{1,0:...) custom-call(bf16[8,512,128]{2,1,0:T(8,128)(2,1)S(1)} %get-tuple-element.40.feat.mfeat, ...), custom_call_target="tpu_custom_call" | custom-call | tf_op jit(solution)/shard_map/pallas_call | solution.py:362
  25.9 1.0 %collective-permute-done.5.cfar = bf16[34,32,128]{2,1,0:T(8,128)(2,1)S(1)} collective-permute-done((bf16[34,32,128]{2,1,0:T(8,128)(2,1)S(1)}, bf16[34,32,128]{2,1,0:T(8,128)(2,1)S(1)}, u32[]{:S(2)}, u32[]{:S(2)}) %collective-permute-start.5) | collective-permute-done | bytes 278560 | tf_op jit(solution)/shard_map/ppermute | solution.py:39
  26.9 5.9 %shard_map.123 = (bf16[10,320,128]{2,1,0:T(8,128)(2,1)S(1)}, bf16[1024,128]{1,0:T(8,128)(2,1)S(1)}) custom-call(bf16[8,512,128]{2,1,0:T(8,128)(2,1)S(1)} %get-tuple-element.40.feat.mfeat, bf16[4,192,128]{2,1,0:T(8,128)(2,1)S(1)} %get-tuple-element.41.pool.mpool, bf16[36,32,128]{2,1,0:T(8,128)(2,1)S(1)} %collective-permute-done.2.xnear, ...), custom_call_target="tpu_custom_call" | custom-call | tf_op jit(solution)/shard_map/pallas_call | solution.py:367
  32.8 23.7 %all_to_all.10.got = bf16[128,8,128]{2,1,0:T(8,128)(2,1)S(1)} all-to-all(bf16[128,8,128]{2,1,0:T(8,128)(2,1)S(1)} %bitcast.38), channel_id=1, replica_groups=mesh['gx'=16,'gy'=8] {'gx','gy'}, dimensions={0} | all-to-all | bytes 524288 | tf_op jit(solution)/shard_map/all_to_all | solution.py:373
  56.5 0.9 %shard_map.125 = bf16[128,8,128]{2,1,0:T(8,128)(2,1)} custom-call(bf16[128,8,128]{2,1,0:T(8,128)(2,1)S(1)} %all_to_all.10.got), custom_call_target="tpu_custom_call" | custom-call | tf_op jit(solution)/shard_map/pallas_call | solution.py:375
  57.3 4.2 %all-to-all-start.1 = ((bf16[128,8,128]{2,1,0:T(8,128)(2,1)}), bf16[128,8,128]{2,1,0:T(8,128)(2,1)S(1)}, u32[]{:S(2)}, u32[]{:S(2)}) async-start(bf16[128,8,128]{2,1,0:T(8,128)(2,1)} %shard_map.125), calls=%async_computation.1 | async-start | bytes 524288 | tf_op jit(solution)/shard_map/all_to_all | solution.py:376
  61.6 1.1 %shard_map.124 = bf16[8,256,128]{2,1,0:T(8,128)(2,1)S(1)} custom-call(bf16[10,320,128]{2,1,0:T(8,128)(2,1)S(1)} %get-tuple-element.58.one, f32[3,8,128]{2,1,0:T(8,128)S(1)} %pad.9.mask, bf16[192,384]{1,0:T(8,128)(2,1)S(1)} %get-tuple-element.59.f1), custom_call_target="tpu_custom_call" | custom-call | tf_op jit(solution)/shard_map/pallas_call | solution.py:374
  62.7 1.0 %copy.20 = bf16[8,8,32,128]{3,1,0,2:T(8,128)(2,1)} copy(bf16[8,8,32,128]{3,2,1,0:T(8,128)(2,1)S(1)} %bitcast.34) | data formatting | bytes 1048576 | tf_op jit(solution)/shard_map/reshape | solution.py:383
  63.7 8.9 %all-to-all-done.1 = bf16[128,8,128]{2,1,0:T(8,128)(2,1)S(1)} async-done(((bf16[128,8,128]{2,1,0:T(8,128)(2,1)}), bf16[128,8,128]{2,1,0:T(8,128)(2,1)S(1)}, u32[]{:S(2)}, u32[]{:S(2)}) %all-to-all-start.1) | async-done | bytes 262176 | tf_op jit(solution)/shard_map/all_to_all | solution.py:376
  72.6 1.1 %shard_map.126 = (f32[27,32,32]{2,1,0:T(8,128)}, f32[27,32,32]{2,1,0:T(8,128)}, f32[1,32]{1,0:T(1,128)}, f32[1,32]{1,0:T(1,128)}) custom-call(bf16[1024,128]{1,0:T(8,128)(2,1)S(1)} %bitcast.37), custom_call_target="tpu_custom_call" | custom-call | tf_op jit(solution)/shard_map/pallas_call | solution.py:377
  (22 shorter events, 0.4 us)
Async XLA Ops:
  1.4 1.2 %copy-start.5 = (bf16[32,4,4,64]{3,2,1,0:T(4,128)(2,1)S(1)}, bf16[32,4,4,64]{3,2,1,0:T(4,128)(2,1)}, u32[]{:S(2)}) copy-start(bf16[32,4,4,64]{3,2,1,0:T(4,128)(2,1)} %param.14) | copy-start | bytes 196612
  1.6 1.3 %copy-start.4 = (bf16[32,8,8,128]{3,2,1,0:T(8,128)(2,1)S(1)}, bf16[32,8,8,128]{3,2,1,0:T(8,128)(2,1)}, u32[]{:S(2)}) copy-start(bf16[32,8,8,128]{3,2,1,0:T(8,128)(2,1)} %param.8) | copy-start | bytes 1572868
  3.3 10.0 %copy-start = (bf16[32,3,3,3,32]{4,0,3,2,1:T(8,128)(2,1)S(1)}, bf16[32,3,3,3,32]{4,0,3,2,1:T(8,128)(2,1)}, u32[]{:S(2)}) copy-start(bf16[32,3,3,3,32]{4,0,3,2,1:T(8,128)(2,1)} %param.10) | copy-start | bytes 165892
  3.3 10.0 %copy-start.1 = (bf16[32,3,3,3,32]{4,0,3,2,1:T(8,128)(2,1)S(1)}, bf16[32,3,3,3,32]{4,0,3,2,1:T(8,128)(2,1)}, u32[]{:S(2)}) copy-start(bf16[32,3,3,3,32]{4,0,3,2,1:T(8,128)(2,1)} %param.12) | copy-start | bytes 165892
  3.4 11.8 %collective-permute-start = (bf16[36,32,128]{2,1,0:T(8,128)(2,1)S(1)}, bf16[36,32,128]{2,1,0:T(8,128)(2,1)S(1)}, u32[]{:S(2)}, u32[]{:S(2)}) collective-permute-start(bf16[36,32,128]{2,1,0:T(8,128)(2,1)S(1)} %get-tuple-element.38), channel_id=1, source_target_pairs={{0,1},{1,2},{2,3},{3,4},{4,5},{5,6},{6,7},{8,9},{9,10},{10,11},{11... | collective-permute-start | bytes 884744 | tf_op jit(solution)/shard_map/ppermute | solution.py:32
  7.5 9.5 %collective-permute-start.1 = (bf16[36,32,128]{2,1,0:T(8,128)(2,1)S(1)}, bf16[36,32,128]{2,1,0:T(8,128)(2,1)S(1)}, u32[]{:S(2)}, u32[]{:S(2)}) collective-permute-start(bf16[36,32,128]{2,1,0:T(8,128)(2,1)S(1)} %get-tuple-element.39), channel_id=1, source_target_pairs={{1,0},{2,1},{3,2},{4,3},{5,4},{6,5},{7,6},{9,8},{10,9},{11,10},{12... | collective-permute-start | bytes 884744 | tf_op jit(solution)/shard_map/ppermute | solution.py:32
  8.8 17.0 %collective-permute-start.2 = (bf16[36,32,128]{2,1,0:T(8,128)(2,1)S(1)}, bf16[36,32,128]{2,1,0:T(8,128)(2,1)S(1)}, u32[]{:S(2)}, u32[]{:S(2)}) collective-permute-start(bf16[36,32,128]{2,1,0:T(8,128)(2,1)S(1)} %get-tuple-element.42), channel_id=1, source_target_pairs={{0,8},{8,0},{16,24},{24,16},{32,40},{40,32},{48,56},{56,48},{64,72... | collective-permute-start | bytes 884744 | tf_op jit(solution)/shard_map/ppermute | solution.py:39
  9.8 16.0 %collective-permute-start.3 = (bf16[36,32,128]{2,1,0:T(8,128)(2,1)S(1)}, bf16[36,32,128]{2,1,0:T(8,128)(2,1)S(1)}, u32[]{:S(2)}, u32[]{:S(2)}) collective-permute-start(bf16[36,32,128]{2,1,0:T(8,128)(2,1)S(1)} %get-tuple-element.43), channel_id=1, source_target_pairs={{8,16},{16,8},{24,32},{32,24},{40,48},{48,40},{56,64},{64,56},{72,... | collective-permute-start | bytes 884744 | tf_op jit(solution)/shard_map/ppermute | solution.py:39
  13.3 0.7 copy-start.2
  13.3 0.7 copy-start.3
  17.1 8.7 %collective-permute-start.4 = (bf16[34,32,128]{2,1,0:T(8,128)(2,1)S(1)}, bf16[34,32,128]{2,1,0:T(8,128)(2,1)S(1)}, u32[]{:S(2)}, u32[]{:S(2)}) collective-permute-start(bf16[34,32,128]{2,1,0:T(8,128)(2,1)S(1)} %get-tuple-element.44), channel_id=1, source_target_pairs={{0,8},{8,0},{16,24},{24,16},{32,40},{40,32},{48,56},{56,48},{64,72... | collective-permute-start | bytes 835592 | tf_op jit(solution)/shard_map/ppermute | solution.py:39
  19.0 7.9 %collective-permute-start.5 = (bf16[34,32,128]{2,1,0:T(8,128)(2,1)S(1)}, bf16[34,32,128]{2,1,0:T(8,128)(2,1)S(1)}, u32[]{:S(2)}, u32[]{:S(2)}) collective-permute-start(bf16[34,32,128]{2,1,0:T(8,128)(2,1)S(1)} %get-tuple-element.45), channel_id=1, source_target_pairs={{8,16},{16,8},{24,32},{32,24},{40,48},{48,40},{56,64},{64,56},{72,... | collective-permute-start | bytes 835592 | tf_op jit(solution)/shard_map/ppermute | solution.py:39
  57.3 15.3 %all-to-all-start.1 = ((bf16[128,8,128]{2,1,0:T(8,128)(2,1)}), bf16[128,8,128]{2,1,0:T(8,128)(2,1)S(1)}, u32[]{:S(2)}, u32[]{:S(2)}) async-start(bf16[128,8,128]{2,1,0:T(8,128)(2,1)} %shard_map.125), calls=%async_computation.1 | async-start | bytes 524288 | tf_op jit(solution)/shard_map/all_to_all | solution.py:376

commit v7 on v6

--- a/solution.py
+++ b/solution.py
@@ -124,8 +124,8 @@
     return jnp.where(row == col // 2, 1.0, 0.0).astype(BF)
 
 
-def conv_pair(rows_at, x, weight, width, write, i):
-    for j in range(width // 2):
+def conv_pair(rows_at, x, weight, pairs, write, i):
+    for j in pairs:
         rows = [rows_at(x + d, 2 * j, 4) for d in range(4)]
         tile = jnp.concatenate(
             [jnp.concatenate([rows[d], rows[d + 1]], axis=1) for d in range(3)], axis=0)
@@ -184,14 +184,14 @@
     return ups_at
 
 
-def term(x, bias, src_at, off_s, delta_at, off_d, acc):
+def term(x, ys, bias, src_at, off_s, delta_at, off_d, acc):
     rights = []
-    for y in range(N):
+    for y in ys:
         d = delta_at(x + off_d, y + off_d).astype(F32)
         bias[...] += d
         rights.append(jnp.concatenate([before(d), d, after(d)], axis=0).astype(BF))
     left = jnp.concatenate(
-        [jnp.concatenate([src_at(x + off_s + a, y + off_s, 3) for y in range(N)], axis=1)
+        [jnp.concatenate([src_at(x + off_s + a, y + off_s, 3) for y in ys], axis=1)
          for a in range(3)], axis=0)
     acc[...] += lax.dot_general(left, jnp.concatenate(rights, axis=1), (((1,), (1,)), ((), ())),
                                 preferred_element_type=F32)
@@ -209,30 +209,35 @@
     for ref in (acc1, acc2, s1, s2):
         ref[...] = jnp.zeros_like(ref)
     for i in (2, 3, 4):
-        conv_pair(feat_at, 2 * i, t1, W - 2, write_hidden, i)
+        conv_pair(feat_at, 2 * i, t1, range(W // 2 - 1), write_hidden, i)
     for i in (2, 3):
-        conv_pair(hid_at, 2 * i, t2, W - 4, write_two, i)
-    conv_pair(two_at, 4, f2, W - 6, write_one, 2)
+        conv_pair(hid_at, 2 * i, t2, range(W // 2 - 2), write_two, i)
+    conv_pair(two_at, 4, f2, range(W // 2 - 3), write_one, 2)
     for x in range(2, 6):
-        term(x, s2, hid_at, H - 2, two_at, H - 2, acc2)
+        term(x, range(N), s2, hid_at, H - 2, two_at, H - 2, acc2)
     for x in range(3, 5):
-        term(x, s1, feat_at, H - 1, one_at, H - 3, acc1)
-
-
-def outer(mfeat, mpool, xnear, xfar, cnear, cfar, mhid, mtwo, mone, macc1, macc2, ms1, ms2, mask,
-          t1, t2, f2, b1, b2, one, parts, xlow, xhigh, clow, chigh, hid, two, ups, acc1, acc2, s1, s2):
-    odd = odd_place()
-
-    @pl.when(odd == 0)
-    def _():
-        xlow[...], xhigh[...] = xfar[...], xnear[...]
-        clow[...], chigh[...] = cfar[...], cnear[...]
-
-    @pl.when(odd == 1)
-    def _():
-        xlow[...], xhigh[...] = xnear[...], xfar[...]
-        clow[...], chigh[...] = cnear[...], cfar[...]
-
+        term(x, range(N), s1, feat_at, H - 1, one_at, H - 3, acc1)
+
+
+def packed(x, mid):
+    return x if x < 4 else x - mid
+
+
+def merged(ref, full, mid, inner=None, count=0):
+    def one_cell(p, y):
+        if 4 <= y < 4 + count:
+            return inner[p, cell(y - 4), :]
+        return ref[p, cell(y), :]
+
+    def rows_at(x, y, n=1):
+        if 4 <= x < 4 + mid:
+            return full[x - 4, cell(y, n), :]
+        return jnp.concatenate([one_cell(packed(x, mid), v) for v in range(y, y + n)], axis=0)
+
+    return rows_at
+
+
+def features_at(mfeat, xlow, xhigh, clow, chigh):
     def feat_at(x, y, n=1):
         if H <= x < H + N:
             return mfeat[x - H, cell(y, n), :]
@@ -245,6 +250,63 @@
                 cells.append(corner[k * N + (v if v < H else v - N)])
         return jnp.concatenate(cells, axis=0)
 
+    return feat_at
+
+
+def resolve(near, far, low, high):
+    odd = odd_place()
+
+    @pl.when(odd == 0)
+    def _():
+        low[...], high[...] = far[...], near[...]
+
+    @pl.when(odd == 1)
+    def _():
+        low[...], high[...] = near[...], far[...]
+
+
+def rim(mfeat, mpool, xnear, xfar, mhid, mtwo, mone, macc1, macc2, ms1, ms2, mask,
+        t1, t2, f2, b1, b2, xlow, xhigh, hid, two, one, acc1, acc2, s1, s2, ups):
+    resolve(xnear, xfar, xlow, xhigh)
+    spread = spreader()
+    for row, side in ((0, xlow), (3, xhigh)):
+        for y in range(2, Q):
+            ups[row, cell(y), :] = jnp.dot(
+                side[N * H + y - 1], spread, preferred_element_type=F32)
+    ups[1] = jnp.dot(mpool[0], spread, preferred_element_type=F32)
+    ups[2] = jnp.dot(mpool[Q - 1], spread, preferred_element_type=F32)
+
+    def inner_put(ref, mid):
+        def put(x, y, v):
+            ref[packed(x, mid), cell(y - 4), :] = v
+
+        return put
+
+    feat_at = features_at(mfeat, xlow, xhigh, None, None)
+    hid_at = merged(None, mhid, 6, hid, 6)
+    two_at = merged(None, mtwo, 4, two, 4)
+    one_at = merged(None, mone, 2, one, 2)
+    write_hidden, write_two, write_one = writers(
+        mask, b1, b2, upstream(ups, lambda i: packed(i, 2) if i > 3 else i), hid_at,
+        inner_put(hid, 6), inner_put(two, 4), inner_put(one, 2))
+    for dst, src in ((acc1, macc1), (acc2, macc2), (s1, ms1), (s2, ms2)):
+        dst[...] = src[...]
+    for i in (0, 1, 5, 6):
+        conv_pair(feat_at, 2 * i, t1, (2, 3, 4), write_hidden, i)
+    for i in (0, 1, 4, 5):
+        conv_pair(hid_at, 2 * i, t2, (2, 3), write_two, i)
+    for i in (0, 1, 3, 4):
+        conv_pair(two_at, 2 * i, f2, (2,), write_one, i)
+    for x in (0, 1, 6, 7):
+        term(x, (2, 3, 4, 5), s2, hid_at, H - 2, two_at, H - 2, acc2)
+    for x in (0, 1, 2, 5, 6, 7):
+        term(x, (3, 4), s1, feat_at, H - 1, one_at, H - 3, acc1)
+
+
+def outer(mfeat, mpool, cnear, cfar, mhid, mtwo, mone, xlow, xhigh, rhid, rtwo, rone,
+          macc1, macc2, ms1, ms2, mask, t1, t2, f2, b1, b2, one, parts,
+          clow, chigh, hid, two, ups, acc1, acc2, s1, s2):
+    resolve(cnear, cfar, clow, chigh)
     spread = spreader()
     for row, side, corner in ((0, xlow, clow), (3, xhigh, chigh)):
         for y in range(Q + 2):
@@ -256,36 +318,35 @@
     ups[1] = jnp.dot(mpool[0], spread, preferred_element_type=F32)
     ups[2] = jnp.dot(mpool[Q - 1], spread, preferred_element_type=F32)
 
-    def merged(ref, mid, count):
-        def rows_at(x, y, n=1):
-            if 4 <= x < 4 + count:
-                return mid[x - 4, cell(y, n), :]
-            return ref[x if x < 4 else x - count, cell(y, n), :]
-
-        return rows_at
-
-    hid_at, two_at = merged(hid, mhid, 6), merged(two, mtwo, 4)
+    def rim_put(ref, mid):
+        return putter(ref, lambda x: packed(x, mid))
+
+    feat_at = features_at(mfeat, xlow, xhigh, clow, chigh)
+    hid_at = merged(hid, mhid, 6, rhid, 6)
+    two_at = merged(two, mtwo, 4, rtwo, 4)
     one_at = planes(one)
-    for x in range(2):
-        one[4 + x] = mone[x]
+    for x in range(10):
+        if 4 <= x < 6:
+            one[x] = mone[x - 4]
+        else:
+            one[x, cell(4, 2), :] = rone[packed(x, 2)]
     write_hidden, write_two, write_one = writers(
-        mask, b1, b2, upstream(ups, lambda i: i if i < 2 else i - 2), hid_at,
-        putter(hid, lambda x: x if x < 4 else x - 6),
-        putter(two, lambda x: x if x < 4 else x - 4), putter(one, lambda x: x))
+        mask, b1, b2, upstream(ups, lambda i: packed(i, 2) if i > 3 else i), hid_at,
+        rim_put(hid, 6), rim_put(two, 4), putter(one, lambda x: x))
     acc1[...] = macc1[...]
     acc2[...] = macc2[...]
     s1[...] = ms1[...]
     s2[...] = ms2[...]
     for i in (0, 1, 5, 6):
-        conv_pair(feat_at, 2 * i, t1, W - 2, write_hidden, i)
+        conv_pair(feat_at, 2 * i, t1, (0, 1, 5, 6), write_hidden, i)
     for i in (0, 1, 4, 5):
-        conv_pair(hid_at, 2 * i, t2, W - 4, write_two, i)
+        conv_pair(hid_at, 2 * i, t2, (0, 1, 4, 5), write_two, i)
     for i in (0, 1, 3, 4):
-        conv_pair(two_at, 2 * i, f2, W - 6, write_one, i)
+        conv_pair(two_at, 2 * i, f2, (0, 1, 3, 4), write_one, i)
     for x in (0, 1, 6, 7):
-        term(x, s2, hid_at, H - 2, two_at, H - 2, acc2)
+        term(x, (0, 1, 6, 7), s2, hid_at, H - 2, two_at, H - 2, acc2)
     for x in (0, 1, 2, 5, 6, 7):
-        term(x, s1, feat_at, H - 1, one_at, H - 3, acc1)
+        term(x, (0, 1, 2, 5, 6, 7), s1, feat_at, H - 1, one_at, H - 3, acc1)
     rows9 = 9 * C
     pad = jnp.zeros((rows9, Z - 3 * C), F32)
     for k, (acc, sums) in enumerate(((acc1, s1), (acc2, s2))):
@@ -320,7 +381,7 @@
         out[2 * i + xo, cell(2 * j + yo), :] = (v * mask[1][1:2, :]).astype(BF)
 
     for i in range(N // 2):
-        conv_pair(planes(one), 2 * i, f1, N, write_out, i)
+        conv_pair(planes(one), 2 * i, f1, range(N // 2), write_out, i)
 
 
 def steps(features, occupancy, weight_one, bias_one, weight_two, bias_two, grad_pooled, pool_choice):
@@ -364,10 +425,15 @@
         [((6, (W - 2) * C, Z), BF), ((4, (W - 4) * C, Z), BF), ((2, (W - 6) * C, Z), BF)] + grads,
         [((2, (Q + 2) * C, 2 * Z), F32)])(mfeat, mpool, mask, t1, t2, f2, b1, b2)
 
+    rims = call(
+        rim,
+        [face, face, ((8, 6 * C, Z), BF), ((8, 4 * C, Z), BF), ((8, 2 * C, Z), BF)] + grads,
+        [((4, (Q + 2) * C, 2 * Z), F32)])(mfeat, mpool, xnear, xfar, *mids, mask, t1, t2, f2, b1, b2)
+
     one, parts = call(
         outer, [((W - 6, (W - 6) * C, Z), BF), ((devices * ROWS, Z), BF)],
-        [face, face, corner, corner, ((8, (W - 2) * C, Z), BF), ((8, (W - 4) * C, Z), BF),
-         ((4, (Q + 2) * C, 2 * Z), F32)] + grads)(mfeat, mpool, xnear, xfar, cnear, cfar, *mids, mask, t1, t2, f2, b1, b2)
+        [corner, corner, ((8, (W - 2) * C, Z), BF), ((8, (W - 4) * C, Z), BF),
+         ((4, (Q + 2) * C, 2 * Z), F32)] + grads)(mfeat, mpool, cnear, cfar, *mids[:3], *rims, mask, t1, t2, f2, b1, b2)
 
     block = (devices, ROWS, Z)
     got = lax.all_to_all(parts.reshape(block), axes, 0, 0, tiled=True)

time: 74.1 us -> 72.2 us (0.974)
  blocking collectives: 23.7 us -> 22.4 us
  waiting for transfers between devices: 11.7 us -> 10.7 us
    pallas_call x0 -> x1, Pallas kernels: none -> 2.31 us  [steps(): call(rim, [face, face, ((8, 6 * C, Z), BF), ((8, 4 * C, Z), BF), ((8, 2 *...]
    pallas_call x1, Pallas kernels: 5.89 us -> 4.04 us  [steps(): call(outer, [((W - 6, (W - 6) * C, Z), BF), ((devices * ROWS, Z), BF)], [...]
    all_to_all x1, blocking collectives: 23.7 us -> 22.4 us  [steps(): got = lax.all_to_all(parts.reshape(block), axes, 0, 0, tiled=True)]
    ppermute x4, waiting for transfers between devices: 1.01 us -> 0.01 us  [swap(): return lax.ppermute(v, axis, pairs)]
  transfers between devices with their start and end apart: 7 -> 7, of which waited for: 3 -> 2; matrix products, arithmetic and copies ran while one was open for 1% -> 1% of each run, Pallas kernels for 8% -> 11%
where the time goes in v7:
time: 72.2 us; the launch traced here: 71.9 us
  blocking collectives  22.4 us (31%)
  starting transfers between devices  19.4 us (27%)
  Pallas kernels  14.2 us (20%)
  waiting for transfers between devices  10.7 us (15%)
  local copies, waits for them, and re-layouts  2.23 us (3%)
  other arithmetic  2.01 us (3%)
  between operations  0.88 us (1%)
    all_to_all x1, blocking collectives, steps(): got = lax.all_to_all(parts.reshape(block), axes, 0, 0, tiled=True)  22.4 us
    ppermute x4, starting transfers between devices, swap(): return lax.ppermute(v, axis, pairs)  9.81 us
    all_to_all x1, waiting for transfers between devices, steps(): lax.all_to_all(mine, axes, 0, 0, tiled=True).reshape(devices * ROWS, Z)  8.94 us
    ppermute x2, starting transfers between devices, shift(): return lax.ppermute(v, axis, pairs)  5.37 us
    all_to_all x1, starting transfers between devices, steps(): lax.all_to_all(mine, axes, 0, 0, tiled=True).reshape(devices * ROWS, Z)  4.25 us
    pallas_call x1, Pallas kernels, steps(): call(outer, [((W - 6, (W - 6) * C, Z), BF), ((devices * ROWS, Z), BF)], [...  4.04 us
    pallas_call x1, Pallas kernels, steps(): call(middle, [((6, (W - 2) * C, Z), BF), ((4, (W - 4) * C, Z), BF), ((2,...  3.33 us
    pallas_call x1, Pallas kernels, steps(): call(rim, [face, face, ((8, 6 * C, Z), BF), ((8, 4 * C, Z), BF), ((8, 2 *...  2.31 us
  transfers between devices with their start and end apart: 7, of which 2 were waited for; matrix products, arithmetic and copies ran while one was open for 1% of the time, Pallas kernels for 11%

profile of v7, /device:TPU:1, one launch (start us, length us, event | category | flops | bytes accessed | tf_op | source)
XLA Modules:
  0.0 71.9 jit_solution(1473189768310308470)
XLA Ops:
  0.6 0.7 %fusion = f32[3,3,16]{2,1,0:T(4,128)S(1)} fusion(s32[]{:T(128)S(6)} %select_n.6, s32[]{:T(128)S(6)} %select_n.7, s32[16,8,16]{2,1,0:T(8,128)} %param.9), kind=kLoop, calls=%fused_computation.4 | loop fusion | flops 144 | bytes 8776 | tf_op jit(solution)/shard_map/convert_element_type | solution.py:393
  1.6 1.1 %convert_element_type.23 = bf16[32,4,4,64]{3,2,1,0:T(4,128)(2,1)S(1)} convert(s32[32,4,4,64]{3,2,1,0:T(4,128)} %param.15) | non-fusion elementwise | flops 32768 | bytes 196608 | tf_op jit(solution)/shard_map/convert_element_type | solution.py:396
  2.7 0.2 maximum_bitcast_fusion
  3.0 0.3 copy.16
  3.4 4.1 %collective-permute-start = (bf16[36,32,128]{2,1,0:T(8,128)(2,1)S(1)}, bf16[36,32,128]{2,1,0:T(8,128)(2,1)S(1)}, u32[]{:S(2)}, u32[]{:S(2)}) collective-permute-start(bf16[36,32,128]{2,1,0:T(8,128)(2,1)S(1)} %get-tuple-element.47), channel_id=1, source_target_pairs={{0,1},{1,2},{2,3},{3,4},{4,5},{5,6},{6,7},{8,9},{9,10},{10,11},{11... | collective-permute-start | bytes 884744 | tf_op jit(solution)/shard_map/ppermute | solution.py:32
  7.5 1.3 %collective-permute-start.1 = (bf16[36,32,128]{2,1,0:T(8,128)(2,1)S(1)}, bf16[36,32,128]{2,1,0:T(8,128)(2,1)S(1)}, u32[]{:S(2)}, u32[]{:S(2)}) collective-permute-start(bf16[36,32,128]{2,1,0:T(8,128)(2,1)S(1)} %get-tuple-element.48), channel_id=1, source_target_pairs={{1,0},{2,1},{3,2},{4,3},{5,4},{6,5},{7,6},{9,8},{10,9},{11,10},{12... | collective-permute-start | bytes 884744 | tf_op jit(solution)/shard_map/ppermute | solution.py:32
  8.8 1.0 %collective-permute-start.4 = (bf16[36,32,128]{2,1,0:T(8,128)(2,1)S(1)}, bf16[36,32,128]{2,1,0:T(8,128)(2,1)S(1)}, u32[]{:S(2)}, u32[]{:S(2)}) collective-permute-start(bf16[36,32,128]{2,1,0:T(8,128)(2,1)S(1)} %get-tuple-element.61), channel_id=1, source_target_pairs={{0,8},{8,0},{16,24},{24,16},{32,40},{40,32},{48,56},{56,48},{64,72... | collective-permute-start | bytes 884744 | tf_op jit(solution)/shard_map/ppermute | solution.py:39
  9.8 3.5 %collective-permute-start.5 = (bf16[36,32,128]{2,1,0:T(8,128)(2,1)S(1)}, bf16[36,32,128]{2,1,0:T(8,128)(2,1)S(1)}, u32[]{:S(2)}, u32[]{:S(2)}) collective-permute-start(bf16[36,32,128]{2,1,0:T(8,128)(2,1)S(1)} %get-tuple-element.62), channel_id=1, source_target_pairs={{8,16},{16,8},{24,32},{32,24},{40,48},{48,40},{56,64},{64,56},{72,... | collective-permute-start | bytes 884744 | tf_op jit(solution)/shard_map/ppermute | solution.py:39
  13.3 0.6 copy-done.2
  14.0 1.3 %shard_map.119 = (bf16[192,384]{1,0:T(8,128)(2,1)S(1)}, bf16[192,384]{1,0:T(8,128)(2,1)S(1)}, bf16[192,384]{1,0:T(8,128)(2,1)S(1)}, bf16[192,384]{1,0:T(8,128)(2...) custom-call(bf16[27,32,32]{2,1,0:T(8,128)(2,1)S(1)} %bitcast.39, bf16[27,32,32]{2,1,0:T(8,128)(2,1)S(1)} %bitcast.40, ...), custom_call_target="tpu_custom_call" | custom-call | tf_op jit(solution)/shard_map/pallas_call | solution.py:409
  15.2 1.8 %collective-permute-done.1.yhigh = bf16[36,32,128]{2,1,0:T(8,128)(2,1)S(1)} collective-permute-done((bf16[36,32,128]{2,1,0:T(8,128)(2,1)S(1)}, bf16[36,32,128]{2,1,0:T(8,128)(2,1)S(1)}, u32[]{:S(2)}, u32[]{:S(2)}) %collective-permute-start.1) | collective-permute-done | bytes 294944 | tf_op jit(solution)/shard_map/ppermute | solution.py:32
  17.0 0.1 shard_map.121
  17.1 1.9 %collective-permute-start.2 = (bf16[34,32,128]{2,1,0:T(8,128)(2,1)S(1)}, bf16[34,32,128]{2,1,0:T(8,128)(2,1)S(1)}, u32[]{:S(2)}, u32[]{:S(2)}) collective-permute-start(bf16[34,32,128]{2,1,0:T(8,128)(2,1)S(1)} %get-tuple-element.51), channel_id=1, source_target_pairs={{0,8},{8,0},{16,24},{24,16},{32,40},{40,32},{48,56},{56,48},{64,72... | collective-permute-start | bytes 835592 | tf_op jit(solution)/shard_map/ppermute | solution.py:39
  19.0 3.4 %collective-permute-start.3 = (bf16[34,32,128]{2,1,0:T(8,128)(2,1)S(1)}, bf16[34,32,128]{2,1,0:T(8,128)(2,1)S(1)}, u32[]{:S(2)}, u32[]{:S(2)}) collective-permute-start(bf16[34,32,128]{2,1,0:T(8,128)(2,1)S(1)} %get-tuple-element.52), channel_id=1, source_target_pairs={{8,16},{16,8},{24,32},{32,24},{40,48},{48,40},{56,64},{64,56},{72,... | collective-permute-start | bytes 835592 | tf_op jit(solution)/shard_map/ppermute | solution.py:39
  22.5 3.3 %shard_map.122 = (bf16[6,448,128]{2,1,0:T(8,128)(2,1)S(1)}, bf16[4,384,128]{2,1,0:T(8,128)(2,1)S(1)}, bf16[2,320,128]{2,1,0:T(8,128)(2,1)S(1)}, f32[288,96]{1,0:...) custom-call(bf16[8,512,128]{2,1,0:T(8,128)(2,1)S(1)} %get-tuple-element.49.feat.mfeat, ...), custom_call_target="tpu_custom_call" | custom-call | tf_op jit(solution)/shard_map/pallas_call | solution.py:423
  25.8 2.3 %shard_map.123 = (bf16[36,32,128]{2,1,0:T(8,128)(2,1)S(1)}, bf16[36,32,128]{2,1,0:T(8,128)(2,1)S(1)}, bf16[8,192,128]{2,1,0:T(8,128)(2,1)S(1)}, bf16[8,128,128]{...) custom-call(bf16[8,512,128]{2,1,0:T(8,128)(2,1)S(1)} %get-tuple-elem, ...), custom_call_target="tpu_custom_call" | custom-call | tf_op jit(solution)/shard_map/pallas_call | solution.py:428
  28.2 4.0 %shard_map.124 = (bf16[10,320,128]{2,1,0:T(8,128)(2,1)S(1)}, bf16[1024,128]{1,0:T(8,128)(2,1)S(1)}) custom-call(bf16[8,512,128]{2,1,0:T(8,128)(2,1)S(1)} %get-tuple-element.49.feat.mfeat, bf16[4,192,128]{2,1,0:T(8,128)(2,1)S(1)} %get-tuple-element.50.pool.mpool, bf16[34,32,128]{2,1,0:T(8,128)(2,1)S(1)} %collective-permute-done.2.cnear, ...), custom_call_target="tpu_custom_call" | custom-call | tf_op jit(solution)/shard_map/pallas_call | solution.py:433
  32.2 22.4 %all_to_all.10.got = bf16[128,8,128]{2,1,0:T(8,128)(2,1)S(1)} all-to-all(bf16[128,8,128]{2,1,0:T(8,128)(2,1)S(1)} %bitcast.38), channel_id=1, replica_groups=mesh['gx'=16,'gy'=8] {'gx','gy'}, dimensions={0} | all-to-all | bytes 524288 | tf_op jit(solution)/shard_map/all_to_all | solution.py:439
  54.6 0.9 %shard_map.126 = bf16[128,8,128]{2,1,0:T(8,128)(2,1)} custom-call(bf16[128,8,128]{2,1,0:T(8,128)(2,1)S(1)} %all_to_all.10.got), custom_call_target="tpu_custom_call" | custom-call | tf_op jit(solution)/shard_map/pallas_call | solution.py:441
  55.5 4.2 %all-to-all-start.1 = ((bf16[128,8,128]{2,1,0:T(8,128)(2,1)}), bf16[128,8,128]{2,1,0:T(8,128)(2,1)S(1)}, u32[]{:S(2)}, u32[]{:S(2)}) async-start(bf16[128,8,128]{2,1,0:T(8,128)(2,1)} %shard_map.126), calls=%async_computation.1 | async-start | bytes 524288 | tf_op jit(solution)/shard_map/all_to_all | solution.py:442
  59.7 1.1 %shard_map.125 = bf16[8,256,128]{2,1,0:T(8,128)(2,1)S(1)} custom-call(bf16[10,320,128]{2,1,0:T(8,128)(2,1)S(1)} %get-tuple-element.76.one, f32[3,8,128]{2,1,0:T(8,128)S(1)} %pad.9.mask, bf16[192,384]{1,0:T(8,128)(2,1)S(1)} %get-tuple-element.77.f1), custom_call_target="tpu_custom_call" | custom-call | tf_op jit(solution)/shard_map/pallas_call | solution.py:440
  60.8 1.0 %copy.20 = bf16[8,8,32,128]{3,1,0,2:T(8,128)(2,1)} copy(bf16[8,8,32,128]{3,2,1,0:T(8,128)(2,1)S(1)} %bitcast.34) | data formatting | bytes 1048576 | tf_op jit(solution)/shard_map/reshape | solution.py:449
  61.8 8.9 %all-to-all-done.1 = bf16[128,8,128]{2,1,0:T(8,128)(2,1)S(1)} async-done(((bf16[128,8,128]{2,1,0:T(8,128)(2,1)}), bf16[128,8,128]{2,1,0:T(8,128)(2,1)S(1)}, u32[]{:S(2)}, u32[]{:S(2)}) %all-to-all-start.1) | async-done | bytes 262176 | tf_op jit(solution)/shard_map/all_to_all | solution.py:442
  70.7 1.1 %shard_map.127 = (f32[27,32,32]{2,1,0:T(8,128)}, f32[27,32,32]{2,1,0:T(8,128)}, f32[1,32]{1,0:T(1,128)}, f32[1,32]{1,0:T(1,128)}) custom-call(bf16[1024,128]{1,0:T(8,128)(2,1)S(1)} %bitcast.37), custom_call_target="tpu_custom_call" | custom-call | tf_op jit(solution)/shard_map/pallas_call | solution.py:443
  (23 shorter events, 0.4 us)
Async XLA Ops:
  1.4 1.2 %copy-start.5 = (bf16[32,4,4,64]{3,2,1,0:T(4,128)(2,1)S(1)}, bf16[32,4,4,64]{3,2,1,0:T(4,128)(2,1)}, u32[]{:S(2)}) copy-start(bf16[32,4,4,64]{3,2,1,0:T(4,128)(2,1)} %param.14) | copy-start | bytes 196612
  1.6 1.3 %copy-start.4 = (bf16[32,8,8,128]{3,2,1,0:T(8,128)(2,1)S(1)}, bf16[32,8,8,128]{3,2,1,0:T(8,128)(2,1)}, u32[]{:S(2)}) copy-start(bf16[32,8,8,128]{3,2,1,0:T(8,128)(2,1)} %param.8) | copy-start | bytes 1572868
  3.3 10.0 %copy-start = (bf16[32,3,3,3,32]{4,0,3,2,1:T(8,128)(2,1)S(1)}, bf16[32,3,3,3,32]{4,0,3,2,1:T(8,128)(2,1)}, u32[]{:S(2)}) copy-start(bf16[32,3,3,3,32]{4,0,3,2,1:T(8,128)(2,1)} %param.10) | copy-start | bytes 165892
  3.3 10.0 %copy-start.1 = (bf16[32,3,3,3,32]{4,0,3,2,1:T(8,128)(2,1)S(1)}, bf16[32,3,3,3,32]{4,0,3,2,1:T(8,128)(2,1)}, u32[]{:S(2)}) copy-start(bf16[32,3,3,3,32]{4,0,3,2,1:T(8,128)(2,1)} %param.12) | copy-start | bytes 165892
  3.4 11.8 %collective-permute-start = (bf16[36,32,128]{2,1,0:T(8,128)(2,1)S(1)}, bf16[36,32,128]{2,1,0:T(8,128)(2,1)S(1)}, u32[]{:S(2)}, u32[]{:S(2)}) collective-permute-start(bf16[36,32,128]{2,1,0:T(8,128)(2,1)S(1)} %get-tuple-element.47), channel_id=1, source_target_pairs={{0,1},{1,2},{2,3},{3,4},{4,5},{5,6},{6,7},{8,9},{9,10},{10,11},{11... | collective-permute-start | bytes 884744 | tf_op jit(solution)/shard_map/ppermute | solution.py:32
  7.5 9.5 %collective-permute-start.1 = (bf16[36,32,128]{2,1,0:T(8,128)(2,1)S(1)}, bf16[36,32,128]{2,1,0:T(8,128)(2,1)S(1)}, u32[]{:S(2)}, u32[]{:S(2)}) collective-permute-start(bf16[36,32,128]{2,1,0:T(8,128)(2,1)S(1)} %get-tuple-element.48), channel_id=1, source_target_pairs={{1,0},{2,1},{3,2},{4,3},{5,4},{6,5},{7,6},{9,8},{10,9},{11,10},{12... | collective-permute-start | bytes 884744 | tf_op jit(solution)/shard_map/ppermute | solution.py:32
  8.8 17.0 %collective-permute-start.4 = (bf16[36,32,128]{2,1,0:T(8,128)(2,1)S(1)}, bf16[36,32,128]{2,1,0:T(8,128)(2,1)S(1)}, u32[]{:S(2)}, u32[]{:S(2)}) collective-permute-start(bf16[36,32,128]{2,1,0:T(8,128)(2,1)S(1)} %get-tuple-element.61), channel_id=1, source_target_pairs={{0,8},{8,0},{16,24},{24,16},{32,40},{40,32},{48,56},{56,48},{64,72... | collective-permute-start | bytes 884744 | tf_op jit(solution)/shard_map/ppermute | solution.py:39
  9.8 16.0 %collective-permute-start.5 = (bf16[36,32,128]{2,1,0:T(8,128)(2,1)S(1)}, bf16[36,32,128]{2,1,0:T(8,128)(2,1)S(1)}, u32[]{:S(2)}, u32[]{:S(2)}) collective-permute-start(bf16[36,32,128]{2,1,0:T(8,128)(2,1)S(1)} %get-tuple-element.62), channel_id=1, source_target_pairs={{8,16},{16,8},{24,32},{32,24},{40,48},{48,40},{56,64},{64,56},{72,... | collective-permute-start | bytes 884744 | tf_op jit(solution)/shard_map/ppermute | solution.py:39
  13.3 0.7 copy-start.2
  13.3 0.7 copy-start.3
  17.1 11.0 %collective-permute-start.2 = (bf16[34,32,128]{2,1,0:T(8,128)(2,1)S(1)}, bf16[34,32,128]{2,1,0:T(8,128)(2,1)S(1)}, u32[]{:S(2)}, u32[]{:S(2)}) collective-permute-start(bf16[34,32,128]{2,1,0:T(8,128)(2,1)S(1)} %get-tuple-element.51), channel_id=1, source_target_pairs={{0,8},{8,0},{16,24},{24,16},{32,40},{40,32},{48,56},{56,48},{64,72... | collective-permute-start | bytes 835592 | tf_op jit(solution)/shard_map/ppermute | solution.py:39
  19.0 9.1 %collective-permute-start.3 = (bf16[34,32,128]{2,1,0:T(8,128)(2,1)S(1)}, bf16[34,32,128]{2,1,0:T(8,128)(2,1)S(1)}, u32[]{:S(2)}, u32[]{:S(2)}) collective-permute-start(bf16[34,32,128]{2,1,0:T(8,128)(2,1)S(1)} %get-tuple-element.52), channel_id=1, source_target_pairs={{8,16},{16,8},{24,32},{32,24},{40,48},{48,40},{56,64},{64,56},{72,... | collective-permute-start | bytes 835592 | tf_op jit(solution)/shard_map/ppermute | solution.py:39
  55.5 15.3 %all-to-all-start.1 = ((bf16[128,8,128]{2,1,0:T(8,128)(2,1)}), bf16[128,8,128]{2,1,0:T(8,128)(2,1)S(1)}, u32[]{:S(2)}, u32[]{:S(2)}) async-start(bf16[128,8,128]{2,1,0:T(8,128)(2,1)} %shard_map.126), calls=%async_computation.1 | async-start | bytes 524288 | tf_op jit(solution)/shard_map/all_to_all | solution.py:442

commit v8 on v7

--- a/solution.py
+++ b/solution.py
@@ -26,12 +26,6 @@
     )
 
 
-def shift(v, axis, step):
-    devices = lax.axis_size(axis)
-    pairs = [(i, i + step) for i in range(devices) if 0 <= i + step < devices]
-    return lax.ppermute(v, axis, pairs)
-
-
 def swap(v, axis, first):
     pairs = []
     for i in range(first, lax.axis_size(axis) - 1, 2):
@@ -39,8 +33,8 @@
     return lax.ppermute(v, axis, pairs)
 
 
-def odd_place():
-    return lax.axis_index("gx") % 2
+def odd_place(axis="gx"):
+    return lax.axis_index(axis) % 2
 
 
 def cell(y, n=1):
@@ -69,15 +63,51 @@
         dst[...] = jnp.transpose(jnp.broadcast_to(src[...], (Z, C)))
 
 
-def pack_faces(own, pown, ylow, yhigh, near, far):
+def flags_around(occ, x, y):
+    nx, ny, nz = occ.shape
+    row = lax.broadcasted_iota(jnp.int32, (8, ny), 0)
+    col = lax.broadcasted_iota(jnp.int32, (8, ny), 1)
+    brick = lax.broadcasted_iota(jnp.int32, (nz, Z), 0)
+    lane = lax.broadcasted_iota(jnp.int32, (nz, Z), 1)
+    widen = jnp.where(lane // (Z // nz) == brick, 1.0, 0.0)
+    out = []
+    for d in range(3):
+        at = x + d - 1
+        inside = ((at >= 0) & (at < nx)).astype(F32)
+        tile = occ[jnp.clip(at, 0, nx - 1)].astype(F32) * inside
+        pick = jnp.where((col == row + y - 1) & (row < 3), 1.0, 0.0)
+        near = jnp.dot(pick, tile, preferred_element_type=F32)
+        out.append(jnp.dot(near, widen, preferred_element_type=F32))
+    return out
+
+
+def pack_faces(cells, grad, pick, occ, own, pown, mask, ynear, yfar, near, far):
     odd = odd_place()
+    for d, flags in enumerate(flags_around(occ, lax.axis_index("gx"), lax.axis_index("gy"))):
+        mask[d] = flags
+    here = mask[1][1:2, :]
     for x in range(N):
-        for k in range(H):
-            ylow[x * H + k] = own[x, cell(N - H + k), :]
-            yhigh[x * H + k] = own[x, cell(k), :]
-    for q in range(Q):
-        ylow[N * H + q] = pown[q, cell(Q - 1), :]
-        yhigh[N * H + q] = pown[q, cell(0), :]
+        own[x] = (cells[x].astype(F32) * here).astype(BF)
+    for x in range(Q):
+        pown[x] = jnp.concatenate([grad[x].astype(F32), pick[x].astype(F32)], axis=1).astype(BF)
+
+    def sides(low, high):
+        for x in range(N):
+            for k in range(H):
+                high[x * H + k] = own[x, cell(N - H + k), :]
+                low[x * H + k] = own[x, cell(k), :]
+        for q in range(Q):
+            high[N * H + q] = pown[q, cell(Q - 1), :]
+            low[N * H + q] = pown[q, cell(0), :]
+
+    @pl.when(odd_place("gy") == 0)
+    def _():
+        sides(yfar, ynear)
+
+    @pl.when(odd_place("gy") == 1)
+    def _():
+        sides(ynear, yfar)
+
     for ref, low in ((near, odd), (far, 1 - odd)):
         for k in range(H):
             for y in range(N):
@@ -86,7 +116,8 @@
             ref[N * H + q] = pown[(Q - 1) * (1 - low), cell(q), :]
 
 
-def pack_corners(own, pown, ylow, yhigh, feat, pool, near, far):
+def pack_corners(own, pown, ynear, yfar, feat, pool, near, far, ylow, yhigh):
+    resolve(ynear, yfar, ylow, yhigh, "gy")
     odd = odd_place()
     for ref, low in ((near, odd), (far, 1 - odd)):
         for x in range(H):
@@ -253,8 +284,8 @@
     return feat_at
 
 
-def resolve(near, far, low, high):
-    odd = odd_place()
+def resolve(near, far, low, high, axis="gx"):
+    odd = odd_place(axis)
 
     @pl.when(odd == 0)
     def _():
@@ -387,19 +418,15 @@
 def steps(features, occupancy, weight_one, bias_one, weight_two, bias_two, grad_pooled, pool_choice):
     axes = ("gx", "gy")
     devices = lax.axis_size("gx") * lax.axis_size("gy")
-    flags = jnp.pad(occupancy, ((1, 1), (1, 1), (0, 0)))
-    window = lax.dynamic_slice(
-        flags, (lax.axis_index("gx"), lax.axis_index("gy"), jnp.int32(0)), (3, 3, occupancy.shape[2]))
-    mask = jnp.repeat(window, 8, axis=2).astype(F32)
-    own = (features * mask[1, 1].astype(BF)).transpose(1, 2, 0, 3).reshape(N, N * C, Z)
-    mask = jnp.pad(mask, ((0, 0), (0, 5), (0, 0)))
-    pown = jnp.concatenate([grad_pooled, pool_choice.astype(BF)], axis=3)
-    pown = pown.transpose(1, 2, 0, 3).reshape(Q, Q * C, Z)
+
+    def inner(v):
+        return v.transpose(1, 2, 0, 3).reshape(v.shape[1], v.shape[2] * C, v.shape[3])
 
     face = ((N * H + Q, C, Z), BF)
-    ydown, yup, near, far = call(pack_faces, [face] * 4)(own, pown)
-    ylow = shift(ydown, "gy", 1)
-    yhigh = shift(yup, "gy", -1)
+    own, pown, mask, ynear, yfar, near, far = call(
+        pack_faces, [((N, N * C, Z), BF), ((Q, Q * C, Z), BF), ((3, 8, Z), F32)] + [face] * 4)(inner(features), inner(grad_pooled), inner(pool_choice), occupancy)
+    yfar = swap(yfar, "gy", 1)
+    ynear = swap(ynear, "gy", 0)
     xfar = swap(far, "gx", 1)
     xnear = swap(near, "gx", 0)
 
@@ -415,7 +442,8 @@
     corner = ((N * H + 2, C, Z), BF)
     mfeat, mpool, near, far = call(
         pack_corners,
-        [((N, W * C, Z), BF), ((Q, (Q + 2) * C, Z), BF)] + [corner] * 2)(own, pown, ylow, yhigh)
+        [((N, W * C, Z), BF), ((Q, (Q + 2) * C, Z), BF)] + [corner] * 2,
+        [face, face])(own, pown, ynear, yfar)
     cfar = swap(far, "gx", 1)
     cnear = swap(near, "gx", 0)
 

time: 72.2 us -> 69.3 us (0.960)
  starting transfers between devices: 19.4 us -> 16.1 us
  blocking collectives: 22.4 us -> 24.8 us
  other arithmetic: 2.01 us -> 0 us
  waiting for transfers between devices: 10.7 us -> 8.95 us
  local copies, waits for them, and re-layouts: 2.23 us -> 3.64 us
    ppermute x2 -> x0, starting transfers between devices: 5.37 us -> none  [shift(): return lax.ppermute(v, axis, pairs)]
    all_to_all x1, blocking collectives: 22.4 us -> 24.8 us  [steps(): got = lax.all_to_all(parts.reshape(block), axes, 0, 0, tiled=True)]
    ppermute x4 -> x6, starting transfers between devices: 9.81 us -> 11.8 us  [swap(): return lax.ppermute(v, axis, pairs)]
    convert_element_type x2 -> x0, other arithmetic: 1.79 us -> none  [the longest x1 1.06 us: steps(): pown = jnp.concatenate([grad_pooled, pool_choice.astype(BF)], axis=3)]
    ppermute x2 -> x0, waiting for transfers between devices: 1.77 us -> none  [shift(): return lax.ppermute(v, axis, pairs)]
    transpose x2 -> x3, local copies, waits for them, and re-layouts: 0.38 us -> 1.44 us  [inner(): v.transpose(1, 2, 0, 3).reshape(v.shape[1], v.shape[2] * C, v.shape[3])]
  transfers between devices with their start and end apart: 7 -> 7, of which waited for: 2 -> 1; matrix products, arithmetic and copies ran while one was open for 1% -> 1% of each run, Pallas kernels for 11% -> 12%
where the time goes in v8:
time: 69.3 us; the launch traced here: 69 us
  blocking collectives  24.8 us (36%)
  starting transfers between devices  16.1 us (23%)
  Pallas kernels  14.6 us (21%)
  waiting for transfers between devices  8.95 us (13%)
  local copies, waits for them, and re-layouts  3.64 us (5%)
  between operations  0.82 us (1%)
    all_to_all x1, blocking collectives, steps(): got = lax.all_to_all(parts.reshape(block), axes, 0, 0, tiled=True)  24.8 us
    ppermute x6, starting transfers between devices, swap(): return lax.ppermute(v, axis, pairs)  11.8 us
    all_to_all x1, waiting for transfers between devices, steps(): lax.all_to_all(mine, axes, 0, 0, tiled=True).reshape(devices * ROWS, Z)  8.93 us
    all_to_all x1, starting transfers between devices, steps(): lax.all_to_all(mine, axes, 0, 0, tiled=True).reshape(devices * ROWS, Z)  4.25 us
    pallas_call x1, Pallas kernels, steps(): call(outer, [((W - 6, (W - 6) * C, Z), BF), ((devices * ROWS, Z), BF)], [...  4.07 us
    pallas_call x1, Pallas kernels, steps(): call(middle, [((6, (W - 2) * C, Z), BF), ((4, (W - 4) * C, Z), BF), ((2,...  3.34 us
    pallas_call x1, Pallas kernels, steps(): call(rim, [face, face, ((8, 6 * C, Z), BF), ((8, 4 * C, Z), BF), ((8, 2 *...  2.3 us
    transpose x3, local copies, waits for them, and re-layouts, inner(): v.transpose(1, 2, 0, 3).reshape(v.shape[1], v.shape[2] * C, v.shape[3])  1.44 us
  transfers between devices with their start and end apart: 7, of which 1 were waited for; matrix products, arithmetic and copies ran while one was open for 1% of the time, Pallas kernels for 12%

profile of v8, /device:TPU:1, one launch (start us, length us, event | category | flops | bytes accessed | tf_op | source)
XLA Modules:
  0.0 69.0 jit_solution(6882920087066839779)
XLA Ops:
  0.7 1.0 %copy.14 = bf16[4,4,32,64]{3,2,1,0:T(8,128)(2,1)S(1)} copy(bf16[4,4,32,64]{3,1,0,2:T(4,128)(2,1)} %bitcast.41) | data formatting | bytes 131072 | tf_op jit(solution)/shard_map/transpose | solution.py:423
  1.7 0.1 copy.15
  1.8 0.3 copy.13
  2.2 0.5 copy-done.2
  2.7 0.4 shard_map.119
  3.1 2.1 %collective-permute-start = (bf16[36,32,128]{2,1,0:T(8,128)(2,1)S(1)}, bf16[36,32,128]{2,1,0:T(8,128)(2,1)S(1)}, u32[]{:S(2)}, u32[]{:S(2)}) collective-permute-start(bf16[36,32,128]{2,1,0:T(8,128)(2,1)S(1)} %get-tuple-element.52), channel_id=1, source_target_pairs={{0,1},{1,0},{2,3},{3,2},{4,5},{5,4},{6,7},{7,6},{8,9},{9,8},{10,11... | collective-permute-start | bytes 884744 | tf_op jit(solution)/shard_map/ppermute | solution.py:33
  5.2 0.7 collective-permute-start.1
  5.9 1.0 %collective-permute-start.4 = (bf16[36,32,128]{2,1,0:T(8,128)(2,1)S(1)}, bf16[36,32,128]{2,1,0:T(8,128)(2,1)S(1)}, u32[]{:S(2)}, u32[]{:S(2)}) collective-permute-start(bf16[36,32,128]{2,1,0:T(8,128)(2,1)S(1)} %get-tuple-element.67), channel_id=1, source_target_pairs={{0,8},{8,0},{16,24},{24,16},{32,40},{40,32},{48,56},{56,48},{64,72... | collective-permute-start | bytes 884744 | tf_op jit(solution)/shard_map/ppermute | solution.py:33
  6.9 3.4 %collective-permute-start.5 = (bf16[36,32,128]{2,1,0:T(8,128)(2,1)S(1)}, bf16[36,32,128]{2,1,0:T(8,128)(2,1)S(1)}, u32[]{:S(2)}, u32[]{:S(2)}) collective-permute-start(bf16[36,32,128]{2,1,0:T(8,128)(2,1)S(1)} %get-tuple-element.68), channel_id=1, source_target_pairs={{8,16},{16,8},{24,32},{32,24},{40,48},{48,40},{56,64},{64,56},{72,... | collective-permute-start | bytes 884744 | tf_op jit(solution)/shard_map/ppermute | solution.py:33
  10.4 0.6 copy-done.3
  11.0 1.3 %shard_map.120 = (bf16[192,384]{1,0:T(8,128)(2,1)S(1)}, bf16[192,384]{1,0:T(8,128)(2,1)S(1)}, bf16[192,384]{1,0:T(8,128)(2,1)S(1)}, bf16[192,384]{1,0:T(8,128)(2...) custom-call(bf16[27,32,32]{2,1,0:T(8,128)(2,1)S(1)} %bitcast.34, bf16[27,32,32]{2,1,0:T(8,128)(2,1)S(1)} %bitcast.35, ...), custom_call_target="tpu_custom_call" | custom-call | tf_op jit(solution)/shard_map/pallas_call | solution.py:436
  12.3 0.2 shard_map.121
  12.5 0.9 %collective-permute-start.2 = (bf16[34,32,128]{2,1,0:T(8,128)(2,1)S(1)}, bf16[34,32,128]{2,1,0:T(8,128)(2,1)S(1)}, u32[]{:S(2)}, u32[]{:S(2)}) collective-permute-start(bf16[34,32,128]{2,1,0:T(8,128)(2,1)S(1)} %get-tuple-element.56), channel_id=1, source_target_pairs={{0,8},{8,0},{16,24},{24,16},{32,40},{40,32},{48,56},{56,48},{64,72... | collective-permute-start | bytes 835592 | tf_op jit(solution)/shard_map/ppermute | solution.py:33
  13.4 3.7 %collective-permute-start.3 = (bf16[34,32,128]{2,1,0:T(8,128)(2,1)S(1)}, bf16[34,32,128]{2,1,0:T(8,128)(2,1)S(1)}, u32[]{:S(2)}, u32[]{:S(2)}) collective-permute-start(bf16[34,32,128]{2,1,0:T(8,128)(2,1)S(1)} %get-tuple-element.57), channel_id=1, source_target_pairs={{8,16},{16,8},{24,32},{32,24},{40,48},{48,40},{56,64},{64,56},{72,... | collective-permute-start | bytes 835592 | tf_op jit(solution)/shard_map/ppermute | solution.py:33
  17.1 3.3 %shard_map.122 = (bf16[6,448,128]{2,1,0:T(8,128)(2,1)S(1)}, bf16[4,384,128]{2,1,0:T(8,128)(2,1)S(1)}, bf16[2,320,128]{2,1,0:T(8,128)(2,1)S(1)}, f32[288,96]{1,0:...) custom-call(bf16[8,512,128]{2,1,0:T(8,128)(2,1)S(1)} %get-tuple-element.54.feat.mfeat, ...), custom_call_target="tpu_custom_call" | custom-call | tf_op jit(solution)/shard_map/pallas_call | solution.py:451
  20.5 2.3 %shard_map.123 = (bf16[36,32,128]{2,1,0:T(8,128)(2,1)S(1)}, bf16[36,32,128]{2,1,0:T(8,128)(2,1)S(1)}, bf16[8,192,128]{2,1,0:T(8,128)(2,1)S(1)}, bf16[8,128,128]{...) custom-call(bf16[8,512,128]{2,1,0:T(8,128)(2,1)S(1)} %get-tuple-elem, ...), custom_call_target="tpu_custom_call" | custom-call | tf_op jit(solution)/shard_map/pallas_call | solution.py:456
  22.8 4.1 %shard_map.124 = (bf16[10,320,128]{2,1,0:T(8,128)(2,1)S(1)}, bf16[1024,128]{1,0:T(8,128)(2,1)S(1)}) custom-call(bf16[8,512,128]{2,1,0:T(8,128)(2,1)S(1)} %get-tuple-element.54.feat.mfeat, bf16[4,192,128]{2,1,0:T(8,128)(2,1)S(1)} %get-tuple-element.55.pool.mpool, bf16[34,32,128]{2,1,0:T(8,128)(2,1)S(1)} %collective-permute-done.2.cnear, ...), custom_call_target="tpu_custom_call" | custom-call | tf_op jit(solution)/shard_map/pallas_call | solution.py:461
  26.9 24.8 %all_to_all.10.got = bf16[128,8,128]{2,1,0:T(8,128)(2,1)S(1)} all-to-all(bf16[128,8,128]{2,1,0:T(8,128)(2,1)S(1)} %bitcast.33), channel_id=1, replica_groups=mesh['gx'=16,'gy'=8] {'gx','gy'}, dimensions={0} | all-to-all | bytes 524288 | tf_op jit(solution)/shard_map/all_to_all | solution.py:467
  51.7 0.9 %shard_map.126 = bf16[128,8,128]{2,1,0:T(8,128)(2,1)} custom-call(bf16[128,8,128]{2,1,0:T(8,128)(2,1)S(1)} %all_to_all.10.got), custom_call_target="tpu_custom_call" | custom-call | tf_op jit(solution)/shard_map/pallas_call | solution.py:469
  52.6 4.2 %all-to-all-start.1 = ((bf16[128,8,128]{2,1,0:T(8,128)(2,1)}), bf16[128,8,128]{2,1,0:T(8,128)(2,1)S(1)}, u32[]{:S(2)}, u32[]{:S(2)}) async-start(bf16[128,8,128]{2,1,0:T(8,128)(2,1)} %shard_map.126), calls=%async_computation.1 | async-start | bytes 524288 | tf_op jit(solution)/shard_map/all_to_all | solution.py:470
  56.8 1.1 %shard_map.125 = bf16[8,256,128]{2,1,0:T(8,128)(2,1)S(1)} custom-call(bf16[10,320,128]{2,1,0:T(8,128)(2,1)S(1)} %get-tuple-element.82.one, f32[3,8,128]{2,1,0:T(8,128)S(1)} %get-tuple-element.58.mask, bf16[192,384]{1,0:T(8,128)(2,1)S(1)} %get-tuple-element.83.f1), custom_call_target="tpu_custom_call" | custom-call | tf_op jit(solution)/shard_map/pallas_call | solution.py:468
  57.9 1.0 %copy.18 = bf16[8,8,32,128]{3,1,0,2:T(8,128)(2,1)} copy(bf16[8,8,32,128]{3,2,1,0:T(8,128)(2,1)S(1)} %bitcast.28) | data formatting | bytes 1048576 | tf_op jit(solution)/shard_map/reshape | solution.py:477
  58.9 8.9 %all-to-all-done.1 = bf16[128,8,128]{2,1,0:T(8,128)(2,1)S(1)} async-done(((bf16[128,8,128]{2,1,0:T(8,128)(2,1)}), bf16[128,8,128]{2,1,0:T(8,128)(2,1)S(1)}, u32[]{:S(2)}, u32[]{:S(2)}) %all-to-all-start.1) | async-done | bytes 262176 | tf_op jit(solution)/shard_map/all_to_all | solution.py:470
  67.8 1.1 %shard_map.127 = (f32[27,32,32]{2,1,0:T(8,128)}, f32[27,32,32]{2,1,0:T(8,128)}, f32[1,32]{1,0:T(1,128)}, f32[1,32]{1,0:T(1,128)}) custom-call(bf16[1024,128]{1,0:T(8,128)(2,1)S(1)} %bitcast.30), custom_call_target="tpu_custom_call" | custom-call | tf_op jit(solution)/shard_map/pallas_call | solution.py:471
  (18 shorter events, 0.1 us)
Async XLA Ops:
  0.6 1.0 %copy-start.6 = (s32[32,4,4,64]{3,2,1,0:T(4,128)S(1)}, s32[32,4,4,64]{3,2,1,0:T(4,128)}, u32[]{:S(2)}) copy-start(s32[32,4,4,64]{3,2,1,0:T(4,128)} %param.15) | copy-start | bytes 393220
  0.6 1.2 %copy-start.5 = (bf16[32,8,8,128]{3,2,1,0:T(8,128)(2,1)S(1)}, bf16[32,8,8,128]{3,2,1,0:T(8,128)(2,1)}, u32[]{:S(2)}) copy-start(bf16[32,8,8,128]{3,2,1,0:T(8,128)(2,1)} %param.8) | copy-start | bytes 1572868
  1.8 0.8 %copy-start.2 = (s32[16,8,16]{2,1,0:T(8,128)S(1)}, s32[16,8,16]{2,1,0:T(8,128)}, u32[]{:S(2)}) copy-start(s32[16,8,16]{2,1,0:T(8,128)} %occ.1) | copy-start | bytes 24580
  2.7 7.7 %copy-start = (bf16[32,3,3,3,32]{4,0,3,2,1:T(8,128)(2,1)S(1)}, bf16[32,3,3,3,32]{4,0,3,2,1:T(8,128)(2,1)}, u32[]{:S(2)}) copy-start(bf16[32,3,3,3,32]{4,0,3,2,1:T(8,128)(2,1)} %param.10) | copy-start | bytes 165892
  2.7 7.7 %copy-start.1 = (bf16[32,3,3,3,32]{4,0,3,2,1:T(8,128)(2,1)S(1)}, bf16[32,3,3,3,32]{4,0,3,2,1:T(8,128)(2,1)}, u32[]{:S(2)}) copy-start(bf16[32,3,3,3,32]{4,0,3,2,1:T(8,128)(2,1)} %param.12) | copy-start | bytes 165892
  3.1 9.2 %collective-permute-start = (bf16[36,32,128]{2,1,0:T(8,128)(2,1)S(1)}, bf16[36,32,128]{2,1,0:T(8,128)(2,1)S(1)}, u32[]{:S(2)}, u32[]{:S(2)}) collective-permute-start(bf16[36,32,128]{2,1,0:T(8,128)(2,1)S(1)} %get-tuple-element.52), channel_id=1, source_target_pairs={{0,1},{1,0},{2,3},{3,2},{4,5},{5,4},{6,7},{7,6},{8,9},{9,8},{10,11... | collective-permute-start | bytes 884744 | tf_op jit(solution)/shard_map/ppermute | solution.py:33
  5.2 7.1 %collective-permute-start.1 = (bf16[36,32,128]{2,1,0:T(8,128)(2,1)S(1)}, bf16[36,32,128]{2,1,0:T(8,128)(2,1)S(1)}, u32[]{:S(2)}, u32[]{:S(2)}) collective-permute-start(bf16[36,32,128]{2,1,0:T(8,128)(2,1)S(1)} %get-tuple-element.53), channel_id=1, source_target_pairs={{1,2},{2,1},{3,4},{4,3},{5,6},{6,5},{9,10},{10,9},{11,12},{12,11},... | collective-permute-start | bytes 884744 | tf_op jit(solution)/shard_map/ppermute | solution.py:33
  5.9 14.6 %collective-permute-start.4 = (bf16[36,32,128]{2,1,0:T(8,128)(2,1)S(1)}, bf16[36,32,128]{2,1,0:T(8,128)(2,1)S(1)}, u32[]{:S(2)}, u32[]{:S(2)}) collective-permute-start(bf16[36,32,128]{2,1,0:T(8,128)(2,1)S(1)} %get-tuple-element.67), channel_id=1, source_target_pairs={{0,8},{8,0},{16,24},{24,16},{32,40},{40,32},{48,56},{56,48},{64,72... | collective-permute-start | bytes 884744 | tf_op jit(solution)/shard_map/ppermute | solution.py:33
  6.9 13.6 %collective-permute-start.5 = (bf16[36,32,128]{2,1,0:T(8,128)(2,1)S(1)}, bf16[36,32,128]{2,1,0:T(8,128)(2,1)S(1)}, u32[]{:S(2)}, u32[]{:S(2)}) collective-permute-start(bf16[36,32,128]{2,1,0:T(8,128)(2,1)S(1)} %get-tuple-element.68), channel_id=1, source_target_pairs={{8,16},{16,8},{24,32},{32,24},{40,48},{48,40},{56,64},{64,56},{72,... | collective-permute-start | bytes 884744 | tf_op jit(solution)/shard_map/ppermute | solution.py:33
  10.3 0.7 copy-start.3
  10.4 0.7 copy-start.4
  12.5 10.3 %collective-permute-start.2 = (bf16[34,32,128]{2,1,0:T(8,128)(2,1)S(1)}, bf16[34,32,128]{2,1,0:T(8,128)(2,1)S(1)}, u32[]{:S(2)}, u32[]{:S(2)}) collective-permute-start(bf16[34,32,128]{2,1,0:T(8,128)(2,1)S(1)} %get-tuple-element.56), channel_id=1, source_target_pairs={{0,8},{8,0},{16,24},{24,16},{32,40},{40,32},{48,56},{56,48},{64,72... | collective-permute-start | bytes 835592 | tf_op jit(solution)/shard_map/ppermute | solution.py:33
  13.4 9.4 %collective-permute-start.3 = (bf16[34,32,128]{2,1,0:T(8,128)(2,1)S(1)}, bf16[34,32,128]{2,1,0:T(8,128)(2,1)S(1)}, u32[]{:S(2)}, u32[]{:S(2)}) collective-permute-start(bf16[34,32,128]{2,1,0:T(8,128)(2,1)S(1)} %get-tuple-element.57), channel_id=1, source_target_pairs={{8,16},{16,8},{24,32},{32,24},{40,48},{48,40},{56,64},{64,56},{72,... | collective-permute-start | bytes 835592 | tf_op jit(solution)/shard_map/ppermute | solution.py:33
  52.6 15.3 %all-to-all-start.1 = ((bf16[128,8,128]{2,1,0:T(8,128)(2,1)}), bf16[128,8,128]{2,1,0:T(8,128)(2,1)S(1)}, u32[]{:S(2)}, u32[]{:S(2)}) async-start(bf16[128,8,128]{2,1,0:T(8,128)(2,1)} %shard_map.126), calls=%async_computation.1 | async-start | bytes 524288 | tf_op jit(solution)/shard_map/all_to_all | solution.py:470

commit v9 on v8

--- a/solution.py
+++ b/solution.py
@@ -41,7 +41,7 @@
     return slice(y * C, (y + n) * C)
 
 
-def prepare(w1, w2, b1, b2, t1, t2, f2, f1, c1, c2):
+def prepare(w1, w2, t1, t2, f2, f1):
     zero = jnp.zeros((C, C), F32)
     for src, plain, flip in ((w1, t1, f1), (w2, t2, f2)):
         for a in range(3):
@@ -59,8 +59,6 @@
                 line = jnp.transpose(tall)
                 flip[rows, cols] = line.astype(BF)
                 flip[high, cols] = pltpu.roll(line, C, 1).astype(BF)
-    for src, dst in ((b1, c1), (b2, c2)):
-        dst[...] = jnp.transpose(jnp.broadcast_to(src[...], (Z, C)))
 
 
 def flags_around(occ, x, y):
@@ -81,10 +79,13 @@
     return out
 
 
-def pack_faces(cells, grad, pick, occ, own, pown, mask, ynear, yfar, near, far):
+def pack_faces(cells, grad, pick, occ, b1, b2,
+               own, pown, mask, c1, c2, ynear, yfar, near, far):
     odd = odd_place()
     for d, flags in enumerate(flags_around(occ, lax.axis_index("gx"), lax.axis_index("gy"))):
         mask[d] = flags
+    for src, dst in ((b1, c1), (b2, c2)):
+        dst[...] = jnp.transpose(jnp.broadcast_to(src[...], (Z, C)))
     here = mask[1][1:2, :]
     for x in range(N):
         own[x] = (cells[x].astype(F32) * here).astype(BF)
@@ -390,8 +391,10 @@
 
 
 def add_up(got, out):
-    total = jnp.sum(got[...].astype(F32), axis=0, keepdims=True).astype(BF)
-    out[...] = jnp.broadcast_to(total, out.shape)
+    total = jnp.sum(got[...].astype(F32), axis=0)
+    total = total[:ROWS] + total[ROWS:]
+    pair = jnp.concatenate([total, total], axis=0).astype(BF)
+    out[...] = jnp.broadcast_to(pair[None], out.shape)
 
 
 def unpack(summed, w1, w2, b1, b2):
@@ -423,8 +426,11 @@
         return v.transpose(1, 2, 0, 3).reshape(v.shape[1], v.shape[2] * C, v.shape[3])
 
     face = ((N * H + Q, C, Z), BF)
-    own, pown, mask, ynear, yfar, near, far = call(
-        pack_faces, [((N, N * C, Z), BF), ((Q, Q * C, Z), BF), ((3, 8, Z), F32)] + [face] * 4)(inner(features), inner(grad_pooled), inner(pool_choice), occupancy)
+    own, pown, mask, b1, b2, ynear, yfar, near, far = call(
+        pack_faces,
+        [((N, N * C, Z), BF), ((Q, Q * C, Z), BF), ((3, 8, Z), F32)] + [((C, Z), F32)] * 2
+        + [face] * 4)(inner(features), inner(grad_pooled), inner(pool_choice), occupancy,
+                      bias_one.reshape(1, C), bias_two.reshape(1, C))
     yfar = swap(yfar, "gy", 1)
     ynear = swap(ynear, "gy", 0)
     xfar = swap(far, "gx", 1)
@@ -433,10 +439,8 @@
     def blocks(weight):
         return weight.transpose(1, 2, 3, 0, 4).reshape(27, C, C)
 
-    t1, t2, f2, f1, b1, b2 = call(
-        prepare, [((6 * C, 12 * C), BF)] * 4 + [((C, Z), F32)] * 2)(
-            blocks(weight_one), blocks(weight_two),
-            bias_one.reshape(1, C), bias_two.reshape(1, C))
+    t1, t2, f2, f1 = call(prepare, [((6 * C, 12 * C), BF)] * 4)(
+        blocks(weight_one), blocks(weight_two))
 
     own, pown, t1 = lax.optimization_barrier((own, pown, t1))
     corner = ((N * H + 2, C, Z), BF)
@@ -466,8 +470,9 @@
     block = (devices, ROWS, Z)
     got = lax.all_to_all(parts.reshape(block), axes, 0, 0, tiled=True)
     out, = call(final, [((N, N * C, Z), BF)])(one, mask, f1)
-    mine, = call(add_up, [(block, BF)])(got)
-    summed = lax.all_to_all(mine, axes, 0, 0, tiled=True).reshape(devices * ROWS, Z)
+    tiles = (devices // 2, 2 * ROWS, Z)
+    mine, = call(add_up, [(tiles, BF)])(got.reshape(tiles))
+    summed = lax.all_to_all(mine.reshape(block), axes, 0, 0, tiled=True).reshape(devices * ROWS, Z)
     gw1, gw2, gb1, gb2 = call(
         unpack, [((27, C, C), F32)] * 2 + [((1, C), F32)] * 2)(summed)
 

time: 69.3 us -> 69.4 us (level)
  starting transfers between devices: 16.1 us -> 16.8 us
    ppermute x6, starting transfers between devices: 11.8 us -> 12.6 us  [swap(): return lax.ppermute(v, axis, pairs)]
where the time goes in v9:
time: 69.4 us; the launch traced here: 69.1 us
  blocking collectives  24.8 us (36%)
  starting transfers between devices  16.8 us (24%)
  Pallas kernels  14.5 us (21%)
  waiting for transfers between devices  8.96 us (13%)
  local copies, waits for them, and re-layouts  3.17 us (5%)
  between operations  0.83 us (1%)
    all_to_all x1, blocking collectives, steps(): got = lax.all_to_all(parts.reshape(block), axes, 0, 0, tiled=True)  24.8 us
    ppermute x6, starting transfers between devices, swap(): return lax.ppermute(v, axis, pairs)  12.6 us
    all_to_all x1, waiting for transfers between devices, steps(): lax.all_to_all(mine.reshape(block), axes, 0, 0, tiled=True)  8.94 us
    all_to_all x1, starting transfers between devices, steps(): lax.all_to_all(mine.reshape(block), axes, 0, 0, tiled=True)  4.25 us
    pallas_call x1, Pallas kernels, steps(): call(outer, [((W - 6, (W - 6) * C, Z), BF), ((devices * ROWS, Z), BF)], [...  4.07 us
    pallas_call x1, Pallas kernels, steps(): call(middle, [((6, (W - 2) * C, Z), BF), ((4, (W - 4) * C, Z), BF), ((2,...  3.34 us
    pallas_call x1, Pallas kernels, steps(): call(rim, [face, face, ((8, 6 * C, Z), BF), ((8, 4 * C, Z), BF), ((8, 2 *...  2.3 us
    transpose x3, local copies, waits for them, and re-layouts, inner(): v.transpose(1, 2, 0, 3).reshape(v.shape[1], v.shape[2] * C, v.shape[3])  1.44 us
  transfers between devices with their start and end apart: 7, of which 1 were waited for; matrix products, arithmetic and copies ran while one was open for 1% of the time, Pallas kernels for 12%

profile of v9, /device:TPU:1, one launch (start us, length us, event | category | flops | bytes accessed | tf_op | source)
XLA Modules:
  0.0 69.1 jit_solution(2322214346068355808)
XLA Ops:
  0.7 1.0 %copy.14 = bf16[4,4,32,64]{3,2,1,0:T(8,128)(2,1)S(1)} copy(bf16[4,4,32,64]{3,1,0,2:T(4,128)(2,1)} %bitcast.44) | data formatting | bytes 131072 | tf_op jit(solution)/shard_map/transpose | solution.py:426
  1.7 0.1 copy.15
  1.8 0.3 copy.13
  2.2 0.5 copy-done.2
  2.7 0.2 copy-done.3
  2.9 0.4 shard_map.119
  3.3 2.1 %collective-permute-start = (bf16[36,32,128]{2,1,0:T(8,128)(2,1)S(1)}, bf16[36,32,128]{2,1,0:T(8,128)(2,1)S(1)}, u32[]{:S(2)}, u32[]{:S(2)}) collective-permute-start(bf16[36,32,128]{2,1,0:T(8,128)(2,1)S(1)} %get-tuple-element.52), channel_id=1, source_target_pairs={{0,1},{1,0},{2,3},{3,2},{4,5},{5,4},{6,7},{7,6},{8,9},{9,8},{10,11... | collective-permute-start | bytes 884744 | tf_op jit(solution)/shard_map/ppermute | solution.py:33
  5.4 0.7 collective-permute-start.1
  6.1 1.0 %collective-permute-start.4 = (bf16[36,32,128]{2,1,0:T(8,128)(2,1)S(1)}, bf16[36,32,128]{2,1,0:T(8,128)(2,1)S(1)}, u32[]{:S(2)}, u32[]{:S(2)}) collective-permute-start(bf16[36,32,128]{2,1,0:T(8,128)(2,1)S(1)} %get-tuple-element.67), channel_id=1, source_target_pairs={{0,8},{8,0},{16,24},{24,16},{32,40},{40,32},{48,56},{56,48},{64,72... | collective-permute-start | bytes 884744 | tf_op jit(solution)/shard_map/ppermute | solution.py:33
  7.1 3.4 %collective-permute-start.5 = (bf16[36,32,128]{2,1,0:T(8,128)(2,1)S(1)}, bf16[36,32,128]{2,1,0:T(8,128)(2,1)S(1)}, u32[]{:S(2)}, u32[]{:S(2)}) collective-permute-start(bf16[36,32,128]{2,1,0:T(8,128)(2,1)S(1)} %get-tuple-element.68), channel_id=1, source_target_pairs={{8,16},{16,8},{24,32},{32,24},{40,48},{48,40},{56,64},{64,56},{72,... | collective-permute-start | bytes 884744 | tf_op jit(solution)/shard_map/ppermute | solution.py:33
  10.6 1.2 %shard_map.120 = (bf16[192,384]{1,0:T(8,128)(2,1)S(1)}, bf16[192,384]{1,0:T(8,128)(2,1)S(1)}, bf16[192,384]{1,0:T(8,128)(2,1)S(1)}, bf16[192,384]{1,0:T(8,128)(2,1)S(1)}) custom-call(bf16[27,32,32]{2,1,0:T(8,128)(2,1)S(1)} %bitcast.37, bf16[27,32,32]{2,1,0:T(8,128)(2,1)S(1)} %bitcast.38), custom_call_target="tpu_custom_call" | custom-call | tf_op jit(solution)/shard_map/pallas_call | solution.py:442
  11.8 0.2 shard_map.121
  12.0 1.6 %collective-permute-start.2 = (bf16[34,32,128]{2,1,0:T(8,128)(2,1)S(1)}, bf16[34,32,128]{2,1,0:T(8,128)(2,1)S(1)}, u32[]{:S(2)}, u32[]{:S(2)}) collective-permute-start(bf16[34,32,128]{2,1,0:T(8,128)(2,1)S(1)} %get-tuple-element.56), channel_id=1, source_target_pairs={{0,8},{8,0},{16,24},{24,16},{32,40},{40,32},{48,56},{56,48},{64,72... | collective-permute-start | bytes 835592 | tf_op jit(solution)/shard_map/ppermute | solution.py:33
  13.6 3.7 %collective-permute-start.3 = (bf16[34,32,128]{2,1,0:T(8,128)(2,1)S(1)}, bf16[34,32,128]{2,1,0:T(8,128)(2,1)S(1)}, u32[]{:S(2)}, u32[]{:S(2)}) collective-permute-start(bf16[34,32,128]{2,1,0:T(8,128)(2,1)S(1)} %get-tuple-element.57), channel_id=1, source_target_pairs={{8,16},{16,8},{24,32},{32,24},{40,48},{48,40},{56,64},{64,56},{72,... | collective-permute-start | bytes 835592 | tf_op jit(solution)/shard_map/ppermute | solution.py:33
  17.3 3.3 %shard_map.122 = (bf16[6,448,128]{2,1,0:T(8,128)(2,1)S(1)}, bf16[4,384,128]{2,1,0:T(8,128)(2,1)S(1)}, bf16[2,320,128]{2,1,0:T(8,128)(2,1)S(1)}, f32[288,96]{1,0:...) custom-call(bf16[8,512,128]{2,1,0:T(8,128)(2,1)S(1)} %get-tuple-element.54.feat.mfeat, ...), custom_call_target="tpu_custom_call" | custom-call | tf_op jit(solution)/shard_map/pallas_call | solution.py:455
  20.7 2.3 %shard_map.123 = (bf16[36,32,128]{2,1,0:T(8,128)(2,1)S(1)}, bf16[36,32,128]{2,1,0:T(8,128)(2,1)S(1)}, bf16[8,192,128]{2,1,0:T(8,128)(2,1)S(1)}, bf16[8,128,128]{...) custom-call(bf16[8,512,128]{2,1,0:T(8,128)(2,1)S(1)} %get-tuple-elem, ...), custom_call_target="tpu_custom_call" | custom-call | tf_op jit(solution)/shard_map/pallas_call | solution.py:460
  23.0 4.1 %shard_map.124 = (bf16[10,320,128]{2,1,0:T(8,128)(2,1)S(1)}, bf16[1024,128]{1,0:T(8,128)(2,1)S(1)}) custom-call(bf16[8,512,128]{2,1,0:T(8,128)(2,1)S(1)} %get-tuple-element.54.feat.mfeat, bf16[4,192,128]{2,1,0:T(8,128)(2,1)S(1)} %get-tuple-element.55.pool.mpool, bf16[34,32,128]{2,1,0:T(8,128)(2,1)S(1)} %collective-permute-done.2.cnear, ...), custom_call_target="tpu_custom_call" | custom-call | tf_op jit(solution)/shard_map/pallas_call | solution.py:465
  27.1 24.8 %all_to_all.10 = bf16[128,8,128]{2,1,0:T(8,128)(2,1)S(1)} all-to-all(bf16[128,8,128]{2,1,0:T(8,128)(2,1)S(1)} %bitcast.36), channel_id=1, replica_groups=mesh['gx'=16,'gy'=8] {'gx','gy'}, dimensions={0} | all-to-all | bytes 524288 | tf_op jit(solution)/shard_map/all_to_all | solution.py:471
  51.9 0.8 %shard_map.126 = bf16[64,16,128]{2,1,0:T(8,128)(2,1)} custom-call(bf16[64,16,128]{2,1,0:T(8,128)(2,1)S(1)} %bitcast.34), custom_call_target="tpu_custom_call" | custom-call | tf_op jit(solution)/shard_map/pallas_call | solution.py:474
  52.7 4.2 %all-to-all-start.1 = ((bf16[128,8,128]{2,1,0:T(8,128)(2,1)}), bf16[128,8,128]{2,1,0:T(8,128)(2,1)S(1)}, u32[]{:S(2)}, u32[]{:S(2)}) async-start(bf16[128,8,128]{2,1,0:T(8,128)(2,1)} %bitcast.16), calls=%async_computation.1 | async-start | bytes 524288 | tf_op jit(solution)/shard_map/all_to_all | solution.py:475
  56.9 1.1 %shard_map.125 = bf16[8,256,128]{2,1,0:T(8,128)(2,1)S(1)} custom-call(bf16[10,320,128]{2,1,0:T(8,128)(2,1)S(1)} %get-tuple-element.82.one, f32[3,8,128]{2,1,0:T(8,128)S(1)} %get-tuple-element.58.mask, bf16[192,384]{1,0:T(8,128)(2,1)S(1)} %get-tuple-element.83.f1), custom_call_target="tpu_custom_call" | custom-call | tf_op jit(solution)/shard_map/pallas_call | solution.py:472
  58.0 1.0 %copy.18 = bf16[8,8,32,128]{3,1,0,2:T(8,128)(2,1)} copy(bf16[8,8,32,128]{3,2,1,0:T(8,128)(2,1)S(1)} %bitcast.30) | data formatting | bytes 1048576 | tf_op jit(solution)/shard_map/reshape | solution.py:482
  59.0 8.9 %all-to-all-done.1 = bf16[128,8,128]{2,1,0:T(8,128)(2,1)S(1)} async-done(((bf16[128,8,128]{2,1,0:T(8,128)(2,1)}), bf16[128,8,128]{2,1,0:T(8,128)(2,1)S(1)}, u32[]{:S(2)}, u32[]{:S(2)}) %all-to-all-start.1) | async-done | bytes 262176 | tf_op jit(solution)/shard_map/all_to_all | solution.py:475
  68.0 1.1 %shard_map.127 = (f32[27,32,32]{2,1,0:T(8,128)}, f32[27,32,32]{2,1,0:T(8,128)}, f32[1,32]{1,0:T(1,128)}, f32[1,32]{1,0:T(1,128)}) custom-call(bf16[1024,128]{1,0:T(8,128)(2,1)S(1)} %bitcast.33), custom_call_target="tpu_custom_call" | custom-call | tf_op jit(solution)/shard_map/pallas_call | solution.py:476
  (18 shorter events, 0.1 us)
Async XLA Ops:
  0.6 1.0 %copy-start.6 = (s32[32,4,4,64]{3,2,1,0:T(4,128)S(1)}, s32[32,4,4,64]{3,2,1,0:T(4,128)}, u32[]{:S(2)}) copy-start(s32[32,4,4,64]{3,2,1,0:T(4,128)} %param.15) | copy-start | bytes 393220
  0.6 1.2 %copy-start.5 = (bf16[32,8,8,128]{3,2,1,0:T(8,128)(2,1)S(1)}, bf16[32,8,8,128]{3,2,1,0:T(8,128)(2,1)}, u32[]{:S(2)}) copy-start(bf16[32,8,8,128]{3,2,1,0:T(8,128)(2,1)} %param.8) | copy-start | bytes 1572868
  1.8 0.8 %copy-start.2 = (s32[16,8,16]{2,1,0:T(8,128)S(1)}, s32[16,8,16]{2,1,0:T(8,128)}, u32[]{:S(2)}) copy-start(s32[16,8,16]{2,1,0:T(8,128)} %occ.1) | copy-start | bytes 24580
  2.2 0.7 copy-start.3
  2.2 0.7 copy-start.4
  2.8 7.7 %copy-start = (bf16[32,3,3,3,32]{4,0,3,2,1:T(8,128)(2,1)S(1)}, bf16[32,3,3,3,32]{4,0,3,2,1:T(8,128)(2,1)}, u32[]{:S(2)}) copy-start(bf16[32,3,3,3,32]{4,0,3,2,1:T(8,128)(2,1)} %param.10) | copy-start | bytes 165892
  2.9 7.7 %copy-start.1 = (bf16[32,3,3,3,32]{4,0,3,2,1:T(8,128)(2,1)S(1)}, bf16[32,3,3,3,32]{4,0,3,2,1:T(8,128)(2,1)}, u32[]{:S(2)}) copy-start(bf16[32,3,3,3,32]{4,0,3,2,1:T(8,128)(2,1)} %param.12) | copy-start | bytes 165892
  3.3 8.5 %collective-permute-start = (bf16[36,32,128]{2,1,0:T(8,128)(2,1)S(1)}, bf16[36,32,128]{2,1,0:T(8,128)(2,1)S(1)}, u32[]{:S(2)}, u32[]{:S(2)}) collective-permute-start(bf16[36,32,128]{2,1,0:T(8,128)(2,1)S(1)} %get-tuple-element.52), channel_id=1, source_target_pairs={{0,1},{1,0},{2,3},{3,2},{4,5},{5,4},{6,7},{7,6},{8,9},{9,8},{10,11... | collective-permute-start | bytes 884744 | tf_op jit(solution)/shard_map/ppermute | solution.py:33
  5.4 6.4 %collective-permute-start.1 = (bf16[36,32,128]{2,1,0:T(8,128)(2,1)S(1)}, bf16[36,32,128]{2,1,0:T(8,128)(2,1)S(1)}, u32[]{:S(2)}, u32[]{:S(2)}) collective-permute-start(bf16[36,32,128]{2,1,0:T(8,128)(2,1)S(1)} %get-tuple-element.53), channel_id=1, source_target_pairs={{1,2},{2,1},{3,4},{4,3},{5,6},{6,5},{9,10},{10,9},{11,12},{12,11},... | collective-permute-start | bytes 884744 | tf_op jit(solution)/shard_map/ppermute | solution.py:33
  6.1 14.6 %collective-permute-start.4 = (bf16[36,32,128]{2,1,0:T(8,128)(2,1)S(1)}, bf16[36,32,128]{2,1,0:T(8,128)(2,1)S(1)}, u32[]{:S(2)}, u32[]{:S(2)}) collective-permute-start(bf16[36,32,128]{2,1,0:T(8,128)(2,1)S(1)} %get-tuple-element.67), channel_id=1, source_target_pairs={{0,8},{8,0},{16,24},{24,16},{32,40},{40,32},{48,56},{56,48},{64,72... | collective-permute-start | bytes 884744 | tf_op jit(solution)/shard_map/ppermute | solution.py:33
  7.1 13.6 %collective-permute-start.5 = (bf16[36,32,128]{2,1,0:T(8,128)(2,1)S(1)}, bf16[36,32,128]{2,1,0:T(8,128)(2,1)S(1)}, u32[]{:S(2)}, u32[]{:S(2)}) collective-permute-start(bf16[36,32,128]{2,1,0:T(8,128)(2,1)S(1)} %get-tuple-element.68), channel_id=1, source_target_pairs={{8,16},{16,8},{24,32},{32,24},{40,48},{48,40},{56,64},{64,56},{72,... | collective-permute-start | bytes 884744 | tf_op jit(solution)/shard_map/ppermute | solution.py:33
  12.0 11.0 %collective-permute-start.2 = (bf16[34,32,128]{2,1,0:T(8,128)(2,1)S(1)}, bf16[34,32,128]{2,1,0:T(8,128)(2,1)S(1)}, u32[]{:S(2)}, u32[]{:S(2)}) collective-permute-start(bf16[34,32,128]{2,1,0:T(8,128)(2,1)S(1)} %get-tuple-element.56), channel_id=1, source_target_pairs={{0,8},{8,0},{16,24},{24,16},{32,40},{40,32},{48,56},{56,48},{64,72... | collective-permute-start | bytes 835592 | tf_op jit(solution)/shard_map/ppermute | solution.py:33
  13.6 9.4 %collective-permute-start.3 = (bf16[34,32,128]{2,1,0:T(8,128)(2,1)S(1)}, bf16[34,32,128]{2,1,0:T(8,128)(2,1)S(1)}, u32[]{:S(2)}, u32[]{:S(2)}) collective-permute-start(bf16[34,32,128]{2,1,0:T(8,128)(2,1)S(1)} %get-tuple-element.57), channel_id=1, source_target_pairs={{8,16},{16,8},{24,32},{32,24},{40,48},{48,40},{56,64},{64,56},{72,... | collective-permute-start | bytes 835592 | tf_op jit(solution)/shard_map/ppermute | solution.py:33
  52.7 15.3 %all-to-all-start.1 = ((bf16[128,8,128]{2,1,0:T(8,128)(2,1)}), bf16[128,8,128]{2,1,0:T(8,128)(2,1)S(1)}, u32[]{:S(2)}, u32[]{:S(2)}) async-start(bf16[128,8,128]{2,1,0:T(8,128)(2,1)} %bitcast.16), calls=%async_computation.1 | async-start | bytes 524288 | tf_op jit(solution)/shard_map/all_to_all | solution.py:475
